TPU v7x, 128 devices: a whole 4x4x4 slice. The times are simulated.
128 devices in a mesh: gx: 4 (over z), gy: 16 (over y, x), gz: 2 (over core).
Axes of the slice: x: 4, y: 4, z: 4, core: 2. Of those that a mesh axis runs over, the one named last changes fastest.
Arguments:
- particles: float32 [8, 1048576], P(None, ('gx', 'gy', 'gz')), may hold values from -0.5 to 0.5
- dest_key: int32 [1048576], P(('gx', 'gy', 'gz')), may hold values from 0 to 127, as said below
- cell_a: int32 [1048576], P(('gx', 'gy', 'gz')), may hold values from 0 to 255
- cell_b: int32 [1048576], P(('gx', 'gy', 'gz')), may hold values from 0 to 127
- velocity: float32 [2, 1024, 4096], P(None, 'gx', ('gy', 'gz')), may hold values from -6 to 6
Outputs:
- binned: float32 [8, 4194304], P(None, ('gx', 'gy', 'gz'))
- binned_cell: int32 [4194304], P(('gx', 'gy', 'gz'))
Inputs may be any that keep to these rules, and one draw needn't show every extreme that they name: Of the particles of one device at most 256 have any one value of dest_key, and one device is named by exactly 256 particles of every device.
All inputs are finite; a program needn't handle non-finite values.
Results may differ from a plain program's by a relative error of at most 0.0003.
Values sent between devices are 32-bit elements; how exact they have to be, the bound alone decides.
No kernel may reach another device: no remote copies, remote signals or barrier semaphores. Data moves between devices by JAX's collectives and lax.ppermute only.
A program may use at most 64 MiB of HBM per device.

v0:
```python
import math

import jax
import jax.numpy as jnp
from jax import lax
from jax.sharding import Mesh
from jax.sharding import PartitionSpec as P

GX_GY_GZ = ("gx", "gy_0", "gy_1", "gz")
GY_GZ = ("gy_0", "gy_1", "gz")


step_length = 0.5


def extended(x, sides, width):
    for axis, dim in sides:
        peers, length = (lax.axis_size(axis), x.shape[dim])
        up = [(i, (i + 1) % peers) for i in range(peers - 1)]
        down = [(j, i) for i, j in up]
        last = lax.slice_in_dim(x, length - width, length, axis=dim)
        initial = lax.slice_in_dim(x, 0, width, axis=dim)
        before = lax.ppermute(last, axis, up)
        after = lax.ppermute(initial, axis, down)
        x = jnp.concatenate([before, x, after], axis=dim)
    return x


def split_up(x, dim, peers):
    before, after = (x.shape[:dim], x.shape[dim + 1 :])
    return jnp.moveaxis(x.reshape(*before, peers, -1, *after), dim, 0)


def in_order(pieces, dim):
    pieces = jnp.moveaxis(pieces, 0, dim)
    lengths = pieces.shape
    return pieces.reshape(*lengths[:dim], lengths[dim] * lengths[dim + 1], *lengths[dim + 2 :])


def turned_blocks(pieces, axes, sequence):
    lengths = [lax.axis_size(a) for a in axes]
    pieces = pieces.reshape(*lengths, *pieces.shape[1:])
    for k in sequence:
        pieces = lax.all_to_all(pieces, axes[k], split_axis=k, concat_axis=k, tiled=True)
    return pieces.reshape(-1, *pieces.shape[len(axes) :])


def core_and_chips(x, groups, sequence, split_dim, concat_dim):
    peers = lax.axis_size(groups[0]) * lax.axis_size(groups[1])
    pieces = split_up(x, split_dim, peers)
    return in_order(turned_blocks(pieces, groups, sequence), concat_dim)


def quad_weights(frac):
    return (0.5 * frac * (frac - 1.0), 1.0 - frac * frac, 0.5 * frac * (frac + 1.0))


def counted_ranks(dest_key, owners):
    block_size = math.gcd(dest_key.shape[0], 1024)
    owner_ids = lax.iota(jnp.int32, owners)
    lower = (
        lax.iota(jnp.int32, block_size)[:, None] > lax.iota(jnp.int32, block_size)[None, :]
    ).astype(jnp.bfloat16)

    def rank_block(seen_counts, keys_block):
        one_hot = (keys_block[:, None] == owner_ids[None, :]).astype(jnp.float32)
        before = jnp.dot(lower, one_hot.astype(jnp.bfloat16), preferred_element_type=jnp.float32)
        block_ranks = jnp.sum((before + seen_counts[None, :]) * one_hot, axis=1)
        return (seen_counts + jnp.sum(one_hot, axis=0), block_ranks.astype(jnp.int32))

    start_counts = jnp.zeros((owners,), jnp.float32)
    unused, ranks = lax.scan(rank_block, start_counts, dest_key.reshape(-1, block_size))
    return ranks.reshape(-1)


def bucket_rows(payload, dest_key, ranking, owners, capacity):
    count = dest_key.shape[0]
    block_size = math.gcd(count, 1024)
    owner_ids = lax.iota(jnp.int32, owners)
    rank_ids = lax.iota(jnp.int32, capacity)
    rows = payload.shape[0]

    def add_block(total, index):
        start = index * block_size
        keys_block = lax.dynamic_slice_in_dim(dest_key, start, block_size, 0)
        ranks_block = lax.dynamic_slice_in_dim(ranking, start, block_size, 0)
        values = lax.dynamic_slice_in_dim(payload, start, block_size, 1)
        owner_hot = (keys_block[:, None] == owner_ids[None, :]).astype(jnp.float32)
        rank_hot = (ranks_block[:, None] == rank_ids[None, :]).astype(jnp.float32)
        spread = values[:, :, None] * rank_hot[None, :, :]
        placed = lax.dot_general(
            spread,
            owner_hot,
            (((1,), (0,)), ((), ())),
            precision=lax.Precision.HIGHEST,
            preferred_element_type=jnp.float32,
        )
        return (total + placed, None)

    start_total = jnp.zeros((rows, capacity, owners), jnp.float32)
    total, unused = lax.scan(
        add_block, start_total, jnp.arange(count // block_size, dtype=jnp.int32)
    )
    return jnp.transpose(total, (0, 2, 1))


def shards(particles, dest_key, cell_a, cell_b, velocity):
    owners = lax.axis_size(GX_GY_GZ)
    particle_count = particles.shape[1]
    capacity = 4 * particle_count // owners
    tile_height = velocity.shape[1]
    tile_width = velocity.shape[2]
    ranking = counted_ranks(dest_key, owners)
    cell_shifted = (cell_a * tile_width + cell_b + 1).astype(jnp.float32)
    payload = jnp.concatenate([particles, cell_shifted[None, :]], axis=0)
    placed = bucket_rows(payload, dest_key, ranking, owners, capacity)
    outgoing = jnp.concatenate([placed[0:8], placed[8:9] - 1.0], axis=0)
    padded = extended(velocity, (("gx", 1), (GY_GZ, 2)), 1)
    padded_width = tile_width + 2
    both_fields = jnp.concatenate([padded[0], padded[1]], axis=1)
    row_ids = lax.iota(jnp.int32, tile_height + 2)
    col_ids = lax.iota(jnp.int32, padded_width)

    def interpolate(arrived_block):
        cell_ids = arrived_block[8].astype(jnp.int32)
        is_live = cell_ids >= 0
        safe_ids = jnp.maximum(cell_ids, 0)
        node_row = safe_ids // tile_width
        node_col = safe_ids % tile_width
        weights_a = quad_weights(arrived_block[0])
        weights_b = quad_weights(arrived_block[1])
        row_weight = jnp.zeros((cell_ids.shape[0], tile_height + 2), jnp.float32)
        col_weight = jnp.zeros((cell_ids.shape[0], padded_width), jnp.float32)
        for shift in range(3):
            row_weight = row_weight + weights_a[shift][:, None] * (
                node_row[:, None] + shift == row_ids[None, :]
            ).astype(jnp.float32)
            col_weight = col_weight + weights_b[shift][:, None] * (
                node_col[:, None] + shift == col_ids[None, :]
            ).astype(jnp.float32)
        rows_mixed = jnp.dot(
            row_weight,
            both_fields,
            precision=lax.Precision.HIGHEST,
            preferred_element_type=jnp.float32,
        )
        speed_first = jnp.sum(rows_mixed[:, :padded_width] * col_weight, axis=1)
        speed_second = jnp.sum(rows_mixed[:, padded_width:] * col_weight, axis=1)
        speed = jnp.stack([speed_first, speed_second], axis=0)
        return jnp.where(is_live[None], step_length * speed, 0.0)

    arrived = core_and_chips(outgoing, (("gx", "gy_0", "gy_1"), "gz"), (1, 0), 1, 1)
    flat = arrived.reshape(9, -1)
    count = flat.shape[1]
    block_size = math.gcd(count, 2048)

    def one_block(index):
        return interpolate(lax.dynamic_slice_in_dim(flat, index * block_size, block_size, 1))

    displace = lax.map(one_block, jnp.arange(count // block_size, dtype=jnp.int32))
    displace = jnp.transpose(displace, (1, 0, 2)).reshape(2, count)
    advanced = jnp.concatenate([flat[0:2], flat[2:4] + displace, flat[4:8]], axis=0)
    cell_ids = flat[8].astype(jnp.int32)
    advanced, cell_rows = (
        advanced.reshape((8,) + arrived.shape[1:]),
        cell_ids.reshape((1,) + arrived.shape[1:]),
    )
    binned = advanced.reshape(8, -1)
    binned_cell = cell_rows.reshape(-1)
    return (binned, binned_cell)


def solution(mesh):
    split = Mesh(
        mesh.devices.reshape(mesh.shape["gx"], 4, 4, mesh.shape["gz"]), ("gx", "gy_0", "gy_1", "gz")
    )
    in_specs = (P(None, GX_GY_GZ), P(GX_GY_GZ), P(GX_GY_GZ), P(GX_GY_GZ), P(None, "gx", GY_GZ))
    out_specs = (P(None, GX_GY_GZ), P(GX_GY_GZ))
    return jax.shard_map(
        shards, mesh=split, in_specs=in_specs, out_specs=out_specs, check_vma=False
    )
```

profile of v0, /device:TPU:43, one launch (start us, length us, event | category | flops | bytes accessed | tf_op | source)
XLA Modules:
  0.0 259.1 jit_solution(3912188636909918199)
XLA Ops:
  0.7 0.8 reshape.317
  1.5 7.5 %while.40 = (s32[]{:T(128)}, f32[128]{0:T(128)S(1)}, s32[8,1024]{1,0:T(8,128)S(1)}, s32[8,1024]{1,0:T(8,128)S(1)}, s32[]{:T(128)}, /*index=5*/s32[]{:T(128)}) while((s32[]{:T(128)}, f32[128]{0:T(128)S(1)}, s32[8,1024]{1,0:T(8,128)S(1)}, s32[8,1024]{1,0:T(8,128)S(1)}, s32[]{:T(128)}, /*index=5*/s32[]{:T(128)}) %tuple.104), condition=%wide.region_3.4_spmd.clone, body=%wide.region_0.3_spmd.clone.sunk | while | flops 271843456 | bytes 40023 | solution.py:72
  9.1 59.6 %while.41 = (s32[]{:T(128)}, f32[9,256,128]{2,1,0:T(8,128)S(1)}, s32[8]{0:T(128)S(1)}, f32[9,8192]{1,0:T(8,128)S(1)}, s32[8192]{0:T(1024)S(1)}, /*index=5*/s32[8...) while((s32[]{:T(128)}, f32[9,256,128]{2,1,0:T(8,128)S(1)}, s32[8]{0:T(128)S(1)}, ...), condition=%wide.region_5.6_spmd.clone, body=%wide.region_4.5_spmd.clone.sunk | while | flops 3627483136 | bytes 4591797 | solution.py:101
  10.6 0.7 dynamic_slice.54
  11.3 5.3 %fusion.85 = f32[9,256,128]{2,1,0:T(8,128)S(1)} fusion(f32[1024,256]{0,1:T(8,128)S(1)} %fusion.84, f32[9,1024]{1,0:T(8,128)S(1)} %constant_dynamic-slice_fusion.6, f32[9,256,128]{2,1,0:T(8,128)S(1)} %get-tuple-element.513, pred[]{:T(512)S(6)} %compare.16, s32[1024]{0:T(1024)S(1)} %dynamic_slice.54), kind=kOutput, calls=%fused_computation.23.clone.1 | convolution fusion | flops 3626958848 | bytes 3448833 | tf_op jit(solution)/shard_map/while/body/eval_jaxpr/dot_general | solution.py:91
  18.7 5.3 %fusion.85 = f32[9,256,128]{2,1,0:T(8,128)S(1)} fusion(f32[1024,256]{0,1:T(8,128)S(1)} %fusion.84, f32[9,1024]{1,0:T(8,128)S(1)} %constant_dynamic-slice_fusion.6, f32[9,256,128]{2,1,0:T(8,128)S(1)} %get-tuple-element.513, pred[]{:T(512)S(6)} %compare.16, s32[1024]{0:T(1024)S(1)} %dynamic_slice.54), kind=kOutput, calls=%fused_computation.23.clone.1 | convolution fusion | flops 3626958848 | bytes 3448833 | tf_op jit(solution)/shard_map/while/body/eval_jaxpr/dot_general | solution.py:91
  25.5 0.7 dynamic_slice.54
  26.2 5.3 %fusion.85 = f32[9,256,128]{2,1,0:T(8,128)S(1)} fusion(f32[1024,256]{0,1:T(8,128)S(1)} %fusion.84, f32[9,1024]{1,0:T(8,128)S(1)} %constant_dynamic-slice_fusion.6, f32[9,256,128]{2,1,0:T(8,128)S(1)} %get-tuple-element.513, pred[]{:T(512)S(6)} %compare.16, s32[1024]{0:T(1024)S(1)} %dynamic_slice.54), kind=kOutput, calls=%fused_computation.23.clone.1 | convolution fusion | flops 3626958848 | bytes 3448833 | tf_op jit(solution)/shard_map/while/body/eval_jaxpr/dot_general | solution.py:91
  33.6 5.3 %fusion.85 = f32[9,256,128]{2,1,0:T(8,128)S(1)} fusion(f32[1024,256]{0,1:T(8,128)S(1)} %fusion.84, f32[9,1024]{1,0:T(8,128)S(1)} %constant_dynamic-slice_fusion.6, f32[9,256,128]{2,1,0:T(8,128)S(1)} %get-tuple-element.513, pred[]{:T(512)S(6)} %compare.16, s32[1024]{0:T(1024)S(1)} %dynamic_slice.54), kind=kOutput, calls=%fused_computation.23.clone.1 | convolution fusion | flops 3626958848 | bytes 3448833 | tf_op jit(solution)/shard_map/while/body/eval_jaxpr/dot_general | solution.py:91
  40.4 0.7 dynamic_slice.54
  41.1 5.3 %fusion.85 = f32[9,256,128]{2,1,0:T(8,128)S(1)} fusion(f32[1024,256]{0,1:T(8,128)S(1)} %fusion.84, f32[9,1024]{1,0:T(8,128)S(1)} %constant_dynamic-slice_fusion.6, f32[9,256,128]{2,1,0:T(8,128)S(1)} %get-tuple-element.513, pred[]{:T(512)S(6)} %compare.16, s32[1024]{0:T(1024)S(1)} %dynamic_slice.54), kind=kOutput, calls=%fused_computation.23.clone.1 | convolution fusion | flops 3626958848 | bytes 3448833 | tf_op jit(solution)/shard_map/while/body/eval_jaxpr/dot_general | solution.py:91
  48.5 5.3 %fusion.85 = f32[9,256,128]{2,1,0:T(8,128)S(1)} fusion(f32[1024,256]{0,1:T(8,128)S(1)} %fusion.84, f32[9,1024]{1,0:T(8,128)S(1)} %constant_dynamic-slice_fusion.6, f32[9,256,128]{2,1,0:T(8,128)S(1)} %get-tuple-element.513, pred[]{:T(512)S(6)} %compare.16, s32[1024]{0:T(1024)S(1)} %dynamic_slice.54), kind=kOutput, calls=%fused_computation.23.clone.1 | convolution fusion | flops 3626958848 | bytes 3448833 | tf_op jit(solution)/shard_map/while/body/eval_jaxpr/dot_general | solution.py:91
  56.0 5.3 %fusion.85 = f32[9,256,128]{2,1,0:T(8,128)S(1)} fusion(f32[1024,256]{0,1:T(8,128)S(1)} %fusion.84, f32[9,1024]{1,0:T(8,128)S(1)} %constant_dynamic-slice_fusion.6, f32[9,256,128]{2,1,0:T(8,128)S(1)} %get-tuple-element.513, pred[]{:T(512)S(6)} %compare.16, s32[1024]{0:T(1024)S(1)} %dynamic_slice.54), kind=kOutput, calls=%fused_computation.23.clone.1 | convolution fusion | flops 3626958848 | bytes 3448833 | tf_op jit(solution)/shard_map/while/body/eval_jaxpr/dot_general | solution.py:91
  63.4 5.3 %fusion.85 = f32[9,256,128]{2,1,0:T(8,128)S(1)} fusion(f32[1024,256]{0,1:T(8,128)S(1)} %fusion.84, f32[9,1024]{1,0:T(8,128)S(1)} %constant_dynamic-slice_fusion.6, f32[9,256,128]{2,1,0:T(8,128)S(1)} %get-tuple-element.513, pred[]{:T(512)S(6)} %compare.16, s32[1024]{0:T(1024)S(1)} %dynamic_slice.54), kind=kOutput, calls=%fused_computation.23.clone.1 | convolution fusion | flops 3626958848 | bytes 3448833 | tf_op jit(solution)/shard_map/while/body/eval_jaxpr/dot_general | solution.py:91
  69.0 1.8 copy.25
  70.8 0.8 copy.26
  71.6 5.0 %all_to_all.10 = f32[64,2,9,1,256]{4,3,2,0,1:T(1,128)S(1)} all-to-all(f32[64,2,9,1,256]{4,3,2,0,1:T(1,128)S(1)} %copy.26), channel_id=1, replica_groups=mesh['gx'=4,'gy_0'=4,'gy_1'=4,'gz'=2] {'gz'}, dimensions={1} | all-to-all | bytes 2359296 | tf_op jit(solution)/shard_map/all_to_all | solution.py:44
  76.6 1.8 copy.27
  78.4 10.5 %all-to-all-start.1 = ((f32[64,2,9,1,256]{4,3,2,1,0:T(1,128)}), f32[64,2,9,1,256]{4,3,2,1,0:T(1,128)S(1)}, u32[]{:S(2)}, u32[]{:S(2)}) async-start(f32[64,2,9,1,256]{4,3,2,1,0:T(1,128)} %copy.27), calls=%async_computation.1 | async-start | bytes 2359296 | tf_op jit(solution)/shard_map/all_to_all | solution.py:44
  88.9 3.2 %collective-permute-start = (f32[2,1,128]{2,1,0:T(1,128)S(1)}, f32[2,1,128]{2,1,0:T(1,128)S(1)}, u32[]{:S(2)}, u32[]{:S(2)}) collective-permute-start(f32[2,1,128]{2,1,0:T(1,128)S(1)} %get-tuple-element.349), channel_id=1, source_target_pairs={{0,32},{32,64},{64,96},{1,33},{33,65},{65,97},{2,34},{34,66},{66,9... | collective-permute-start | bytes 3080 | tf_op jit(solution)/shard_map/ppermute | solution.py:23
  92.2 2.1 collective-permute-start.1
  94.2 1.8 collective-permute-done
  96.0 1.5 collective-permute-done.1
  97.7 10.0 %collective-permute-start.2 = (f32[2,258,1]{2,1,0:T(8,128)S(1)}, f32[2,258,1]{2,1,0:T(8,128)S(1)}, u32[]{:S(2)}, u32[]{:S(2)}) collective-permute-start(f32[2,258,1]{2,1,0:T(8,128)S(1)} %get-tuple-element.347), channel_id=1, source_target_pairs={{0,1},{1,2},{2,3},{3,4},{4,5},{5,6},{6,7},{7,8},{8,9},{9,10},{10,1... | collective-permute-start | bytes 6200 | tf_op jit(solution)/shard_map/ppermute | solution.py:23
  107.7 2.1 collective-permute-start.3
  109.8 1.3 collective-permute-done.2
  111.1 4.4 %collective-permute-done.3 = f32[2,258,1]{2,1,0:T(8,128)S(1)} collective-permute-done((f32[2,258,1]{2,1,0:T(8,128)S(1)}, f32[2,258,1]{2,1,0:T(8,128)S(1)}, u32[]{:S(2)}, u32[]{:S(2)}) %collective-permute-start.3) | collective-permute-done | bytes 2096 | tf_op jit(solution)/shard_map/ppermute | solution.py:24
  115.8 0.9 pad_maximum_fusion.3
  117.6 0.7 slice_convert_fusion
  118.5 1.2 copy.35
  119.7 137.0 %while.39 = (s32[]{:T(128)}, f32[16,2,2048]{2,1,0:T(2,128)S(1)}, s32[16]{0:T(128)S(1)}, f32[9,32768]{1,0:T(8,128)S(1)}, f32[258,260]{1,0:T(8,128)}, /*index=5*/s...) while((s32[]{:T(128)}, f32[16,2,2048]{2,1,0:T(2,128)S(1)}, ...), condition=%wide.region_9.10_spmd.clone.clone, body=%wide.region_6.9_spmd.clone.clone.sunk | while | flops 1656059904 | bytes 4856059 | solution.py:160
  121.4 6.3 %fusion.76 = f32[2048,260]{0,1:T(8,128)S(1)} fusion(f32[258,260]{1,0:T(8,128)} %get-tuple-element.558, f32[2048]{0:T(1024)S(1)} %bitcast.130, s32[2048]{0:T(1024)S(1)} %broadcast_add_fusion.5, f32[2048]{0:T(1024)S(1)} %bitcast.129, s32[2048]{0:T(1024)S(1)} %get-tuple-element.461, f32[2048]{0:T(1024)S(1)} %bitcast.128, s32[2048]{0:T(1024)S(1)} %get-tuple-element.459), kind=kOutput, calls=%fused_computation.33.clone.1 | convolution fusion | flops 1652785152 | bytes 2447392 | tf_op jit(solution)/shard_map/while/body/eval_jaxpr/dot_general | solution.py:141
  129.9 6.3 %fusion.76 = f32[2048,260]{0,1:T(8,128)S(1)} fusion(f32[258,260]{1,0:T(8,128)} %get-tuple-element.558, f32[2048]{0:T(1024)S(1)} %bitcast.130, s32[2048]{0:T(1024)S(1)} %broadcast_add_fusion.5, f32[2048]{0:T(1024)S(1)} %bitcast.129, s32[2048]{0:T(1024)S(1)} %get-tuple-element.461, f32[2048]{0:T(1024)S(1)} %bitcast.128, s32[2048]{0:T(1024)S(1)} %get-tuple-element.459), kind=kOutput, calls=%fused_computation.33.clone.1 | convolution fusion | flops 1652785152 | bytes 2447392 | tf_op jit(solution)/shard_map/while/body/eval_jaxpr/dot_general | solution.py:141
  138.5 6.3 %fusion.76 = f32[2048,260]{0,1:T(8,128)S(1)} fusion(f32[258,260]{1,0:T(8,128)} %get-tuple-element.558, f32[2048]{0:T(1024)S(1)} %bitcast.130, s32[2048]{0:T(1024)S(1)} %broadcast_add_fusion.5, f32[2048]{0:T(1024)S(1)} %bitcast.129, s32[2048]{0:T(1024)S(1)} %get-tuple-element.461, f32[2048]{0:T(1024)S(1)} %bitcast.128, s32[2048]{0:T(1024)S(1)} %get-tuple-element.459), kind=kOutput, calls=%fused_computation.33.clone.1 | convolution fusion | flops 1652785152 | bytes 2447392 | tf_op jit(solution)/shard_map/while/body/eval_jaxpr/dot_general | solution.py:141
  147.1 6.3 %fusion.76 = f32[2048,260]{0,1:T(8,128)S(1)} fusion(f32[258,260]{1,0:T(8,128)} %get-tuple-element.558, f32[2048]{0:T(1024)S(1)} %bitcast.130, s32[2048]{0:T(1024)S(1)} %broadcast_add_fusion.5, f32[2048]{0:T(1024)S(1)} %bitcast.129, s32[2048]{0:T(1024)S(1)} %get-tuple-element.461, f32[2048]{0:T(1024)S(1)} %bitcast.128, s32[2048]{0:T(1024)S(1)} %get-tuple-element.459), kind=kOutput, calls=%fused_computation.33.clone.1 | convolution fusion | flops 1652785152 | bytes 2447392 | tf_op jit(solution)/shard_map/while/body/eval_jaxpr/dot_general | solution.py:141
  155.6 6.3 %fusion.76 = f32[2048,260]{0,1:T(8,128)S(1)} fusion(f32[258,260]{1,0:T(8,128)} %get-tuple-element.558, f32[2048]{0:T(1024)S(1)} %bitcast.130, s32[2048]{0:T(1024)S(1)} %broadcast_add_fusion.5, f32[2048]{0:T(1024)S(1)} %bitcast.129, s32[2048]{0:T(1024)S(1)} %get-tuple-element.461, f32[2048]{0:T(1024)S(1)} %bitcast.128, s32[2048]{0:T(1024)S(1)} %get-tuple-element.459), kind=kOutput, calls=%fused_computation.33.clone.1 | convolution fusion | flops 1652785152 | bytes 2447392 | tf_op jit(solution)/shard_map/while/body/eval_jaxpr/dot_general | solution.py:141
  164.2 6.3 %fusion.76 = f32[2048,260]{0,1:T(8,128)S(1)} fusion(f32[258,260]{1,0:T(8,128)} %get-tuple-element.558, f32[2048]{0:T(1024)S(1)} %bitcast.130, s32[2048]{0:T(1024)S(1)} %broadcast_add_fusion.5, f32[2048]{0:T(1024)S(1)} %bitcast.129, s32[2048]{0:T(1024)S(1)} %get-tuple-element.461, f32[2048]{0:T(1024)S(1)} %bitcast.128, s32[2048]{0:T(1024)S(1)} %get-tuple-element.459), kind=kOutput, calls=%fused_computation.33.clone.1 | convolution fusion | flops 1652785152 | bytes 2447392 | tf_op jit(solution)/shard_map/while/body/eval_jaxpr/dot_general | solution.py:141
  172.7 6.3 %fusion.76 = f32[2048,260]{0,1:T(8,128)S(1)} fusion(f32[258,260]{1,0:T(8,128)} %get-tuple-element.558, f32[2048]{0:T(1024)S(1)} %bitcast.130, s32[2048]{0:T(1024)S(1)} %broadcast_add_fusion.5, f32[2048]{0:T(1024)S(1)} %bitcast.129, s32[2048]{0:T(1024)S(1)} %get-tuple-element.461, f32[2048]{0:T(1024)S(1)} %bitcast.128, s32[2048]{0:T(1024)S(1)} %get-tuple-element.459), kind=kOutput, calls=%fused_computation.33.clone.1 | convolution fusion | flops 1652785152 | bytes 2447392 | tf_op jit(solution)/shard_map/while/body/eval_jaxpr/dot_general | solution.py:141
  181.3 6.3 %fusion.76 = f32[2048,260]{0,1:T(8,128)S(1)} fusion(f32[258,260]{1,0:T(8,128)} %get-tuple-element.558, f32[2048]{0:T(1024)S(1)} %bitcast.130, s32[2048]{0:T(1024)S(1)} %broadcast_add_fusion.5, f32[2048]{0:T(1024)S(1)} %bitcast.129, s32[2048]{0:T(1024)S(1)} %get-tuple-element.461, f32[2048]{0:T(1024)S(1)} %bitcast.128, s32[2048]{0:T(1024)S(1)} %get-tuple-element.459), kind=kOutput, calls=%fused_computation.33.clone.1 | convolution fusion | flops 1652785152 | bytes 2447392 | tf_op jit(solution)/shard_map/while/body/eval_jaxpr/dot_general | solution.py:141
  189.9 6.3 %fusion.76 = f32[2048,260]{0,1:T(8,128)S(1)} fusion(f32[258,260]{1,0:T(8,128)} %get-tuple-element.558, f32[2048]{0:T(1024)S(1)} %bitcast.130, s32[2048]{0:T(1024)S(1)} %broadcast_add_fusion.5, f32[2048]{0:T(1024)S(1)} %bitcast.129, s32[2048]{0:T(1024)S(1)} %get-tuple-element.461, f32[2048]{0:T(1024)S(1)} %bitcast.128, s32[2048]{0:T(1024)S(1)} %get-tuple-element.459), kind=kOutput, calls=%fused_computation.33.clone.1 | convolution fusion | flops 1652785152 | bytes 2447392 | tf_op jit(solution)/shard_map/while/body/eval_jaxpr/dot_general | solution.py:141
  198.4 6.3 %fusion.76 = f32[2048,260]{0,1:T(8,128)S(1)} fusion(f32[258,260]{1,0:T(8,128)} %get-tuple-element.558, f32[2048]{0:T(1024)S(1)} %bitcast.130, s32[2048]{0:T(1024)S(1)} %broadcast_add_fusion.5, f32[2048]{0:T(1024)S(1)} %bitcast.129, s32[2048]{0:T(1024)S(1)} %get-tuple-element.461, f32[2048]{0:T(1024)S(1)} %bitcast.128, s32[2048]{0:T(1024)S(1)} %get-tuple-element.459), kind=kOutput, calls=%fused_computation.33.clone.1 | convolution fusion | flops 1652785152 | bytes 2447392 | tf_op jit(solution)/shard_map/while/body/eval_jaxpr/dot_general | solution.py:141
  207.0 6.3 %fusion.76 = f32[2048,260]{0,1:T(8,128)S(1)} fusion(f32[258,260]{1,0:T(8,128)} %get-tuple-element.558, f32[2048]{0:T(1024)S(1)} %bitcast.130, s32[2048]{0:T(1024)S(1)} %broadcast_add_fusion.5, f32[2048]{0:T(1024)S(1)} %bitcast.129, s32[2048]{0:T(1024)S(1)} %get-tuple-element.461, f32[2048]{0:T(1024)S(1)} %bitcast.128, s32[2048]{0:T(1024)S(1)} %get-tuple-element.459), kind=kOutput, calls=%fused_computation.33.clone.1 | convolution fusion | flops 1652785152 | bytes 2447392 | tf_op jit(solution)/shard_map/while/body/eval_jaxpr/dot_general | solution.py:141
  215.5 6.3 %fusion.76 = f32[2048,260]{0,1:T(8,128)S(1)} fusion(f32[258,260]{1,0:T(8,128)} %get-tuple-element.558, f32[2048]{0:T(1024)S(1)} %bitcast.130, s32[2048]{0:T(1024)S(1)} %broadcast_add_fusion.5, f32[2048]{0:T(1024)S(1)} %bitcast.129, s32[2048]{0:T(1024)S(1)} %get-tuple-element.461, f32[2048]{0:T(1024)S(1)} %bitcast.128, s32[2048]{0:T(1024)S(1)} %get-tuple-element.459), kind=kOutput, calls=%fused_computation.33.clone.1 | convolution fusion | flops 1652785152 | bytes 2447392 | tf_op jit(solution)/shard_map/while/body/eval_jaxpr/dot_general | solution.py:141
  224.1 6.3 %fusion.76 = f32[2048,260]{0,1:T(8,128)S(1)} fusion(f32[258,260]{1,0:T(8,128)} %get-tuple-element.558, f32[2048]{0:T(1024)S(1)} %bitcast.130, s32[2048]{0:T(1024)S(1)} %broadcast_add_fusion.5, f32[2048]{0:T(1024)S(1)} %bitcast.129, s32[2048]{0:T(1024)S(1)} %get-tuple-element.461, f32[2048]{0:T(1024)S(1)} %bitcast.128, s32[2048]{0:T(1024)S(1)} %get-tuple-element.459), kind=kOutput, calls=%fused_computation.33.clone.1 | convolution fusion | flops 1652785152 | bytes 2447392 | tf_op jit(solution)/shard_map/while/body/eval_jaxpr/dot_general | solution.py:141
  232.7 6.3 %fusion.76 = f32[2048,260]{0,1:T(8,128)S(1)} fusion(f32[258,260]{1,0:T(8,128)} %get-tuple-element.558, f32[2048]{0:T(1024)S(1)} %bitcast.130, s32[2048]{0:T(1024)S(1)} %broadcast_add_fusion.5, f32[2048]{0:T(1024)S(1)} %bitcast.129, s32[2048]{0:T(1024)S(1)} %get-tuple-element.461, f32[2048]{0:T(1024)S(1)} %bitcast.128, s32[2048]{0:T(1024)S(1)} %get-tuple-element.459), kind=kOutput, calls=%fused_computation.33.clone.1 | convolution fusion | flops 1652785152 | bytes 2447392 | tf_op jit(solution)/shard_map/while/body/eval_jaxpr/dot_general | solution.py:141
  241.2 6.3 %fusion.76 = f32[2048,260]{0,1:T(8,128)S(1)} fusion(f32[258,260]{1,0:T(8,128)} %get-tuple-element.558, f32[2048]{0:T(1024)S(1)} %bitcast.130, s32[2048]{0:T(1024)S(1)} %broadcast_add_fusion.5, f32[2048]{0:T(1024)S(1)} %bitcast.129, s32[2048]{0:T(1024)S(1)} %get-tuple-element.461, f32[2048]{0:T(1024)S(1)} %bitcast.128, s32[2048]{0:T(1024)S(1)} %get-tuple-element.459), kind=kOutput, calls=%fused_computation.33.clone.1 | convolution fusion | flops 1652785152 | bytes 2447392 | tf_op jit(solution)/shard_map/while/body/eval_jaxpr/dot_general | solution.py:141
  249.8 6.3 %fusion.76 = f32[2048,260]{0,1:T(8,128)S(1)} fusion(f32[258,260]{1,0:T(8,128)} %get-tuple-element.558, f32[2048]{0:T(1024)S(1)} %bitcast.130, s32[2048]{0:T(1024)S(1)} %broadcast_add_fusion.5, f32[2048]{0:T(1024)S(1)} %bitcast.129, s32[2048]{0:T(1024)S(1)} %get-tuple-element.461, f32[2048]{0:T(1024)S(1)} %bitcast.128, s32[2048]{0:T(1024)S(1)} %get-tuple-element.459), kind=kOutput, calls=%fused_computation.33.clone.1 | convolution fusion | flops 1652785152 | bytes 2447392 | tf_op jit(solution)/shard_map/while/body/eval_jaxpr/dot_general | solution.py:141
  257.8 1.3 pad_maximum_fusion
  (249 shorter events, 42.9 us)
Async XLA Ops:
  1.4 7.6 %copy-start.2 = (s32[8192]{0:T(1024)S(1)}, s32[8192]{0:T(1024)}, u32[]{:S(2)}) copy-start(s32[8192]{0:T(1024)} %param.14) | copy-start | bytes 98308
  1.4 7.6 %copy-start.3 = (s32[8192]{0:T(1024)S(1)}, s32[8192]{0:T(1024)}, u32[]{:S(2)}) copy-start(s32[8192]{0:T(1024)} %param.13) | copy-start | bytes 98308
  1.5 7.6 %copy-start.1 = (f32[8,8192]{1,0:T(8,128)S(1)}, f32[8,8192]{1,0:T(8,128)}, u32[]{:S(2)}) copy-start(f32[8,8192]{1,0:T(8,128)} %param.11) | copy-start | bytes 786436
  78.4 10.5 %copy-start = (f32[2,256,128]{2,1,0:T(8,128)S(1)}, f32[2,256,128]{2,1,0:T(8,128)}, u32[]{:S(2)}) copy-start(f32[2,256,128]{2,1,0:T(8,128)} %param.15) | copy-start | bytes 786436
  78.4 38.3 %all-to-all-start.1 = ((f32[64,2,9,1,256]{4,3,2,1,0:T(1,128)}), f32[64,2,9,1,256]{4,3,2,1,0:T(1,128)S(1)}, u32[]{:S(2)}, u32[]{:S(2)}) async-start(f32[64,2,9,1,256]{4,3,2,1,0:T(1,128)} %copy.27), calls=%async_computation.1 | async-start | bytes 2359296 | tf_op jit(solution)/shard_map/all_to_all | solution.py:44
  88.9 7.1 %collective-permute-start = (f32[2,1,128]{2,1,0:T(1,128)S(1)}, f32[2,1,128]{2,1,0:T(1,128)S(1)}, u32[]{:S(2)}, u32[]{:S(2)}) collective-permute-start(f32[2,1,128]{2,1,0:T(1,128)S(1)} %get-tuple-element.349), channel_id=1, source_target_pairs={{0,32},{32,64},{64,96},{1,33},{33,65},{65,97},{2,34},{34,66},{66,9... | collective-permute-start | bytes 3080 | tf_op jit(solution)/shard_map/ppermute | solution.py:23
  92.2 5.4 %collective-permute-start.1 = (f32[2,1,128]{2,1,0:T(1,128)S(1)}, f32[2,1,128]{2,1,0:T(1,128)S(1)}, u32[]{:S(2)}, u32[]{:S(2)}) collective-permute-start(f32[2,1,128]{2,1,0:T(1,128)S(1)} %get-tuple-element.350), channel_id=1, source_target_pairs={{32,0},{64,32},{96,64},{33,1},{65,33},{97,65},{34,2},{66,34},{98,6... | collective-permute-start | bytes 3080 | tf_op jit(solution)/shard_map/ppermute | solution.py:24
  97.7 13.4 %collective-permute-start.2 = (f32[2,258,1]{2,1,0:T(8,128)S(1)}, f32[2,258,1]{2,1,0:T(8,128)S(1)}, u32[]{:S(2)}, u32[]{:S(2)}) collective-permute-start(f32[2,258,1]{2,1,0:T(8,128)S(1)} %get-tuple-element.347), channel_id=1, source_target_pairs={{0,1},{1,2},{2,3},{3,4},{4,5},{5,6},{6,7},{7,8},{8,9},{9,10},{10,1... | collective-permute-start | bytes 6200 | tf_op jit(solution)/shard_map/ppermute | solution.py:23
  107.7 7.8 %collective-permute-start.3 = (f32[2,258,1]{2,1,0:T(8,128)S(1)}, f32[2,258,1]{2,1,0:T(8,128)S(1)}, u32[]{:S(2)}, u32[]{:S(2)}) collective-permute-start(f32[2,258,1]{2,1,0:T(8,128)S(1)} %get-tuple-element.348), channel_id=1, source_target_pairs={{1,0},{2,1},{3,2},{4,3},{5,4},{6,5},{7,6},{8,7},{9,8},{10,9},{11,1... | collective-permute-start | bytes 6200 | tf_op jit(solution)/shard_map/ppermute | solution.py:24
where the time goes:
time: 261 us; the launch traced here: 259 us
  matrix products  149 us (57%)
  local copies, waits for them, and re-layouts  30.6 us (12%)
  starting transfers between devices  27.9 us (11%)
  other arithmetic  18.7 us (7%)
  loops' own time  18 us (7%)
  waiting for transfers between devices  8.94 us (3%)
  blocking collectives  4.98 us (2%)
    dot_general x16, matrix products, interpolate(): jnp.dot(row_weight, both_fields, precision=lax.Precision.HIGHEST, preferr...  101 us
    dot_general x8, matrix products, add_block(): lax.dot_general(spread, owner_hot, (((1,), (0,)), ((), ())), precision=la...  42.7 us
    ppermute x2, starting transfers between devices, extended(): before = lax.ppermute(last, axis, up)  13.2 us
    another operation x1, loops' own time, shards(): lax.map(one_block, jnp.arange(count // block_size, dtype=jnp.int32))  12 us
    dynamic_slice x16, local copies, waits for them, and re-layouts, shards(): lax.map(one_block, jnp.arange(count // block_size, dtype=jnp.int32))  10.7 us
    all_to_all x1, starting transfers between devices, turned_blocks(): lax.all_to_all(pieces, axes[k], split_axis=k, concat_axis=k, tiled=True)  10.5 us
    reduce_sum x16, other arithmetic, interpolate(): speed_first = jnp.sum(rows_mixed[:, :padded_width] * col_weight, axis=1)  8.71 us
    ppermute x2, waiting for transfers between devices, extended(): after = lax.ppermute(initial, axis, down)  5.91 us
  transfers between devices with their start and end apart: 5, of which 4 were waited for; matrix products, arithmetic and copies ran while one was open for 1% of the time, Pallas kernels for 0%

commit v1 on v0

v1 whole, which is shorter than its diff:
```python
import jax, jax.numpy as jnp
from jax import lax
from jax.experimental import pallas as pl
from jax.experimental.pallas import tpu as pltpu
f32, bf16, i32 = jnp.float32, jnp.bfloat16, jnp.int32
ROWS = 18

def iota(shape, dim, dt):
    return lax.broadcasted_iota(i32, shape, dim).astype(f32).astype(dt)

def nt(a, b):
    return lax.dot_general(a, b, (((1,), (1,)), ((), ())), preferred_element_type=f32)

def nn(a, b):
    return jnp.dot(a, b, preferred_element_type=f32)

def split(v):
    hi = v.astype(bf16)
    return hi, (v - hi.astype(f32)).astype(bf16)

def bucket_kernel(p_ref, key_ref, a_ref, b_ref, out_ref, acc_ref, base_ref, rank_ref, ut_ref, hot_ref):
    PB = 256
    n = p_ref.shape[1] // PB
    out_ref[...] = jnp.zeros(out_ref.shape, f32)
    acc_ref[...] = jnp.zeros(acc_ref.shape, f32)
    base_ref[...] = jnp.zeros(base_ref.shape, f32)
    r = lax.broadcasted_iota(i32, (PB, PB), 0)
    c = lax.broadcasted_iota(i32, (PB, PB), 1)
    ut_ref[:, :PB] = jnp.where(r < c, 1.0, 0.0).astype(bf16)
    ut_ref[:, PB:] = jnp.ones((PB, 128), bf16)

    def cells(sl):
        return (a_ref[0:1, sl] * 128 + b_ref[0:1, sl] + 1).astype(f32)

    def place(sl, key, t, acc):
        low = jnp.where(key >= 64, key - 64, key)
        pick = iota((64, PB), 0, bf16) == low.astype(f32).astype(bf16)
        cols = jnp.where(iota((256, PB), 0, bf16) == t.astype(bf16), 1.0, 0.0).astype(bf16)
        rows = [p_ref[k:k + 1, sl] for k in range(8)] + [cells(sl)]
        his, los = [], []
        for v in rows:
            hi, lo = split(v)
            his.append(jnp.where(pick, hi, jnp.zeros((), bf16)))
            los.append(jnp.where(pick, lo, jnp.zeros((), bf16)))
        return nt(jnp.concatenate(his, 0), cols) + nt(jnp.concatenate(los, 0), cols)

    def body(i, carry):
        sl = pl.ds(pl.multiple_of(i * PB, PB), PB)
        key = key_ref[0:1, sl]
        oh = lax.broadcasted_iota(i32, (128, PB), 0) == key
        ohb = jnp.where(oh, 1.0, 0.0).astype(bf16)
        res = nn(ohb, ut_ref[...])
        base = base_ref[...]
        before = res[:, :PB] + jnp.concatenate([base, base], 1)
        rank = jnp.sum(jnp.where(oh, before, 0.0), axis=0, keepdims=True)
        base_ref[...] = base + res[:, PB:]
        rank_ref[0:1, sl] = rank
        t = jnp.where(rank < 128.0, rank + jnp.where(key >= 64, 128.0, 0.0), -1.0)
        acc_ref[...] += place(sl, key, t, acc_ref)
        return carry

    lax.fori_loop(0, n, body, 0)

    def flush(half):
        for k in range(9):
            for o in range(2):
                out_ref[pl.ds(o * 64 * ROWS + 9 * half + k, 64, stride=ROWS), :] = acc_ref[k * 64:(k + 1) * 64, o * 128:(o + 1) * 128]

    flush(0)
    counts = base_ref[...]
    ids = lax.broadcasted_iota(i32, (128, 128), 0).astype(f32)
    n_full = jnp.max(jnp.sum(jnp.where(counts > 128.0, 1.0, 0.0), axis=0, keepdims=True))
    hot = jnp.max(jnp.where(counts > 128.0, ids, -1.0)).astype(i32)

    @pl.when(n_full <= 1.0)
    def _():
        hot_ref[...] = jnp.zeros(hot_ref.shape, f32)

        def hot_body(i, carry):
            sl = pl.ds(pl.multiple_of(i * PB, PB), PB)
            key = key_ref[0:1, sl]
            over = jnp.where(key == hot, rank_ref[0:1, sl] - 128.0, -1.0)
            cols = jnp.where(iota((128, PB), 0, bf16) == over.astype(bf16), 1.0, 0.0).astype(bf16)
            hi, lo = split(jnp.concatenate([p_ref[:, sl], jnp.broadcast_to(cells(sl), (8, PB))], 0))
            hot_ref[...] += nt(hi, cols) + nt(lo, cols)
            return carry

        lax.fori_loop(0, n, hot_body, 0)
        at = jnp.maximum(hot, 0) * ROWS + 9
        for k in range(9):
            out_ref[pl.ds(at + k, 1), :] = hot_ref[k:k + 1, :]

    @pl.when(n_full > 1.0)
    def _():
        acc_ref[...] = jnp.zeros(acc_ref.shape, f32)

        def over_body(i, carry):
            sl = pl.ds(pl.multiple_of(i * PB, PB), PB)
            key = key_ref[0:1, sl]
            rank = rank_ref[0:1, sl]
            t = jnp.where(rank >= 128.0, rank - 128.0 + jnp.where(key >= 64, 128.0, 0.0), -1.0)
            acc_ref[...] += place(sl, key, t, acc_ref)
            return carry

        lax.fori_loop(0, n, over_body, 0)
        flush(1)

def bucket(particles, key, a, b):
    n = particles.shape[1]
    return pl.pallas_call(
        bucket_kernel,
        out_shape=jax.ShapeDtypeStruct((128 * ROWS, 128), f32),
        in_specs=[pl.BlockSpec(memory_space=pltpu.VMEM)] * 4,
        out_specs=pl.BlockSpec(memory_space=pltpu.VMEM),
        scratch_shapes=[pltpu.VMEM((576, 256), f32), pltpu.VMEM((128, 128), f32), pltpu.VMEM((1, n), f32),
                        pltpu.VMEM((256, 384), bf16), pltpu.VMEM((16, 128), f32)],
        name="bucket",
    )(particles, key.reshape(1, -1), a.reshape(1, -1), b.reshape(1, -1))

def interp_kernel(r_ref, v_ref, rows_ref, cols_ref, out_ref, cell_ref, fhi_ref, flo_ref, fe_ref):
    S = 4
    N = 256 * S
    for c in range(2):
        t = v_ref[c].T
        hi, lo = split(t)
        fhi_ref[c * 128:(c + 1) * 128, :] = hi
        flo_ref[c * 128:(c + 1) * 128, :] = lo
    hi, lo = split(cols_ref[:, :256])
    fhi_ref[256:272, :] = hi
    flo_ref[256:272, :] = lo
    fe_ref[...] = rows_ref[...]

    def weights(t):
        return 0.5 * t * (t - 1.0), 1.0 - t * t, 0.5 * t * (t + 1.0)

    def body(i, carry):
        for u in range(S):
            s = i * S + u
            base = s * ROWS
            x0 = r_ref[pl.ds(base, 8), :]
            x1 = r_ref[pl.ds(base + 9, 8), :]
            cell = jnp.concatenate([r_ref[pl.ds(base + 8, 1), :], r_ref[pl.ds(base + 17, 1), :]], 1)
            ci = cell.astype(i32) - 1
            live = ci >= 0
            a = jnp.where(live, ci >> 7, -8).astype(f32)
            b = (ci & 127).astype(f32)
            f = jnp.concatenate([x0[0:1], x1[0:1]], 1)
            g = jnp.concatenate([x0[1:2], x1[1:2]], 1)
            wm, w0, wp = [0.5 * w for w in weights(f)]
            gm, g0, gp = weights(g)
            ab = a.astype(bf16)
            am, ap = (a - 1.0).astype(bf16), (a + 1.0).astype(bf16)
            rowid = iota((256, 256), 0, bf16)
            m0, m1, m2 = rowid == am, rowid == ab, rowid == ap
            z = jnp.zeros((), bf16)
            (wmh, wml), (w0h, w0l), (wph, wpl) = split(wm), split(w0), split(wp)
            whi = jnp.where(m0, wmh, jnp.where(m1, w0h, jnp.where(m2, wph, z)))
            wlo = jnp.where(m0, wml, jnp.where(m1, w0l, jnp.where(m2, wpl, z)))
            et = jnp.where(a == 0.0, wm, 0.0)
            eb = jnp.where(a == 255.0, wp, 0.0)
            (eth, etl), (ebh, ebl) = split(et), split(eb)
            k = lax.broadcasted_iota(i32, (16, 256), 0)
            we = jnp.where(k == 0, eth.astype(f32), jnp.where(k == 1, ebh.astype(f32), jnp.where(k == 2, eth.astype(f32),
                 jnp.where(k == 3, ebh.astype(f32), jnp.where(k == 4, etl.astype(f32), jnp.where(k == 5, ebl.astype(f32), 0.0))))))
            we = we.astype(bf16)
            fhi = fhi_ref[...]
            R = nn(fhi, whi) + nn(flo_ref[...], whi) + nn(fhi, wlo) + nn(fe_ref[...], we)
            col = iota((128, 256), 0, f32)
            cw = jnp.where(col == b - 1.0, gm, jnp.where(col == b, g0, jnp.where(col == b + 1.0, gp, 0.0)))
            el = jnp.where(b == 0.0, gm, 0.0)
            er = jnp.where(b == 127.0, gp, 0.0)
            s0 = jnp.sum(R[0:128] * cw, axis=0, keepdims=True) + R[256:257] * el + R[257:258] * er
            s1 = jnp.sum(R[128:256] * cw, axis=0, keepdims=True) + R[258:259] * el + R[259:260] * er
            rid = lax.broadcasted_iota(i32, (8, 256), 0)
            d = jnp.where(rid == 2, s0, jnp.where(rid == 3, s1, 0.0))
            at = pl.multiple_of(s * 256, 256)
            out_ref[:, pl.ds(at, 256)] = jnp.concatenate([x0, x1], 1) + d
            cell_ref[0:1, pl.ds(at, 256)] = ci
        return carry

    lax.fori_loop(0, 128 // S, body, 0)

def interp(recv, velocity, top, bottom, left, right):
    zero = jnp.zeros((2, 1), f32)
    cols = jnp.stack([left[0], right[0], left[1], right[1]], 0)
    main = jnp.pad(cols[:, 1:257], ((0, 12), (0, 0)))
    edge_t = jnp.concatenate([top[0], top[1], cols[:, 0]])
    edge_b = jnp.concatenate([bottom[0], bottom[1], cols[:, 257]])
    e = jnp.stack([edge_t, edge_b], 1)
    eh = lax.reduce_precision(e, 8, 7)
    el = e - eh
    fe = jnp.pad(jnp.concatenate([eh, el, eh], 1), ((0, 12), (0, 10))).astype(bf16)
    n = 128 * 256
    out, cell = pl.pallas_call(
        interp_kernel,
        out_shape=(jax.ShapeDtypeStruct((8, n), f32), jax.ShapeDtypeStruct((1, n), i32)),
        in_specs=[pl.BlockSpec(memory_space=pltpu.VMEM)] * 4,
        out_specs=(pl.BlockSpec(memory_space=pltpu.VMEM),) * 2,
        scratch_shapes=[pltpu.VMEM((272, 256), bf16), pltpu.VMEM((272, 256), bf16), pltpu.VMEM((272, 16), bf16)],
        name="interp",
    )(recv, velocity, fe, main)
    return out, cell.reshape(-1)


from jax.sharding import Mesh
from jax.sharding import PartitionSpec as P

ALL = ("gx", "gy_0", "gy_1", "gz")
WIDE = ("gy_0", "gy_1", "gz")


def both_sides(first, last, axis):
    peers = lax.axis_size(axis)
    up = [(i, i + 1) for i in range(peers - 1)]
    down = [(j, i) for i, j in up]
    return lax.ppermute(last, axis, up), lax.ppermute(first, axis, down)


def shards(particles, dest_key, cell_a, cell_b, velocity):
    rows = velocity.shape[1]
    cols = velocity.shape[2]
    above, below = both_sides(velocity[:, 0, :], velocity[:, rows - 1, :], "gx")

    def column(k):
        return jnp.concatenate([above[:, k:k + 1], velocity[:, :, k], below[:, k:k + 1]], axis=1)

    left, right = both_sides(column(0), column(cols - 1), WIDE)
    outgoing = bucket(particles, dest_key, cell_a, cell_b)
    outgoing = outgoing.reshape(128, ROWS, 1, 128)
    arrived = lax.all_to_all(outgoing, ALL, 0, 0, tiled=True)
    return interp(arrived.reshape(128 * ROWS, 128), velocity, above, below, left, right)


def solution(mesh):
    split_mesh = Mesh(mesh.devices.reshape(mesh.shape["gx"], 4, 4, mesh.shape["gz"]), ALL)
    in_specs = (P(None, ALL), P(ALL), P(ALL), P(ALL), P(None, "gx", WIDE))
    out_specs = (P(None, ALL), P(ALL))
    return jax.shard_map(shards, mesh=split_mesh, in_specs=in_specs, out_specs=out_specs, check_vma=False)
```

time: 261 us -> 91.9 us (0.35)
  the two profiles are of different devices: /device:TPU:43 before, /device:TPU:24 now
where the time goes in v1:
time: 91.9 us; the launch traced here: 91.6 us
  Pallas kernels  55.3 us (60%)
  starting transfers between devices  26.2 us (29%)
  waiting for transfers between devices  5.89 us (6%)
  local copies, waits for them, and re-layouts  3.2 us (3%)
    pallas_call x1, Pallas kernels, interp(): pl.pallas_call(interp_kernel, out_shape=(jax.ShapeDtypeStruct((8, n), f32...  29.5 us
    pallas_call x1, Pallas kernels, bucket(): pl.pallas_call(bucket_kernel, out_shape=jax.ShapeDtypeStruct((128 * ROWS,...  25.8 us
    ppermute x4, starting transfers between devices, both_sides(): return (lax.ppermute(last, axis, up), lax.ppermute(first, axis, down))  15.9 us
    all_to_all x1, starting transfers between devices, shards(): arrived = lax.all_to_all(outgoing, ALL, 0, 0, tiled=True)  10.3 us
    ppermute x4, waiting for transfers between devices, both_sides(): return (lax.ppermute(last, axis, up), lax.ppermute(first, axis, down))  5.89 us
  transfers between devices with their start and end apart: 5, of which 3 were waited for; matrix products, arithmetic and copies ran while one was open for 3% of the time, Pallas kernels for 0%

profile of v1, /device:TPU:24, one launch (start us, length us, event | category | flops | bytes accessed | tf_op | source)
XLA Modules:
  0.0 91.6 jit_solution(4474426876847793805)
XLA Ops:
  0.6 25.8 %bucket.1 = f32[2304,128]{1,0:T(8,128)} custom-call(f32[8,8192]{1,0:T(8,128)} %p_ref.1, s32[1,8192]{1,0:T(1,128)} %bitcast.24, s32[1,8192]{1,0:T(1,128)} %bitcast.25, s32[1,8192]{1,0:T(1,128)} %bitcast.26), custom_call_target="tpu_custom_call" | custom-call | tf_op jit(solution)/shard_map/bucket/pallas_call | solution.py:110
  26.5 0.0 copy-start.1
  26.5 10.3 %all-to-all-start = ((f32[128,18,1,128]{3,2,1,0:T(1,128)}), f32[128,18,1,128]{3,2,1,0:T(1,128)S(1)}, u32[]{:S(2)}, u32[]{:S(2)}) async-start(f32[128,18,1,128]{3,2,1,0:T(1,128)} %bitcast.23), calls=%async_computation | async-start | bytes 2359296 | tf_op jit(solution)/shard_map/all_to_all | solution.py:230
  36.7 0.0 copy-done.1
  36.8 1.3 %collective-permute-start.1 = (f32[2,128]{1,0:T(2,128)S(1)}, f32[2,128]{1,0:T(2,128)S(1)}, u32[]{:S(2)}, u32[]{:S(2)}) collective-permute-start(f32[2,128]{1,0:T(2,128)S(1)} %bitcast.30), channel_id=1, source_target_pairs={{32,0},{64,32},{96,64},{33,1},{65,33},{97,65},{34,2},{66,34},{98,6... | collective-permute-start | bytes 3080 | tf_op jit(solution)/shard_map/ppermute | solution.py:216
  38.1 4.5 %collective-permute-start = (f32[2,128]{1,0:T(2,128)S(1)}, f32[2,128]{1,0:T(2,128)S(1)}, u32[]{:S(2)}, u32[]{:S(2)}) collective-permute-start(f32[2,128]{1,0:T(2,128)S(1)} %bitcast.29), channel_id=1, source_target_pairs={{0,32},{32,64},{64,96},{1,33},{33,65},{65,97},{2,34},{34,66},{66,9... | collective-permute-start | bytes 3080 | tf_op jit(solution)/shard_map/ppermute | solution.py:216
  42.6 0.1 fusion.1
  42.7 0.1 copy.26
  42.9 0.1 copy.24
  43.0 0.1 collective-permute-done.1
  43.1 0.1 fusion.6
  43.1 0.7 collective-permute-done
  43.9 0.1 fusion.5
  44.0 0.1 pad_maximum_fusion.3
  44.0 8.1 %collective-permute-start.3 = (f32[2,258]{1,0:T(2,128)S(1)}, f32[2,258]{1,0:T(2,128)S(1)}, u32[]{:S(2)}, u32[]{:S(2)}) collective-permute-start(f32[2,258]{1,0:T(2,128)S(1)} %pad_maximum_fusion.3), channel_id=1, source_target_pairs={{1,0},{2,1},{3,2},{4,3},{5,4},{6,5},{7,6},{8,7},{9,8},{10,9},{11,1... | collective-permute-start | bytes 6200 | tf_op jit(solution)/shard_map/ppermute | solution.py:216
  52.2 0.1 pad_maximum_fusion.2
  52.3 1.9 %collective-permute-start.2 = (f32[2,258]{1,0:T(2,128)S(1)}, f32[2,258]{1,0:T(2,128)S(1)}, u32[]{:S(2)}, u32[]{:S(2)}) collective-permute-start(f32[2,258]{1,0:T(2,128)S(1)} %pad_maximum_fusion.2), channel_id=1, source_target_pairs={{0,1},{1,2},{2,3},{3,4},{4,5},{5,6},{6,7},{7,8},{8,9},{9,10},{10,1... | collective-permute-start | bytes 6200 | tf_op jit(solution)/shard_map/ppermute | solution.py:216
  54.2 0.0 collective-permute-done.3
  54.2 5.0 %collective-permute-done.2 = f32[2,258]{1,0:T(2,128)S(1)} collective-permute-done((f32[2,258]{1,0:T(2,128)S(1)}, f32[2,258]{1,0:T(2,128)S(1)}, u32[]{:S(2)}, u32[]{:S(2)}) %collective-permute-start.2) | collective-permute-done | bytes 2096 | tf_op jit(solution)/shard_map/ppermute | solution.py:216
  59.3 0.1 slice.82
  59.4 0.2 slice_reduce_fusion.1
  59.6 0.1 copy.22
  59.8 0.6 pad.9.rows_ref
  60.4 0.6 pad.10.cols_ref
  61.0 0.0 all-to-all-done
  61.0 0.0 copy-start
  61.0 1.0 %copy-done = f32[128,18,1,128]{3,2,1,0:T(1,128)} copy-done((f32[128,18,1,128]{3,2,1,0:T(1,128)}, f32[128,18,1,128]{3,2,1,0:T(1,128)S(1)}, u32[]{:S(2)}) %copy-start) | copy-done | bytes 1179672
  62.1 29.5 %interp.1 = (f32[8,32768]{1,0:T(8,128)}, s32[1,32768]{1,0:T(1,128)}) custom-call(f32[2304,128]{1,0:T(8,128)} %bitcast.22, f32[2,256,128]{2,1,0:T(8,128)} %v_ref.1, bf16[272,16]{1,0:T(8,128)(2,1)} %pad.9.rows_ref, f32[16,256]{1,0:T(8,128)} %pad.10.cols_ref), custom_call_target="tpu_custom_call" | custom-call | tf_op jit(solution)/shard_map/interp/pallas_call | solution.py:194
  (11 shorter events, 0.1 us)
Async XLA Ops:
  26.5 10.3 %copy-start.1 = (f32[2,256,128]{2,1,0:T(8,128)S(1)}, f32[2,256,128]{2,1,0:T(8,128)}, u32[]{:S(2)}) copy-start(f32[2,256,128]{2,1,0:T(8,128)} %v_ref.1) | copy-start | bytes 786436
  26.5 34.6 %all-to-all-start = ((f32[128,18,1,128]{3,2,1,0:T(1,128)}), f32[128,18,1,128]{3,2,1,0:T(1,128)S(1)}, u32[]{:S(2)}, u32[]{:S(2)}) async-start(f32[128,18,1,128]{3,2,1,0:T(1,128)} %bitcast.23), calls=%async_computation | async-start | bytes 2359296 | tf_op jit(solution)/shard_map/all_to_all | solution.py:230
  36.8 6.3 %collective-permute-start.1 = (f32[2,128]{1,0:T(2,128)S(1)}, f32[2,128]{1,0:T(2,128)S(1)}, u32[]{:S(2)}, u32[]{:S(2)}) collective-permute-start(f32[2,128]{1,0:T(2,128)S(1)} %bitcast.30), channel_id=1, source_target_pairs={{32,0},{64,32},{96,64},{33,1},{65,33},{97,65},{34,2},{66,34},{98,6... | collective-permute-start | bytes 3080 | tf_op jit(solution)/shard_map/ppermute | solution.py:216
  38.1 5.8 %collective-permute-start = (f32[2,128]{1,0:T(2,128)S(1)}, f32[2,128]{1,0:T(2,128)S(1)}, u32[]{:S(2)}, u32[]{:S(2)}) collective-permute-start(f32[2,128]{1,0:T(2,128)S(1)} %bitcast.29), channel_id=1, source_target_pairs={{0,32},{32,64},{64,96},{1,33},{33,65},{65,97},{2,34},{34,66},{66,9... | collective-permute-start | bytes 3080 | tf_op jit(solution)/shard_map/ppermute | solution.py:216
  44.0 10.2 %collective-permute-start.3 = (f32[2,258]{1,0:T(2,128)S(1)}, f32[2,258]{1,0:T(2,128)S(1)}, u32[]{:S(2)}, u32[]{:S(2)}) collective-permute-start(f32[2,258]{1,0:T(2,128)S(1)} %pad_maximum_fusion.3), channel_id=1, source_target_pairs={{1,0},{2,1},{3,2},{4,3},{5,4},{6,5},{7,6},{8,7},{9,8},{10,9},{11,1... | collective-permute-start | bytes 6200 | tf_op jit(solution)/shard_map/ppermute | solution.py:216
  52.3 7.0 %collective-permute-start.2 = (f32[2,258]{1,0:T(2,128)S(1)}, f32[2,258]{1,0:T(2,128)S(1)}, u32[]{:S(2)}, u32[]{:S(2)}) collective-permute-start(f32[2,258]{1,0:T(2,128)S(1)} %pad_maximum_fusion.2), channel_id=1, source_target_pairs={{0,1},{1,2},{2,3},{3,4},{4,5},{5,6},{6,7},{7,8},{8,9},{9,10},{10,1... | collective-permute-start | bytes 6200 | tf_op jit(solution)/shard_map/ppermute | solution.py:216
  61.0 1.0 %copy-start = (f32[128,18,1,128]{3,2,1,0:T(1,128)}, f32[128,18,1,128]{3,2,1,0:T(1,128)S(1)}, u32[]{:S(2)}) copy-start(f32[128,18,1,128]{3,2,1,0:T(1,128)S(1)} %all-to-all-done) | copy-start | bytes 3538948

commit v2 on v1

v2 whole, which is shorter than its diff:
```python
import jax
import jax.numpy as jnp
from jax import lax
from jax.experimental import pallas as pl
from jax.experimental.pallas import tpu as pltpu

f32, bf16, i32 = jnp.float32, jnp.bfloat16, jnp.int32
OWNERS = 128
HEAD = 3
BODY = 6
HALO = 4
HEAD_ROWS = 2 * HEAD + HALO
BODY_ROWS = 2 * BODY
PB = 512
VMEM = pl.BlockSpec(memory_space=pltpu.VMEM)
SMEM = pl.BlockSpec(memory_space=pltpu.SMEM)


def iota(shape, dim, dt):
    return lax.broadcasted_iota(i32, shape, dim).astype(f32).astype(dt)


def nt(a, b):
    return lax.dot_general(a, b, (((1,), (1,)), ((), ())), preferred_element_type=f32)


def nn(a, b):
    return jnp.dot(a, b, preferred_element_type=f32)


def split(v):
    hi = v.astype(bf16)
    return hi, (v - hi.astype(f32)).astype(bf16)


def one_hot(size, t):
    hit = iota((size, t.shape[1]), 0, bf16) == t.astype(bf16)
    return jnp.where(hit, jnp.ones((), bf16), jnp.zeros((), bf16))


def block(i):
    return pl.ds(pl.multiple_of(i * PB, PB), PB)


def column_of(key, rank, first):
    off = rank - first
    fits = (off >= 0.0) & (off < 128.0)
    return jnp.where(fits, off + jnp.where(key >= 64, 128.0, 0.0), -1.0)


def fold(key):
    return one_hot(64, jnp.where(key >= 64, key - 64, key).astype(f32))


def add_placed(acc_ref, rows, pick, t):
    m = 64 * len(rows)
    parts = [split(r) for r in rows]
    left = jnp.concatenate([pick * p[0] for p in parts] + [pick * p[1] for p in parts], 0)
    both = nt(left, one_hot(256, t))
    acc_ref[...] += both[:m] + both[m:]


def flush(out_ref, acc_ref, width, first, stride):
    for k in range(width):
        for o in range(2):
            rows = pl.ds(o * 64 * stride + first + k, 64, stride=stride)
            out_ref[rows, :] = acc_ref[k * 64:(k + 1) * 64, o * 128:(o + 1) * 128]


def second_half(rows_of, width, key_ref, rank_ref, counts, out_ref, acc_ref, hot_ref, stride):
    n = key_ref.shape[1] // PB
    ids = lax.broadcasted_iota(i32, (128, 128), 0).astype(f32)
    n_full = jnp.max(jnp.sum(jnp.where(counts > 128.0, 1.0, 0.0), axis=0, keepdims=True))
    hot = jnp.max(jnp.where(counts > 128.0, ids, -1.0)).astype(i32)

    @pl.when(n_full <= 1.0)
    def _():
        hot_ref[...] = jnp.zeros(hot_ref.shape, f32)

        def hot_body(i, carry):
            sl = block(i)
            over = jnp.where(key_ref[0:1, sl] == hot, rank_ref[0:1, sl] - 128.0, -1.0)
            rows = rows_of(sl)
            rows = rows + [jnp.zeros((8 - width, PB), f32)]
            hi, lo = split(jnp.concatenate(rows, 0))
            both = nt(jnp.concatenate([hi, lo], 0), one_hot(128, over))
            hot_ref[...] += both[:8] + both[8:]
            return carry

        lax.fori_loop(0, n, hot_body, 0)
        at = jnp.maximum(hot, 0) * stride + width
        for k in range(width):
            out_ref[pl.ds(at + k, 1), :] = hot_ref[k:k + 1, :]

    @pl.when(n_full > 1.0)
    def _():
        acc_ref[...] = jnp.zeros(acc_ref.shape, f32)

        def over_body(i, carry):
            sl = block(i)
            key = key_ref[0:1, sl]
            add_placed(acc_ref, rows_of(sl), fold(key), column_of(key, rank_ref[0:1, sl], 128.0))
            return carry

        lax.fori_loop(0, n, over_body, 0)
        flush(out_ref, acc_ref, width, width, stride)


def head_kernel(at_ref, p_ref, key_ref, a_ref, b_ref, v_ref, out_ref, rank_ref, count_ref, acc_ref, ut_ref, hot_ref):
    n = p_ref.shape[1] // PB
    out_ref[...] = jnp.zeros(out_ref.shape, f32)
    acc_ref[...] = jnp.zeros(acc_ref.shape, f32)
    count_ref[...] = jnp.zeros(count_ref.shape, f32)
    before = lax.broadcasted_iota(i32, (128, 128), 0) < lax.broadcasted_iota(i32, (128, 128), 1)
    ut_ref[:, :128] = jnp.where(before, 1.0, 0.0).astype(bf16)
    ut_ref[:, 128:] = jnp.ones((128, 128), bf16)

    def rows_of(sl):
        cell = (a_ref[0:1, sl] * 128 + b_ref[0:1, sl] + 1).astype(f32)
        return [p_ref[0:1, sl], p_ref[1:2, sl], cell]

    def rank_block(i):
        sl = block(i)
        key = key_ref[0:1, sl]
        hots = []
        for k in range(PB // 128):
            hit = lax.broadcasted_iota(i32, (128, 128), 0) == key[:, k * 128:(k + 1) * 128]
            hots.append(jnp.where(hit, 1.0, 0.0))
        res = nn(jnp.concatenate([h.astype(bf16) for h in hots], 0), ut_ref[...])
        base = count_ref[...]
        ranks = []
        for k in range(PB // 128):
            r = res[k * 128:(k + 1) * 128]
            ranks.append(jnp.sum(hots[k] * (r[:, :128] + base), axis=0, keepdims=True))
            base = base + r[:, 128:]
        count_ref[...] = base
        return jnp.concatenate(ranks, 1)

    def place_block(i, rank):
        sl = block(i)
        key = key_ref[0:1, sl]
        add_placed(acc_ref, rows_of(sl), fold(key), column_of(key, rank, 0.0))

    rank0 = rank_block(0)
    rank_ref[0:1, block(0)] = rank0

    def body(i, rank):
        nxt = rank_block(i)
        place_block(i - 1, rank)
        rank_ref[0:1, block(i)] = nxt
        return nxt

    place_block(n - 1, lax.fori_loop(1, n, body, rank0))
    flush(out_ref, acc_ref, HEAD, 0, HEAD_ROWS)
    second_half(rows_of, HEAD, key_ref, rank_ref, count_ref[...], out_ref, acc_ref, hot_ref, HEAD_ROWS)

    x, y = at_ref[0], at_ref[1]
    top_x, top_y = at_ref[2] - 1, at_ref[3] - 1
    me = x * (top_y + 1) + y
    cols = v_ref.shape[2]
    turned = [v_ref[c].T for c in range(2)]
    lane = lax.broadcasted_iota(i32, (1, cols), 1)
    for dx in (-1, 0, 1):
        for dy in (-1, 0, 1):
            if dx == 0 and dy == 0:
                continue
            row = v_ref.shape[1] - 1 if dx > 0 else 0
            col = cols - 1 if dy > 0 else 0
            base = (me + dx * (top_y + 1) + dy) * HEAD_ROWS + 2 * HEAD

            @pl.when((x + dx >= 0) & (x + dx <= top_x) & (y + dy >= 0) & (y + dy <= top_y))
            def _():
                for c in range(2):
                    if dx:
                        line = v_ref[c, row:row + 1, :]
                        if dy:
                            one = jnp.sum(jnp.where(lane == col, line, 0.0), axis=1, keepdims=True)
                            line = jnp.broadcast_to(one, (1, cols))
                        out_ref[pl.ds(base + c, 1), :] = line
                    else:
                        for h in range(2):
                            out_ref[pl.ds(base + 2 * c + h, 1), :] = turned[c][col:col + 1, h * 128:(h + 1) * 128]


def body_kernel(p_ref, key_ref, rank_ref, count_ref, out_ref, acc_ref, hot_ref):
    n = p_ref.shape[1] // PB
    out_ref[...] = jnp.zeros(out_ref.shape, f32)
    acc_ref[...] = jnp.zeros(acc_ref.shape, f32)

    def rows_of(sl):
        return [p_ref[k:k + 1, sl] for k in range(2, 8)]

    def body(i, carry):
        sl = block(i)
        key = key_ref[0:1, sl]
        add_placed(acc_ref, rows_of(sl), fold(key), column_of(key, rank_ref[0:1, sl], 0.0))
        return carry

    lax.fori_loop(0, n, body, 0)
    flush(out_ref, acc_ref, BODY, 0, BODY_ROWS)
    second_half(rows_of, BODY, key_ref, rank_ref, count_ref[...], out_ref, acc_ref, hot_ref, BODY_ROWS)


def quad(t):
    return 0.5 * t * (t - 1.0), 1.0 - t * t, 0.5 * t * (t + 1.0)


def windows(start, size, pieces, dt):
    r = iota((size, start.shape[1]), 0, f32).astype(dt)
    hits = [r == (start + float(k)).astype(dt) for k in range(3)]
    over = [r == (start + float(k - size)).astype(dt) for k in range(3)]
    z = jnp.zeros((), dt)
    low = [jnp.where(hits[0], w[0], jnp.where(hits[1], w[1], jnp.where(hits[2], w[2], z))) for w in pieces]
    high = [jnp.where(over[1], w[1], jnp.where(over[2], w[2], z)) for w in pieces]
    return low, high


def interp_kernel(at_ref, r_ref, v_ref, out_ref, cell_ref, f_ref, t_ref):
    S = 4
    x, y = at_ref[0], at_ref[1]
    top_x, top_y = at_ref[2] - 1, at_ref[3] - 1
    me = x * (top_y + 1) + y

    def from_side(dx, dy, k):
        inside = (x + dx >= 0) & (x + dx <= top_x) & (y + dy >= 0) & (y + dy <= top_y)
        src = jnp.where(inside, me + dx * (top_y + 1) + dy, me)
        row = r_ref[pl.ds(src * HEAD_ROWS + 2 * HEAD + k, 1), :]
        return jnp.where(inside, row, 0.0)

    side_rows = []
    for c in range(2):
        turned = v_ref[c].T
        hi, lo = split(turned)
        f_ref[c * 128:(c + 1) * 128, :] = hi
        f_ref[272 + c * 128:272 + (c + 1) * 128, :] = lo
        for dy in (-1, 1):
            side_rows.append(jnp.concatenate([from_side(0, dy, 2 * c + h) for h in range(2)], 1))
    z6 = jnp.zeros((6, 256), f32)
    hi, lo = split(jnp.concatenate([side_rows[0], side_rows[1], z6, side_rows[2], side_rows[3], z6], 0))
    f_ref[256:272, :] = hi
    f_ref[528:544, :] = lo
    for e, dx in enumerate((-1, 1)):
        lanes = slice(128 * e, 128 * e + 128)
        corners = []
        for c in range(2):
            t_ref[c * 128:(c + 1) * 128, lanes] = jnp.broadcast_to(from_side(dx, 0, c), (128, 128)).T
            corners += [from_side(dx, -1, c), from_side(dx, 1, c), jnp.zeros((6, 128), f32)]
        t_ref[256:272, lanes] = jnp.concatenate(corners, 0)

    def step(i, carry):
        for u in range(S):
            s = i * S + u
            base = s * HEAD_ROWS
            lines = [jnp.concatenate([r_ref[pl.ds(base + k, 1), :], r_ref[pl.ds(base + HEAD + k, 1), :]], 1) for k in range(HEAD)]
            f, g = lines[0], lines[1]
            ci = lines[2].astype(i32) - 1
            live = ci >= 0
            a = jnp.where(live, ci >> 7, 0)
            b = ci & 127
            half = jnp.where(live, 0.5, 0.0)
            wa = [half * w for w in quad(f)]
            wb = quad(g)
            parts = [split(w) for w in wa]
            his, los = [p[0] for p in parts], [p[1] for p in parts]
            (h0, l0), (h1, l1) = windows(((a - 1) & 15).astype(f32), 16, [his, los], bf16)
            qa = jnp.broadcast_to(((a - 1) >> 4).astype(f32).astype(bf16), (16, 256))
            zero = jnp.zeros((16, 256), bf16)
            whi, wlo = [], []
            hit = qa == jnp.asarray(-1, bf16)
            for j in range(16):
                prev = hit
                hit = qa == jnp.asarray(j, bf16)
                whi.append(jnp.where(hit, h0, jnp.where(prev, h1, zero)))
                wlo.append(jnp.where(hit, l0, jnp.where(prev, l1, zero)))
            whi, wlo = jnp.concatenate(whi, 0), jnp.concatenate(wlo, 0)
            two = nn(f_ref[...], whi)
            R = two[:272] + two[272:] + nn(f_ref[:272, :], wlo)
            top = jnp.broadcast_to(a, (8, 256)) == 0
            edge = jnp.broadcast_to(jnp.where(a == 0, wa[0], jnp.where(a == 255, wa[2], 0.0)), (8, 256))
            (c0,), (c1,) = windows(((b - 1) & 7).astype(f32), 8, [wb], f32)
            qb = jnp.broadcast_to((b - 1) >> 3, (8, 256))

            def rows(at):
                t = [jnp.concatenate([t_ref[at:at + 8, 128 * k:128 * k + 128]] * 2, 1) for k in range(2)]
                return R[at:at + 8] + edge * jnp.where(top, t[0], t[1])

            zero8 = jnp.zeros((8, 256), f32)
            first = [zero8, zero8]
            second = [zero8, zero8]
            hit = qb == -1
            for j in range(16):
                prev = hit
                hit = qb == j
                for c in range(2):
                    v = rows(c * 128 + 8 * j)
                    first[c] = jnp.where(hit, v, first[c])
                    second[c] = jnp.where(prev, v, second[c])
            el = jnp.where(b == 0, wb[0], 0.0)
            er = jnp.where(b == 127, wb[2], 0.0)
            out = []
            for c in range(2):
                side = rows(256 + 8 * c)
                d = jnp.sum(first[c] * c0 + second[c] * c1, axis=0, keepdims=True)
                out.append(d + side[0:1] * el + side[1:2] * er)
            at = pl.multiple_of(s * 256, 256)
            out_ref[:, pl.ds(at, 256)] = jnp.concatenate([f, g] + out, 0)
            cell_ref[0:1, pl.ds(at, 256)] = ci
        return carry

    lax.fori_loop(0, OWNERS // S, step, 0)


def merge_kernel(d_ref, r_ref, out_ref):
    for s in range(d_ref.shape[1] // 256):
        lines = jnp.concatenate(
            [jnp.concatenate([r_ref[s * BODY_ROWS + h * BODY + k:s * BODY_ROWS + h * BODY + k + 1, :] for h in range(2)], 1) for k in range(BODY)], 0)
        d = d_ref[:, s * 256:(s + 1) * 256]
        out_ref[:, s * 256:(s + 1) * 256] = jnp.concatenate([d[0:2], lines[0:2] + d[2:4], lines[2:6]], 0)


def shape(*dims, dt=f32):
    return jax.ShapeDtypeStruct(dims, dt)


def head(place, particles, key, a, b, velocity):
    n = particles.shape[1]
    return pl.pallas_call(
        head_kernel,
        out_shape=(shape(OWNERS * HEAD_ROWS, 128), shape(1, n), shape(128, 128)),
        in_specs=[SMEM] + [VMEM] * 5,
        out_specs=(VMEM,) * 3,
        scratch_shapes=[pltpu.VMEM((64 * HEAD, 256), f32), pltpu.VMEM((128, 256), bf16), pltpu.VMEM((8, 128), f32)],
        name="head",
    )(place, particles, key, a, b, velocity)


def body(particles, key, rank, count):
    return pl.pallas_call(
        body_kernel,
        out_shape=shape(OWNERS * BODY_ROWS, 128),
        in_specs=[VMEM] * 4,
        out_specs=VMEM,
        scratch_shapes=[pltpu.VMEM((64 * BODY, 256), f32), pltpu.VMEM((8, 128), f32)],
        name="body",
    )(particles, key, rank, count)


def interp(place, arrived, velocity):
    n = OWNERS * 256
    return pl.pallas_call(
        interp_kernel,
        out_shape=(shape(4, n), shape(1, n, dt=i32)),
        in_specs=[SMEM, VMEM, VMEM],
        out_specs=(VMEM,) * 2,
        scratch_shapes=[pltpu.VMEM((544, 256), bf16), pltpu.VMEM((272, 256), f32)],
        name="interp",
    )(place, arrived, velocity)


def merge(moved, arrived):
    n = moved.shape[1]
    g = 8
    return pl.pallas_call(
        merge_kernel,
        out_shape=shape(8, n),
        grid=(g,),
        in_specs=[pl.BlockSpec((4, n // g), lambda i: (0, i)), pl.BlockSpec((OWNERS // g * BODY_ROWS, 128), lambda i: (i, 0))],
        out_specs=pl.BlockSpec((8, n // g), lambda i: (0, i)),
        name="merge",
    )(moved, arrived)


from jax.sharding import Mesh
from jax.sharding import PartitionSpec as P

ALL = ("gx", "gy_0", "gy_1", "gz")
WIDE = ("gy_0", "gy_1", "gz")


def exchange(buckets, rows):
    out = lax.all_to_all(buckets.reshape(OWNERS, rows, 1, 128), ALL, 0, 0, tiled=True)
    return out.reshape(OWNERS * rows, 128)


def shards(particles, dest_key, cell_a, cell_b, velocity):
    place = jnp.stack([lax.axis_index("gx"), lax.axis_index(WIDE), lax.axis_size("gx"), lax.axis_size(WIDE)]).astype(i32)
    key, a, b = [v.reshape(1, -1) for v in (dest_key, cell_a, cell_b)]
    first, rank, count = head(place, particles, key, a, b, velocity)
    arrived = exchange(first, HEAD_ROWS)
    rest = exchange(body(particles, key, rank, count), BODY_ROWS)
    moved, cell = interp(place, arrived, velocity)
    return merge(moved, rest), cell.reshape(-1)


def solution(mesh):
    split_mesh = Mesh(mesh.devices.reshape(mesh.shape["gx"], 4, 4, mesh.shape["gz"]), ALL)
    in_specs = (P(None, ALL), P(ALL), P(ALL), P(ALL), P(None, "gx", WIDE))
    out_specs = (P(None, ALL), P(ALL))
    return jax.shard_map(shards, mesh=split_mesh, in_specs=in_specs, out_specs=out_specs, check_vma=False)
```

time: 91.9 us -> 77.4 us (0.84)
  the two profiles are of different devices: /device:TPU:24 before, /device:TPU:1 now
where the time goes in v2:
time: 77.4 us; the launch traced here: 76.9 us
  Pallas kernels  52.7 us (68%)
  starting transfers between devices  17.5 us (23%)
  waiting for transfers between devices  3.75 us (5%)
  local copies, waits for them, and re-layouts  1.72 us (2%)
    pallas_call x1, Pallas kernels, interp(): pl.pallas_call(interp_kernel, out_shape=(shape(4, n), shape(1, n, dt=i32)...  25.3 us
    all_to_all x2, starting transfers between devices, exchange(): lax.all_to_all(buckets.reshape(OWNERS, rows, 1, 128), ALL, 0, 0, tiled=True)  17.5 us
    pallas_call x1, Pallas kernels, body(): pl.pallas_call(body_kernel, out_shape=shape(OWNERS * BODY_ROWS, 128), in_...  11.3 us
    pallas_call x1, Pallas kernels, head(): pl.pallas_call(head_kernel, out_shape=(shape(OWNERS * HEAD_ROWS, 128), sh...  10.6 us
    pallas_call x1, Pallas kernels, merge(): pl.pallas_call(merge_kernel, out_shape=shape(8, n), grid=(g,), in_specs=[...  5.52 us
    all_to_all x2, waiting for transfers between devices, exchange(): lax.all_to_all(buckets.reshape(OWNERS, rows, 1, 128), ALL, 0, 0, tiled=True)  3.75 us
    unnamed x4, local copies, waits for them, and re-layouts  1.72 us
  transfers between devices with their start and end apart: 2, of which 1 were waited for; matrix products, arithmetic and copies ran while one was open for 0% of the time, Pallas kernels for 48%

profile of v2, /device:TPU:1, one launch (start us, length us, event | category | flops | bytes accessed | tf_op | source)
XLA Modules:
  0.0 76.9 jit_solution(8653342511531919696)
XLA Ops:
  0.6 0.6 pad_add_fusion.at_ref
  1.3 10.6 %head.1 = (f32[1280,128]{1,0:T(8,128)}, f32[1,8192]{1,0:T(1,128)}, f32[128,128]{1,0:T(8,128)}) custom-call(s32[4]{0:T(128)} %pad_add_fusion.at_ref, f32[8,8192]{1,0:T(8,128)} %p_ref.3, s32[1,8192]{1,0:T(1,128)} %bitcast.14, s32[1,8192]{1,0:T(1,128)} %bitcast.16, s32[1,8192]{1,0:T(1,128)} %bitcast.17, f32[2,256,128]{2,1,0:T(8,128)} %v_ref.3), custom_call_target="tpu_custom_call" | custom-call | tf_op jit(solution)/shard_map/head/pallas_call | solution.py:327
  11.9 11.4 %all-to-all-start = ((f32[128,10,1,128]{3,2,1,0:T(1,128)}), f32[128,10,1,128]{3,2,1,0:T(1,128)S(1)}, u32[]{:S(2)}, u32[]{:S(2)}) async-start(f32[128,10,1,128]{3,2,1,0:T(1,128)} %bitcast.13), calls=%async_computation | async-start | bytes 1310720 | tf_op jit(solution)/shard_map/all_to_all | solution.py:381
  23.3 11.3 %body.1 = f32[1536,128]{1,0:T(8,128)} custom-call(f32[8,8192]{1,0:T(8,128)} %p_ref.3, s32[1,8192]{1,0:T(1,128)} %bitcast.15, f32[1,8192]{1,0:T(1,128)} %get-tuple-element.9.rank_ref, f32[128,128]{1,0:T(8,128)} %get-tuple-element.10.count_ref), custom_call_target="tpu_custom_call" | custom-call | tf_op jit(solution)/shard_map/body/pallas_call | solution.py:338
  34.6 3.7 %all-to-all-done = f32[128,10,1,128]{3,2,1,0:T(1,128)S(1)} async-done(((f32[128,10,1,128]{3,2,1,0:T(1,128)}), f32[128,10,1,128]{3,2,1,0:T(1,128)S(1)}, u32[]{:S(2)}, u32[]{:S(2)}) %all-to-all-start) | async-done | bytes 655392 | tf_op jit(solution)/shard_map/all_to_all | solution.py:381
  38.3 0.0 copy-start.1
  38.3 0.8 %copy-done.1 = f32[128,10,1,128]{3,2,1,0:T(1,128)} copy-done((f32[128,10,1,128]{3,2,1,0:T(1,128)}, f32[128,10,1,128]{3,2,1,0:T(1,128)S(1)}, u32[]{:S(2)}) %copy-start.1) | copy-done | bytes 655384
  39.2 6.0 %all-to-all-start.1 = ((f32[128,12,1,128]{3,2,1,0:T(1,128)}), f32[128,12,1,128]{3,2,1,0:T(1,128)S(1)}, u32[]{:S(2)}, u32[]{:S(2)}) async-start(f32[128,12,1,128]{3,2,1,0:T(1,128)} %bitcast.10), calls=%async_computation.1 | async-start | bytes 1572864 | tf_op jit(solution)/shard_map/all_to_all | solution.py:381
  45.2 25.3 %interp.1 = (f32[4,32768]{1,0:T(4,128)}, s32[1,32768]{1,0:T(1,128)}) custom-call(s32[4]{0:T(128)} %pad_add_fusion.at_ref, f32[1280,128]{1,0:T(8,128)} %bitcast.12, f32[2,256,128]{2,1,0:T(8,128)} %v_ref.3), custom_call_target="tpu_custom_call" | custom-call | tf_op jit(solution)/shard_map/interp/pallas_call | solution.py:350
  70.5 0.0 all-to-all-done.1
  70.5 0.0 copy-start
  70.5 0.9 %copy-done = f32[128,12,1,128]{3,2,1,0:T(1,128)} copy-done((f32[128,12,1,128]{3,2,1,0:T(1,128)}, f32[128,12,1,128]{3,2,1,0:T(1,128)S(1)}, u32[]{:S(2)}) %copy-start) | copy-done | bytes 786456
  71.3 5.5 %merge.1 = f32[8,32768]{1,0:T(8,128)} custom-call(f32[4,32768]{1,0:T(4,128)} %get-tuple-element.8.d_ref, f32[1536,128]{1,0:T(8,128)} %bitcast.11), custom_call_target="tpu_custom_call" | custom-call | tf_op jit(solution)/shard_map/merge/pallas_call | solution.py:363
Async XLA Ops:
  11.9 26.5 %all-to-all-start = ((f32[128,10,1,128]{3,2,1,0:T(1,128)}), f32[128,10,1,128]{3,2,1,0:T(1,128)S(1)}, u32[]{:S(2)}, u32[]{:S(2)}) async-start(f32[128,10,1,128]{3,2,1,0:T(1,128)} %bitcast.13), calls=%async_computation | async-start | bytes 1310720 | tf_op jit(solution)/shard_map/all_to_all | solution.py:381
  38.3 0.8 %copy-start.1 = (f32[128,10,1,128]{3,2,1,0:T(1,128)}, f32[128,10,1,128]{3,2,1,0:T(1,128)S(1)}, u32[]{:S(2)}) copy-start(f32[128,10,1,128]{3,2,1,0:T(1,128)S(1)} %all-to-all-done) | copy-start | bytes 1966084
  39.2 31.3 %all-to-all-start.1 = ((f32[128,12,1,128]{3,2,1,0:T(1,128)}), f32[128,12,1,128]{3,2,1,0:T(1,128)S(1)}, u32[]{:S(2)}, u32[]{:S(2)}) async-start(f32[128,12,1,128]{3,2,1,0:T(1,128)} %bitcast.10), calls=%async_computation.1 | async-start | bytes 1572864 | tf_op jit(solution)/shard_map/all_to_all | solution.py:381
  70.5 0.9 %copy-start = (f32[128,12,1,128]{3,2,1,0:T(1,128)}, f32[128,12,1,128]{3,2,1,0:T(1,128)S(1)}, u32[]{:S(2)}) copy-start(f32[128,12,1,128]{3,2,1,0:T(1,128)S(1)} %all-to-all-done.1) | copy-start | bytes 2359300

commit v3 on v2

v3 whole, which is shorter than its diff:
```python
import jax
import jax.numpy as jnp
from jax import lax
from jax.experimental import pallas as pl
from jax.experimental.pallas import tpu as pltpu
from jax.sharding import Mesh
from jax.sharding import PartitionSpec as P

f32, bf16, i32 = jnp.float32, jnp.bfloat16, jnp.int32
ALL = ("gx", "gy_0", "gy_1", "gz")
WIDE = ("gy_0", "gy_1", "gz")
OWNERS = 128
HEAD = 3
BODY = 6
HEAD_ROWS = 10
BODY_ROWS = 12
HALO = 6
PAD = 8
PB = 4096
RB = 4096
VMEM = pl.BlockSpec(memory_space=pltpu.VMEM)


def iota(shape, dim, dt):
    return lax.broadcasted_iota(i32, shape, dim).astype(f32).astype(dt)


def nt(a, b):
    return lax.dot_general(a, b, (((1,), (1,)), ((), ())), preferred_element_type=f32)


def nn(a, b):
    return jnp.dot(a, b, preferred_element_type=f32)


def split(v):
    hi = v.astype(bf16)
    return hi, (v - hi.astype(f32)).astype(bf16)


def one_hot(size, t):
    hit = iota((size, t.shape[1]), 0, bf16) == t.astype(bf16)
    return jnp.where(hit, jnp.ones((), bf16), jnp.zeros((), bf16))


def block(i, size):
    return pl.ds(pl.multiple_of(i * size, size), size)


def column_of(key, rank, first):
    off = rank - first
    fits = (off >= 0.0) & (off < 128.0)
    return jnp.where(fits, off + jnp.where(key >= 64, 128.0, 0.0), -1.0)


def head_row(k, half):
    return 2 * half + k if k < 2 else 4 + half


def body_row(k, half):
    return BODY * half + k


def place_all(rows_of, width, row_at, stride, key_ref, rank_ref, counts, out_ref, acc_ref, left_ref, col_ref, hot_ref):
    n = key_ref.shape[1] // PB
    m = 64 * width
    ids = lax.broadcasted_iota(i32, (128, 128), 0).astype(f32)
    n_full = jnp.max(jnp.sum(jnp.where(counts > 128.0, 1.0, 0.0), axis=0, keepdims=True))
    hot = jnp.max(jnp.where(counts > 128.0, ids, -1.0)).astype(i32)
    few = n_full <= 1.0
    hot_key = jnp.where(few, hot, -1)

    def add_placed(rows, key, t):
        pick = one_hot(64, jnp.where(key >= 64, key - 64, key).astype(f32))
        for k, r in enumerate(rows):
            hi, lo = split(r)
            left_ref[k * 64:(k + 1) * 64, :] = pick * hi
            left_ref[m + k * 64:m + (k + 1) * 64, :] = pick * lo
        col_ref[...] = one_hot(256, t)
        both = nt(left_ref[...], col_ref[...])
        acc_ref[...] += both[:m] + both[m:]

    def flush(half):
        for k in range(width):
            for o in range(2):
                at = pl.ds(o * 64 * stride + row_at(k, half), 64, stride=stride)
                out_ref[at, :] = acc_ref[k * 64:(k + 1) * 64, o * 128:(o + 1) * 128]

    acc_ref[...] = jnp.zeros(acc_ref.shape, f32)
    hot_ref[...] = jnp.zeros(hot_ref.shape, f32)

    def step(i, carry):
        sl = block(i, PB)
        key, rank = key_ref[0:1, sl], rank_ref[0:1, sl]
        rows = rows_of(sl)
        add_placed(rows, key, column_of(key, rank, 0.0))
        over = jnp.where(key == hot_key, rank - 128.0, -1.0)
        hi, lo = split(jnp.concatenate(rows + [jnp.zeros((8 - width, PB), f32)], 0))
        hot_ref[:, :16] += nt(one_hot(128, over), jnp.concatenate([hi, lo], 0))
        return carry

    lax.fori_loop(0, n, step, 0)
    flush(0)
    turned = hot_ref[...].T
    spill = turned[:8] + turned[8:16]
    base = jnp.maximum(hot, 0) * stride
    for k in range(width):
        out_ref[pl.ds(base + row_at(k, 1), 1), :] = spill[k:k + 1]

    @pl.when(jnp.logical_not(few))
    def _():
        acc_ref[...] = jnp.zeros(acc_ref.shape, f32)

        def again(i, carry):
            sl = block(i, PB)
            key = key_ref[0:1, sl]
            add_placed(rows_of(sl), key, column_of(key, rank_ref[0:1, sl], 128.0))
            return carry

        lax.fori_loop(0, n, again, 0)
        flush(1)


def around():
    x, y = lax.axis_index("gx"), lax.axis_index(WIDE)
    nx, ny = lax.axis_size("gx"), lax.axis_size(WIDE)

    def side(dx, dy):
        inside = (x + dx >= 0) & (x + dx < nx) & (y + dy >= 0) & (y + dy < ny)
        return inside, jnp.where(inside, (x + dx) * ny + y + dy, 0)

    return side


def head_kernel(p_ref, key_ref, a_ref, b_ref, v_ref, out_ref, rank_ref, count_ref, acc_ref, left_ref, col_ref, hot_ref, ut_ref, oh_ref):
    n = p_ref.shape[1] // RB
    out_ref[...] = jnp.zeros(out_ref.shape, f32)
    count_ref[...] = jnp.zeros(count_ref.shape, f32)
    before = lax.broadcasted_iota(i32, (128, 128), 0) < lax.broadcasted_iota(i32, (128, 128), 1)
    ut_ref[:, :128] = jnp.where(before, 1.0, 0.0).astype(bf16)
    ut_ref[:, 128:] = jnp.ones((128, 128), bf16)

    def rank_block(i, carry):
        sl = block(i, RB)
        key = key_ref[0:1, sl].astype(f32)
        for k in range(RB // 128):
            oh_ref[k * 128:(k + 1) * 128, :] = one_hot(128, key[:, k * 128:(k + 1) * 128])
        res = nn(oh_ref[...], ut_ref[...])
        base = count_ref[...]
        ranks = []
        for k in range(RB // 128):
            r = res[k * 128:(k + 1) * 128]
            hot = oh_ref[k * 128:(k + 1) * 128, :].astype(f32)
            ranks.append(jnp.sum(hot * (r[:, :128] + base), axis=0, keepdims=True))
            base = base + r[:, 128:]
        count_ref[...] = base
        rank_ref[0:1, sl] = jnp.concatenate(ranks, 1)
        return carry

    lax.fori_loop(0, n, rank_block, 0)

    def rows_of(sl):
        cell = (a_ref[0:1, sl] * 128 + b_ref[0:1, sl] + 1).astype(f32)
        return [p_ref[0:1, sl], p_ref[1:2, sl], cell]

    place_all(rows_of, HEAD, head_row, HEAD_ROWS, key_ref, rank_ref, count_ref[...], out_ref, acc_ref, left_ref, col_ref, hot_ref)

    side = around()
    height, width = v_ref.shape[1:]
    turned = [v_ref[c].T for c in range(2)]
    lane = lax.broadcasted_iota(i32, (1, width), 1)
    for dx in (-1, 0, 1):
        for dy in (-1, 0, 1):
            if dx == 0 and dy == 0:
                continue
            row = height - 1 if dx > 0 else 0
            col = width - 1 if dy > 0 else 0
            inside, who = side(dx, dy)
            base = who * HEAD_ROWS + HALO

            @pl.when(inside)
            def _():
                for c in range(2):
                    if dx:
                        line = v_ref[c, row:row + 1, :]
                        if dy:
                            one = jnp.sum(jnp.where(lane == col, line, 0.0), axis=1, keepdims=True)
                            line = jnp.broadcast_to(one, (1, width))
                        out_ref[pl.ds(base + c, 1), :] = line
                    else:
                        for h in range(2):
                            out_ref[pl.ds(base + 2 * c + h, 1), :] = turned[c][col:col + 1, h * 128:(h + 1) * 128]


def body_kernel(p_ref, key_ref, rank_ref, count_ref, out_ref, acc_ref, left_ref, col_ref, hot_ref):
    out_ref[...] = jnp.zeros(out_ref.shape, f32)

    def rows_of(sl):
        return [p_ref[k:k + 1, sl] for k in range(2, 8)]

    place_all(rows_of, BODY, body_row, BODY_ROWS, key_ref, rank_ref, count_ref[...], out_ref, acc_ref, left_ref, col_ref, hot_ref)


def quad(t):
    return 0.5 * t * (t - 1.0), 1.0 - t * t, 0.5 * t * (t + 1.0)


def pick_of(hits, values, zero):
    out = zero
    for h, v in reversed(list(zip(hits, values))):
        out = jnp.where(h, v, out)
    return out


def interp_kernel(r_ref, v_ref, out_ref, cell_ref, f_ref):
    S = 8
    side = around()

    def from_side(dx, dy, k):
        inside, who = side(dx, dy)
        row = r_ref[pl.ds(who * HEAD_ROWS + HALO + k, 1), :]
        return jnp.where(inside, row, 0.0)

    for c in range(2):
        hi, lo = split(v_ref[c].T)
        f_ref[c * 128:(c + 1) * 128, :] = hi
        f_ref[256 + c * 128:256 + (c + 1) * 128, :] = lo
    z4 = jnp.zeros((4, 128), f32)
    flat = jnp.concatenate([from_side(dx, 0, c) for c in range(2) for dx in (-1, 1)] + [z4], 0)
    west = jnp.concatenate([from_side(dx, -1, c) for c in range(2) for dx in (-1, 1)] + [z4], 0)
    east = jnp.concatenate([from_side(dx, 1, c) for c in range(2) for dx in (-1, 1)] + [z4], 0)
    tall = jnp.concatenate([from_side(0, dy, 2 * c + h) for h in range(2) for c in range(2) for dy in (-1, 1)], 0)
    sub = lax.broadcasted_iota(i32, (8, 128), 0)
    even = (sub & 1) == 0
    upper = sub < 4
    own = [(sub >> 1) == c for c in range(2)]
    own2 = [((sub >> 1) & 1) == c for c in range(2)]
    sub_f = sub.astype(f32)
    row_b = iota((16, 128), 0, bf16)
    zb = jnp.zeros((16, 128), bf16)
    z8 = jnp.zeros((8, 128), f32)

    def step(i, carry):
        groups = []
        for h in range(2):
            f, g, cell = [r_ref[pl.ds(i * (S * HEAD_ROWS) + head_row(k, h), S, stride=HEAD_ROWS), :] for k in range(3)]
            ci = cell.astype(i32) - 1
            cell_ref[pl.ds(i * (2 * S) + h, S, stride=2), :] = ci
            live = ci >= 0
            a = jnp.where(live, ci >> 7, 0)
            b = ci & 127
            half = jnp.where(live, 0.5, 0.0)
            wa = [half * w for w in quad(f)]
            wb = list(quad(g))
            hi = [w.astype(bf16).astype(f32) for w in wa]
            lo = [w - v for w, v in zip(wa, hi)]
            el, er = jnp.where(b == 0, wb[0], 0.0), jnp.where(b == 127, wb[2], 0.0)
            wb[0], wb[2] = wb[0] - el, wb[2] - er
            et, eb = jnp.where(a == 0, wa[0], 0.0), jnp.where(a == 255, wa[2], 0.0)
            at_a = [a - 1 + k for k in range(3)]
            w_half = [[jnp.where((t >> 7) == k, w, 0.0) for k in range(2)] for t, w in zip(at_a, wa)]
            groups.append(dict(
                w=hi + lo + [((a - 1) & 31).astype(f32), ((a - 1) >> 5).astype(f32)],
                wb=wb, start=((b - 1) & 7).astype(f32), q=((b - 1) >> 3) & 15, e=[el, er, et, eb],
                ia=[t & 127 for t in at_a], ib=[(b - 1 + k) & 127 for k in range(3)], w_half=w_half))

        def wide(x, j):
            return jnp.broadcast_to(x[j:j + 1], (8, 128))

        for u in range(S):
            spread = []
            for h in range(2):
                G = groups[h]
                packed = []
                for x in G["w"]:
                    y = wide(x, u)
                    packed.append(jnp.concatenate([y, y], 0).astype(bf16))
                his, los, start, q = packed[:3], packed[3:6], packed[6], packed[7]
                d = row_b - start
                near = [d == jnp.asarray(k, bf16) for k in range(3)]
                far = [d == jnp.asarray(k - 16, bf16) for k in range(3)]
                over = [d == jnp.asarray(k - 32, bf16) for k in (1, 2)]
                pieces = []
                for w in (his, los):
                    pieces.append((pick_of(near, w, zb), pick_of(far, w, zb), pick_of(over, w[1:], zb)))
                hit = q == jnp.asarray(-1, bf16)
                cols = [[], []]
                for j in range(8):
                    prev = hit
                    hit = q == jnp.asarray(j, bf16)
                    for k in range(2):
                        p0, p1, p2 = pieces[k]
                        cols[k].append(jnp.where(hit, p0, jnp.where(prev, p2, zb)))
                        cols[k].append(jnp.where(hit, p1, zb))
                spread.append([jnp.concatenate(c, 0) for c in cols])
            whi, wlo = [jnp.concatenate([spread[0][k], spread[1][k]], 1) for k in range(2)]
            two = nn(f_ref[...], whi)
            R = two[:256] + two[256:] + nn(f_ref[:256, :], wlo)
            for h in range(2):
                G = groups[h]
                V = R[:, 128 * h:128 * h + 128]
                d = sub_f - wide(G["start"], u)
                wb = [wide(w, u) for w in G["wb"]]
                c0 = pick_of([d == float(k) for k in range(3)], wb, z8)
                c1 = pick_of([d == float(k - 8) for k in (1, 2)], wb[1:], z8)
                q = wide(G["q"], u)
                bits = [(q & (1 << k)) != 0 for k in range(4)]

                def mux(v, b0, b1):
                    return jnp.where(b1, jnp.where(b0, v[3], v[2]), jnp.where(b0, v[1], v[0]))

                el, er, et, eb = [wide(e, u) for e in G["e"]]
                ga = [jnp.take_along_axis(tall, wide(t, u), axis=1) for t in G["ia"]]
                gb = [jnp.take_along_axis(flat, wide(t, u), axis=1) for t in G["ib"]]
                wh = [jnp.where(upper, wide(w[0], u), wide(w[1], u)) for w in G["w_half"]]
                beside = (wh[0] * ga[0] + wh[1] * ga[1] + wh[2] * ga[2]) * jnp.where(even, el, er)
                along = (wb[0] * gb[0] + wb[1] * gb[1] + wb[2] * gb[2] + el * west + er * east) * jnp.where(even, et, eb)
                for c in range(2):
                    r = [V[c * 128 + 8 * j:c * 128 + 8 * j + 8] for j in range(16)]
                    e = [mux([r[4 * m + t] for m in range(4)], bits[2], bits[3]) for t in range(4)]
                    e.append(mux([r[(4 * m + 4) % 16] for m in range(4)], bits[2], bits[3]))
                    first = mux(e[:4], bits[0], bits[1])
                    second = mux(e[1:], bits[0], bits[1])
                    total = first * c0 + second * c1 + jnp.where(own2[c], beside, 0.0) + jnp.where(own[c], along, 0.0)
                    row = PAD + 2 * (2 * u + h) + c
                    out_ref[pl.ds(i * (4 * S) + row, 1), :] = jnp.sum(total, axis=0, keepdims=True)
        return carry

    lax.fori_loop(0, OWNERS // S, step, 0)


def merge_kernel(d_ref, r1_ref, r2_ref, out_ref):
    S = out_ref.shape[1] // 256
    s0 = pl.program_id(0) * S
    sub = lax.broadcasted_iota(i32, (8, 128), 0)
    top, mid = sub < 2, sub < 4
    lead = pltpu.roll(r2_ref[0:8, :], 2, 0)
    for s in range(S):
        for h in range(2):
            src = s0 + s
            w = r1_ref[pl.ds(src * HEAD_ROWS + 2 * h, 8), :]
            at = src * BODY_ROWS + BODY * h - 2
            if s == 0 and h == 0:
                u = jnp.where(s0 == 0, lead, r2_ref[pl.ds(jnp.maximum(at, 0), 8), :])
            else:
                u = r2_ref[pl.ds(at, 8), :]
            d = d_ref[pl.ds(PAD + 2 * (2 * src + h) - 2, 8), :]
            out_ref[:, s * 256 + h * 128:s * 256 + h * 128 + 128] = jnp.where(top, w, jnp.where(mid, u + d, u))


def shape(*dims, dt=f32):
    return jax.ShapeDtypeStruct(dims, dt)


def scratch(width):
    return [pltpu.VMEM((64 * width, 256), f32), pltpu.VMEM((128 * width, PB), bf16), pltpu.VMEM((256, PB), bf16), pltpu.VMEM((128, 128), f32)]


def head(particles, key, a, b, velocity):
    n = particles.shape[1]
    return pl.pallas_call(
        head_kernel,
        out_shape=(shape(OWNERS * HEAD_ROWS, 128), shape(1, n), shape(128, 128)),
        in_specs=[VMEM] * 5,
        out_specs=(VMEM,) * 3,
        scratch_shapes=scratch(HEAD) + [pltpu.VMEM((128, 256), bf16), pltpu.VMEM((RB, 128), bf16)],
        name="head",
    )(particles, key, a, b, velocity)


def body(particles, key, rank, count):
    return pl.pallas_call(
        body_kernel,
        out_shape=shape(OWNERS * BODY_ROWS, 128),
        in_specs=[VMEM] * 4,
        out_specs=VMEM,
        scratch_shapes=scratch(BODY),
        name="body",
    )(particles, key, rank, count)


def interp(arrived, velocity):
    return pl.pallas_call(
        interp_kernel,
        out_shape=(shape(PAD + 4 * OWNERS + 8, 128), shape(2 * OWNERS, 128, dt=i32)),
        in_specs=[VMEM] * 2,
        out_specs=(VMEM,) * 2,
        scratch_shapes=[pltpu.VMEM((512, 256), bf16)],
        name="interp",
    )(arrived, velocity)


def merge(moved, head_arrived, body_arrived):
    n = OWNERS * 256
    g = 8
    return pl.pallas_call(
        merge_kernel,
        out_shape=shape(8, n),
        grid=(g,),
        in_specs=[VMEM] * 3,
        out_specs=pl.BlockSpec((8, n // g), lambda i: (0, i)),
        name="merge",
    )(moved, head_arrived, body_arrived)


def exchange(buckets, rows):
    out = lax.all_to_all(buckets.reshape(OWNERS, rows, 1, 128), ALL, 0, 0, tiled=True)
    return out.reshape(OWNERS * rows, 128)


def shards(particles, dest_key, cell_a, cell_b, velocity):
    key, a, b = [v.reshape(1, -1) for v in (dest_key, cell_a, cell_b)]
    first, rank, count = head(particles, key, a, b, velocity)
    arrived = exchange(first, HEAD_ROWS)
    rest = exchange(body(particles, key, rank, count), BODY_ROWS)
    moved, cell = interp(arrived, velocity)
    return merge(moved, arrived, rest), cell.reshape(-1)


def solution(mesh):
    split_mesh = Mesh(mesh.devices.reshape(mesh.shape["gx"], 4, 4, mesh.shape["gz"]), ALL)
    in_specs = (P(None, ALL), P(ALL), P(ALL), P(ALL), P(None, "gx", WIDE))
    out_specs = (P(None, ALL), P(ALL))
    return jax.shard_map(shards, mesh=split_mesh, in_specs=in_specs, out_specs=out_specs, check_vma=False)
```

time: 77.4 us -> 63.9 us (0.83)
  Pallas kernels: 52.7 us -> 36.5 us
  waiting for transfers between devices: 3.75 us -> 8.68 us
  starting transfers between devices: 17.5 us -> 16 us
    pallas_call x1, Pallas kernels: 25.3 us -> 19.1 us  [interp(): pl.pallas_call(interp_kernel, out_shape=(shape(PAD + 4 * OWNERS + 8, 128)...]
    pallas_call x1, Pallas kernels: 11.3 us -> 6.34 us  [body(): pl.pallas_call(body_kernel, out_shape=shape(OWNERS * BODY_ROWS, 128), in_...]
    all_to_all x2, waiting for transfers between devices: 3.75 us -> 8.68 us  [exchange(): lax.all_to_all(buckets.reshape(OWNERS, rows, 1, 128), ALL, 0, 0, tiled=True)]
    pallas_call x1, Pallas kernels: 10.6 us -> 6.88 us  [head(): pl.pallas_call(head_kernel, out_shape=(shape(OWNERS * HEAD_ROWS, 128), sh...]
    all_to_all x2, starting transfers between devices: 17.5 us -> 16 us  [exchange(): lax.all_to_all(buckets.reshape(OWNERS, rows, 1, 128), ALL, 0, 0, tiled=True)]
    pallas_call x1, Pallas kernels: 5.52 us -> 4.22 us  [merge(): pl.pallas_call(merge_kernel, out_shape=shape(8, n), grid=(g,), in_specs=[...]
  transfers between devices with their start and end apart: 2 -> 2, of which waited for: 1 -> 1; matrix products, arithmetic and copies ran while one was open for 0% -> 0% of each run, Pallas kernels for 48% -> 40%
where the time goes in v3:
time: 63.9 us; the launch traced here: 63.6 us
  Pallas kernels  36.5 us (57%)
  starting transfers between devices  16 us (25%)
  waiting for transfers between devices  8.68 us (14%)
  local copies, waits for them, and re-layouts  1.75 us (3%)
  between operations  0.65 us (1%)
    pallas_call x1, Pallas kernels, interp(): pl.pallas_call(interp_kernel, out_shape=(shape(PAD + 4 * OWNERS + 8, 128)...  19.1 us
    all_to_all x2, starting transfers between devices, exchange(): lax.all_to_all(buckets.reshape(OWNERS, rows, 1, 128), ALL, 0, 0, tiled=True)  16 us
    all_to_all x2, waiting for transfers between devices, exchange(): lax.all_to_all(buckets.reshape(OWNERS, rows, 1, 128), ALL, 0, 0, tiled=True)  8.68 us
    pallas_call x1, Pallas kernels, head(): pl.pallas_call(head_kernel, out_shape=(shape(OWNERS * HEAD_ROWS, 128), sh...  6.88 us
    pallas_call x1, Pallas kernels, body(): pl.pallas_call(body_kernel, out_shape=shape(OWNERS * BODY_ROWS, 128), in_...  6.34 us
    pallas_call x1, Pallas kernels, merge(): pl.pallas_call(merge_kernel, out_shape=shape(8, n), grid=(g,), in_specs=[...  4.22 us
    unnamed x4, local copies, waits for them, and re-layouts  1.75 us
  transfers between devices with their start and end apart: 2, of which 1 were waited for; matrix products, arithmetic and copies ran while one was open for 0% of the time, Pallas kernels for 40%

profile of v3, /device:TPU:1, one launch (start us, length us, event | category | flops | bytes accessed | tf_op | source)
XLA Modules:
  0.0 63.6 jit_solution(8548297497328255540)
XLA Ops:
  0.6 6.9 %head.1 = (f32[1280,128]{1,0:T(8,128)}, f32[1,8192]{1,0:T(1,128)}, f32[128,128]{1,0:T(8,128)}) custom-call(f32[8,8192]{1,0:T(8,128)} %p_ref.3, s32[1,8192]{1,0:T(1,128)} %bitcast.13, s32[1,8192]{1,0:T(1,128)} %bitcast.15, s32[1,8192]{1,0:T(1,128)} %bitcast.16, f32[2,256,128]{2,1,0:T(8,128)} %v_ref.3), custom_call_target="tpu_custom_call" | custom-call | tf_op jit(solution)/shard_map/head/pallas_call | solution.py:361
  7.5 11.4 %all-to-all-start = ((f32[128,10,1,128]{3,2,1,0:T(1,128)}), f32[128,10,1,128]{3,2,1,0:T(1,128)S(1)}, u32[]{:S(2)}, u32[]{:S(2)}) async-start(f32[128,10,1,128]{3,2,1,0:T(1,128)} %bitcast.12), calls=%async_computation | async-start | bytes 1310720 | tf_op jit(solution)/shard_map/all_to_all | solution.py:407
  19.0 6.3 %body.1 = f32[1536,128]{1,0:T(8,128)} custom-call(f32[8,8192]{1,0:T(8,128)} %p_ref.3, s32[1,8192]{1,0:T(1,128)} %bitcast.14, f32[1,8192]{1,0:T(1,128)} %get-tuple-element.9.rank_ref, f32[128,128]{1,0:T(8,128)} %get-tuple-element.10.count_ref), custom_call_target="tpu_custom_call" | custom-call | tf_op jit(solution)/shard_map/body/pallas_call | solution.py:372
  25.3 8.7 %all-to-all-done = f32[128,10,1,128]{3,2,1,0:T(1,128)S(1)} async-done(((f32[128,10,1,128]{3,2,1,0:T(1,128)}), f32[128,10,1,128]{3,2,1,0:T(1,128)S(1)}, u32[]{:S(2)}, u32[]{:S(2)}) %all-to-all-start) | async-done | bytes 655392 | tf_op jit(solution)/shard_map/all_to_all | solution.py:407
  34.0 0.0 copy-start
  34.0 0.9 %copy-done = f32[128,10,1,128]{3,2,1,0:T(1,128)} copy-done((f32[128,10,1,128]{3,2,1,0:T(1,128)}, f32[128,10,1,128]{3,2,1,0:T(1,128)S(1)}, u32[]{:S(2)}) %copy-start) | copy-done | bytes 655384
  34.8 4.6 %all-to-all-start.1 = ((f32[128,12,1,128]{3,2,1,0:T(1,128)}), f32[128,12,1,128]{3,2,1,0:T(1,128)S(1)}, u32[]{:S(2)}, u32[]{:S(2)}) async-start(f32[128,12,1,128]{3,2,1,0:T(1,128)} %bitcast.10), calls=%async_computation.1 | async-start | bytes 1572864 | tf_op jit(solution)/shard_map/all_to_all | solution.py:407
  39.4 19.1 %interp.1 = (f32[528,128]{1,0:T(8,128)}, s32[256,128]{1,0:T(8,128)}) custom-call(f32[1280,128]{1,0:T(8,128)} %bitcast.8, f32[2,256,128]{2,1,0:T(8,128)} %v_ref.3), custom_call_target="tpu_custom_call" | custom-call | tf_op jit(solution)/shard_map/interp/pallas_call | solution.py:383
  58.5 0.0 all-to-all-done.1
  58.5 0.0 copy-start.1
  58.5 0.9 %copy-done.1 = f32[128,12,1,128]{3,2,1,0:T(1,128)} copy-done((f32[128,12,1,128]{3,2,1,0:T(1,128)}, f32[128,12,1,128]{3,2,1,0:T(1,128)S(1)}, u32[]{:S(2)}) %copy-start.1) | copy-done | bytes 786456
  59.4 4.2 %merge.1 = f32[8,32768]{1,0:T(8,128)} custom-call(f32[528,128]{1,0:T(8,128)} %get-tuple-element.8.d_ref, f32[1280,128]{1,0:T(8,128)} %bitcast.9, f32[1536,128]{1,0:T(8,128)} %bitcast.11), custom_call_target="tpu_custom_call" | custom-call | tf_op jit(solution)/shard_map/merge/pallas_call | solution.py:396
Async XLA Ops:
  7.5 26.5 %all-to-all-start = ((f32[128,10,1,128]{3,2,1,0:T(1,128)}), f32[128,10,1,128]{3,2,1,0:T(1,128)S(1)}, u32[]{:S(2)}, u32[]{:S(2)}) async-start(f32[128,10,1,128]{3,2,1,0:T(1,128)} %bitcast.12), calls=%async_computation | async-start | bytes 1310720 | tf_op jit(solution)/shard_map/all_to_all | solution.py:407
  34.0 0.9 %copy-start = (f32[128,10,1,128]{3,2,1,0:T(1,128)}, f32[128,10,1,128]{3,2,1,0:T(1,128)S(1)}, u32[]{:S(2)}) copy-start(f32[128,10,1,128]{3,2,1,0:T(1,128)S(1)} %all-to-all-done) | copy-start | bytes 1966084
  34.8 23.7 %all-to-all-start.1 = ((f32[128,12,1,128]{3,2,1,0:T(1,128)}), f32[128,12,1,128]{3,2,1,0:T(1,128)S(1)}, u32[]{:S(2)}, u32[]{:S(2)}) async-start(f32[128,12,1,128]{3,2,1,0:T(1,128)} %bitcast.10), calls=%async_computation.1 | async-start | bytes 1572864 | tf_op jit(solution)/shard_map/all_to_all | solution.py:407
  58.5 0.9 %copy-start.1 = (f32[128,12,1,128]{3,2,1,0:T(1,128)}, f32[128,12,1,128]{3,2,1,0:T(1,128)S(1)}, u32[]{:S(2)}) copy-start(f32[128,12,1,128]{3,2,1,0:T(1,128)S(1)} %all-to-all-done.1) | copy-start | bytes 2359300

commit v4 on v3

--- a/solution.py
+++ b/solution.py
@@ -44,6 +44,8 @@
 
 
 def block(i, size):
+    if isinstance(i, int):
+        return slice(i * size, (i + 1) * size)
     return pl.ds(pl.multiple_of(i * size, size), size)
 
 
@@ -99,7 +101,8 @@
         hot_ref[:, :16] += nt(one_hot(128, over), jnp.concatenate([hi, lo], 0))
         return carry
 
-    lax.fori_loop(0, n, step, 0)
+    for i in range(n):
+        step(i, 0)
     flush(0)
     turned = hot_ref[...].T
     spill = turned[:8] + turned[8:16]
@@ -157,7 +160,8 @@
         rank_ref[0:1, sl] = jnp.concatenate(ranks, 1)
         return carry
 
-    lax.fori_loop(0, n, rank_block, 0)
+    for i in range(n):
+        rank_block(i, 0)
 
     def rows_of(sl):
         cell = (a_ref[0:1, sl] * 128 + b_ref[0:1, sl] + 1).astype(f32)
@@ -168,7 +172,6 @@
     side = around()
     height, width = v_ref.shape[1:]
     turned = [v_ref[c].T for c in range(2)]
-    lane = lax.broadcasted_iota(i32, (1, width), 1)
     for dx in (-1, 0, 1):
         for dy in (-1, 0, 1):
             if dx == 0 and dy == 0:
@@ -182,11 +185,7 @@
             def _():
                 for c in range(2):
                     if dx:
-                        line = v_ref[c, row:row + 1, :]
-                        if dy:
-                            one = jnp.sum(jnp.where(lane == col, line, 0.0), axis=1, keepdims=True)
-                            line = jnp.broadcast_to(one, (1, width))
-                        out_ref[pl.ds(base + c, 1), :] = line
+                        out_ref[pl.ds(base + c, 1), :] = v_ref[c, row:row + 1, :]
                     else:
                         for h in range(2):
                             out_ref[pl.ds(base + 2 * c + h, 1), :] = turned[c][col:col + 1, h * 128:(h + 1) * 128]
@@ -229,6 +228,8 @@
     flat = jnp.concatenate([from_side(dx, 0, c) for c in range(2) for dx in (-1, 1)] + [z4], 0)
     west = jnp.concatenate([from_side(dx, -1, c) for c in range(2) for dx in (-1, 1)] + [z4], 0)
     east = jnp.concatenate([from_side(dx, 1, c) for c in range(2) for dx in (-1, 1)] + [z4], 0)
+    west = jnp.broadcast_to(west[:, 127:128], (8, 128))
+    east = jnp.broadcast_to(east[:, 0:1], (8, 128))
     tall = jnp.concatenate([from_side(0, dy, 2 * c + h) for h in range(2) for c in range(2) for dy in (-1, 1)], 0)
     sub = lax.broadcasted_iota(i32, (8, 128), 0)
     even = (sub & 1) == 0
@@ -352,6 +353,14 @@
     return jax.ShapeDtypeStruct(dims, dt)
 
 
+def held(*dims, dt=f32):
+    return pltpu.VMEM(dims, dt)
+
+
+def near_memory(x):
+    return pltpu.with_memory_space_constraint(x, pltpu.VMEM)
+
+
 def scratch(width):
     return [pltpu.VMEM((64 * width, 256), f32), pltpu.VMEM((128 * width, PB), bf16), pltpu.VMEM((256, PB), bf16), pltpu.VMEM((128, 128), f32)]
 
@@ -360,7 +369,7 @@
     n = particles.shape[1]
     return pl.pallas_call(
         head_kernel,
-        out_shape=(shape(OWNERS * HEAD_ROWS, 128), shape(1, n), shape(128, 128)),
+        out_shape=(held(OWNERS * HEAD_ROWS, 128), held(1, n), held(128, 128)),
         in_specs=[VMEM] * 5,
         out_specs=(VMEM,) * 3,
         scratch_shapes=scratch(HEAD) + [pltpu.VMEM((128, 256), bf16), pltpu.VMEM((RB, 128), bf16)],
@@ -371,18 +380,18 @@
 def body(particles, key, rank, count):
     return pl.pallas_call(
         body_kernel,
-        out_shape=shape(OWNERS * BODY_ROWS, 128),
+        out_shape=held(OWNERS * BODY_ROWS, 128),
         in_specs=[VMEM] * 4,
         out_specs=VMEM,
         scratch_shapes=scratch(BODY),
         name="body",
-    )(particles, key, rank, count)
+    )(particles, key, near_memory(rank), near_memory(count))
 
 
 def interp(arrived, velocity):
     return pl.pallas_call(
         interp_kernel,
-        out_shape=(shape(PAD + 4 * OWNERS + 8, 128), shape(2 * OWNERS, 128, dt=i32)),
+        out_shape=(held(PAD + 4 * OWNERS + 8, 128), shape(2 * OWNERS, 128, dt=i32)),
         in_specs=[VMEM] * 2,
         out_specs=(VMEM,) * 2,
         scratch_shapes=[pltpu.VMEM((512, 256), bf16)],
@@ -400,12 +409,12 @@
         in_specs=[VMEM] * 3,
         out_specs=pl.BlockSpec((8, n // g), lambda i: (0, i)),
         name="merge",
-    )(moved, head_arrived, body_arrived)
+    )(near_memory(moved), head_arrived, body_arrived)
 
 
 def exchange(buckets, rows):
     out = lax.all_to_all(buckets.reshape(OWNERS, rows, 1, 128), ALL, 0, 0, tiled=True)
-    return out.reshape(OWNERS * rows, 128)
+    return near_memory(out.reshape(OWNERS * rows, 128))
 
 
 def shards(particles, dest_key, cell_a, cell_b, velocity):

time: 63.9 us -> 59.5 us (0.931)
  Pallas kernels: 36.5 us -> 33.6 us
  local copies, waits for them, and re-layouts: 1.75 us -> 0 us
    unnamed x4 -> x0, local copies, waits for them, and re-layouts: 1.75 us -> none
    pallas_call x3, Pallas kernels: 32.3 us -> 30.8 us  [the longest x1 18.2 us: interp(): pl.pallas_call(interp_kernel, out_shape=(held(PAD + 4 * OWNERS + 8, 128),...]
    pallas_call x1, Pallas kernels: 4.22 us -> 2.81 us  [merge(): pl.pallas_call(merge_kernel, out_shape=shape(8, n), grid=(g,), in_specs=[...]
  transfers between devices with their start and end apart: 2 -> 2, of which waited for: 1 -> 1; matrix products, arithmetic and copies ran while one was open for 0% -> 0% of each run, Pallas kernels for 40% -> 41%
where the time goes in v4:
time: 59.5 us; the launch traced here: 59.2 us
  Pallas kernels  33.6 us (56%)
  starting transfers between devices  16 us (27%)
  waiting for transfers between devices  8.89 us (15%)
  between operations  0.66 us (1%)
    pallas_call x1, Pallas kernels, interp(): pl.pallas_call(interp_kernel, out_shape=(held(PAD + 4 * OWNERS + 8, 128),...  18.2 us
    all_to_all x2, starting transfers between devices, exchange(): lax.all_to_all(buckets.reshape(OWNERS, rows, 1, 128), ALL, 0, 0, tiled=True)  16 us
    all_to_all x2, waiting for transfers between devices, exchange(): lax.all_to_all(buckets.reshape(OWNERS, rows, 1, 128), ALL, 0, 0, tiled=True)  8.89 us
    pallas_call x1, Pallas kernels, head(): pl.pallas_call(head_kernel, out_shape=(held(OWNERS * HEAD_ROWS, 128), hel...  6.5 us
    pallas_call x1, Pallas kernels, body(): pl.pallas_call(body_kernel, out_shape=held(OWNERS * BODY_ROWS, 128), in_s...  6.12 us
    pallas_call x1, Pallas kernels, merge(): pl.pallas_call(merge_kernel, out_shape=shape(8, n), grid=(g,), in_specs=[...  2.81 us
  transfers between devices with their start and end apart: 2, of which 1 were waited for; matrix products, arithmetic and copies ran while one was open for 0% of the time, Pallas kernels for 41%

profile of v4, /device:TPU:1, one launch (start us, length us, event | category | flops | bytes accessed | tf_op | source)
XLA Modules:
  0.0 59.2 jit_solution(5614740192167170515)
XLA Ops:
  0.6 6.5 %head.1 = (f32[1280,128]{1,0:T(8,128)}, f32[1,8192]{1,0:T(1,128)S(1)}, f32[128,128]{1,0:T(8,128)S(1)}) custom-call(f32[8,8192]{1,0:T(8,128)} %p_ref.3, s32[1,8192]{1,0:T(1,128)} %bitcast.11, s32[1,8192]{1,0:T(1,128)} %bitcast.13, s32[1,8192]{1,0:T(1,128)} %bitcast.14, f32[2,256,128]{2,1,0:T(8,128)} %v_ref.3), custom_call_target="tpu_custom_call" | custom-call | tf_op jit(solution)/shard_map/head/pallas_call | solution.py:370
  7.1 11.5 %all-to-all-start = ((f32[128,10,1,128]{3,2,1,0:T(1,128)}), f32[128,10,1,128]{3,2,1,0:T(1,128)S(1)}, u32[]{:S(2)}, u32[]{:S(2)}) async-start(f32[128,10,1,128]{3,2,1,0:T(1,128)} %bitcast.3), calls=%async_computation | async-start | bytes 1310720 | tf_op jit(solution)/shard_map/all_to_all | solution.py:416
  18.6 6.1 %body.1 = f32[1536,128]{1,0:T(8,128)} custom-call(f32[8,8192]{1,0:T(8,128)} %p_ref.3, s32[1,8192]{1,0:T(1,128)} %bitcast.12, f32[1,8192]{1,0:T(1,128)S(1)} %get-tuple-element.9.rank_ref, f32[128,128]{1,0:T(8,128)S(1)} %get-tuple-element.10.count_ref), custom_call_target="tpu_custom_call" | custom-call | tf_op jit(solution)/shard_map/body/pallas_call | solution.py:381
  24.7 8.9 %all-to-all-done = f32[128,10,1,128]{3,2,1,0:T(1,128)S(1)} async-done(((f32[128,10,1,128]{3,2,1,0:T(1,128)}), f32[128,10,1,128]{3,2,1,0:T(1,128)S(1)}, u32[]{:S(2)}, u32[]{:S(2)}) %all-to-all-start) | async-done | bytes 655392 | tf_op jit(solution)/shard_map/all_to_all | solution.py:416
  33.6 4.6 %all-to-all-start.1 = ((f32[128,12,1,128]{3,2,1,0:T(1,128)}), f32[128,12,1,128]{3,2,1,0:T(1,128)S(1)}, u32[]{:S(2)}, u32[]{:S(2)}) async-start(f32[128,12,1,128]{3,2,1,0:T(1,128)} %bitcast.5), calls=%async_computation.1 | async-start | bytes 1572864 | tf_op jit(solution)/shard_map/all_to_all | solution.py:416
  38.2 18.2 %interp.1 = (f32[528,128]{1,0:T(8,128)S(1)}, s32[256,128]{1,0:T(8,128)}) custom-call(f32[1280,128]{1,0:T(8,128)S(1)} %bitcast.8, f32[2,256,128]{2,1,0:T(8,128)} %v_ref.3), custom_call_target="tpu_custom_call" | custom-call | tf_op jit(solution)/shard_map/interp/pallas_call | solution.py:392
  56.4 0.0 all-to-all-done.1
  56.4 2.8 %merge.1 = f32[8,32768]{1,0:T(8,128)} custom-call(f32[528,128]{1,0:T(8,128)S(1)} %get-tuple-element.8.d_ref, f32[1280,128]{1,0:T(8,128)S(1)} %bitcast.9, f32[1536,128]{1,0:T(8,128)S(1)} %bitcast.10), custom_call_target="tpu_custom_call" | custom-call | tf_op jit(solution)/shard_map/merge/pallas_call | solution.py:405
Async XLA Ops:
  7.1 26.5 %all-to-all-start = ((f32[128,10,1,128]{3,2,1,0:T(1,128)}), f32[128,10,1,128]{3,2,1,0:T(1,128)S(1)}, u32[]{:S(2)}, u32[]{:S(2)}) async-start(f32[128,10,1,128]{3,2,1,0:T(1,128)} %bitcast.3), calls=%async_computation | async-start | bytes 1310720 | tf_op jit(solution)/shard_map/all_to_all | solution.py:416
  33.6 22.8 %all-to-all-start.1 = ((f32[128,12,1,128]{3,2,1,0:T(1,128)}), f32[128,12,1,128]{3,2,1,0:T(1,128)S(1)}, u32[]{:S(2)}, u32[]{:S(2)}) async-start(f32[128,12,1,128]{3,2,1,0:T(1,128)} %bitcast.5), calls=%async_computation.1 | async-start | bytes 1572864 | tf_op jit(solution)/shard_map/all_to_all | solution.py:416

commit v5 on v4

--- a/solution.py
+++ b/solution.py
@@ -67,20 +67,17 @@
     n = key_ref.shape[1] // PB
     m = 64 * width
     ids = lax.broadcasted_iota(i32, (128, 128), 0).astype(f32)
-    n_full = jnp.max(jnp.sum(jnp.where(counts > 128.0, 1.0, 0.0), axis=0, keepdims=True))
-    hot = jnp.max(jnp.where(counts > 128.0, ids, -1.0)).astype(i32)
-    few = n_full <= 1.0
-    hot_key = jnp.where(few, hot, -1)
-
-    def add_placed(rows, key, t):
-        pick = one_hot(64, jnp.where(key >= 64, key - 64, key).astype(f32))
+    n_full = jnp.sum(jnp.where(counts > 128.0, 1.0, 0.0), axis=0, keepdims=True)
+    hot = jnp.max(jnp.where(counts > 128.0, ids, -1.0), axis=0, keepdims=True)
+    lone = jnp.concatenate([jnp.where(n_full <= 1.0, hot, -1.0)] * (PB // 128), 1)
+
+    def fill(rows, low, t):
+        pick = one_hot(64, low)
         for k, r in enumerate(rows):
             hi, lo = split(r)
             left_ref[k * 64:(k + 1) * 64, :] = pick * hi
             left_ref[m + k * 64:m + (k + 1) * 64, :] = pick * lo
         col_ref[...] = one_hot(256, t)
-        both = nt(left_ref[...], col_ref[...])
-        acc_ref[...] += both[:m] + both[m:]
 
     def flush(half):
         for k in range(width):
@@ -90,34 +87,34 @@
 
     acc_ref[...] = jnp.zeros(acc_ref.shape, f32)
     hot_ref[...] = jnp.zeros(hot_ref.shape, f32)
-
-    def step(i, carry):
+    for i in range(n):
         sl = block(i, PB)
         key, rank = key_ref[0:1, sl], rank_ref[0:1, sl]
         rows = rows_of(sl)
-        add_placed(rows, key, column_of(key, rank, 0.0))
-        over = jnp.where(key == hot_key, rank - 128.0, -1.0)
-        hi, lo = split(jnp.concatenate(rows + [jnp.zeros((8 - width, PB), f32)], 0))
-        hot_ref[:, :16] += nt(one_hot(128, over), jnp.concatenate([hi, lo], 0))
-        return carry
-
-    for i in range(n):
-        step(i, 0)
+        over = (key.astype(f32) == lone) & (rank >= 128.0)
+        low = jnp.where(over, -1.0, (key & 63).astype(f32))
+        fill(rows, low, jnp.where(over, rank - 128.0, column_of(key, rank, 0.0)))
+        tail = jnp.concatenate([jnp.where(over, r, 0.0) for r in rows] + [jnp.zeros((8 - width, PB), f32)], 0)
+        hi = tail.astype(bf16).astype(f32)
+        left_ref[2 * m:, :] = jnp.concatenate([hi, tail - hi], 0).astype(bf16)
+        both = nt(left_ref[...], col_ref[...])
+        acc_ref[...] += both[:m] + both[m:2 * m]
+        hot_ref[...] += (both[2 * m:2 * m + 8] + both[2 * m + 8:])[:, :128]
     flush(0)
-    turned = hot_ref[...].T
-    spill = turned[:8] + turned[8:16]
-    base = jnp.maximum(hot, 0) * stride
+    base = jnp.max(jnp.maximum(hot, 0.0)).astype(i32) * stride
     for k in range(width):
-        out_ref[pl.ds(base + row_at(k, 1), 1), :] = spill[k:k + 1]
-
-    @pl.when(jnp.logical_not(few))
+        out_ref[pl.ds(base + row_at(k, 1), 1), :] = hot_ref[k:k + 1, :]
+
+    @pl.when(jnp.max(n_full) > 1.0)
     def _():
         acc_ref[...] = jnp.zeros(acc_ref.shape, f32)
 
         def again(i, carry):
             sl = block(i, PB)
             key = key_ref[0:1, sl]
-            add_placed(rows_of(sl), key, column_of(key, rank_ref[0:1, sl], 128.0))
+            fill(rows_of(sl), (key & 63).astype(f32), column_of(key, rank_ref[0:1, sl], 128.0))
+            both = nt(left_ref[:2 * m, :], col_ref[...])
+            acc_ref[...] += both[:m] + both[m:]
             return carry
 
         lax.fori_loop(0, n, again, 0)
@@ -138,30 +135,21 @@
 def head_kernel(p_ref, key_ref, a_ref, b_ref, v_ref, out_ref, rank_ref, count_ref, acc_ref, left_ref, col_ref, hot_ref, ut_ref, oh_ref):
     n = p_ref.shape[1] // RB
     out_ref[...] = jnp.zeros(out_ref.shape, f32)
-    count_ref[...] = jnp.zeros(count_ref.shape, f32)
-    before = lax.broadcasted_iota(i32, (128, 128), 0) < lax.broadcasted_iota(i32, (128, 128), 1)
-    ut_ref[:, :128] = jnp.where(before, 1.0, 0.0).astype(bf16)
-    ut_ref[:, 128:] = jnp.ones((128, 128), bf16)
-
-    def rank_block(i, carry):
-        sl = block(i, RB)
-        key = key_ref[0:1, sl].astype(f32)
-        for k in range(RB // 128):
-            oh_ref[k * 128:(k + 1) * 128, :] = one_hot(128, key[:, k * 128:(k + 1) * 128])
+    before = lax.broadcasted_iota(i32, (256, 256), 0) < lax.broadcasted_iota(i32, (256, 256), 1)
+    ut_ref[...] = jnp.where(before, 1.0, 0.0).astype(bf16)
+    base = jnp.zeros((128, 1), f32)
+    for i in range(n):
+        key = key_ref[0:1, block(i, RB)].astype(f32)
+        for k in range(RB // 256):
+            oh_ref[k * 128:(k + 1) * 128, :] = one_hot(128, key[:, k * 256:(k + 1) * 256])
         res = nn(oh_ref[...], ut_ref[...])
-        base = count_ref[...]
         ranks = []
-        for k in range(RB // 128):
-            r = res[k * 128:(k + 1) * 128]
+        for k in range(RB // 256):
             hot = oh_ref[k * 128:(k + 1) * 128, :].astype(f32)
-            ranks.append(jnp.sum(hot * (r[:, :128] + base), axis=0, keepdims=True))
-            base = base + r[:, 128:]
-        count_ref[...] = base
-        rank_ref[0:1, sl] = jnp.concatenate(ranks, 1)
-        return carry
-
-    for i in range(n):
-        rank_block(i, 0)
+            ranks.append(jnp.sum(hot * (res[k * 128:(k + 1) * 128] + base), axis=0, keepdims=True))
+            base = base + jnp.sum(hot, axis=1, keepdims=True)
+        rank_ref[0:1, block(i, RB)] = jnp.concatenate(ranks, 1)
+    count_ref[...] = jnp.broadcast_to(base, (128, 128))
 
     def rows_of(sl):
         cell = (a_ref[0:1, sl] * 128 + b_ref[0:1, sl] + 1).astype(f32)
@@ -191,8 +179,12 @@
                             out_ref[pl.ds(base + 2 * c + h, 1), :] = turned[c][col:col + 1, h * 128:(h + 1) * 128]
 
 
-def body_kernel(p_ref, key_ref, rank_ref, count_ref, out_ref, acc_ref, left_ref, col_ref, hot_ref):
+def body_kernel(p_ref, key_ref, rank_ref, count_ref, v_ref, out_ref, f_ref, acc_ref, left_ref, col_ref, hot_ref):
     out_ref[...] = jnp.zeros(out_ref.shape, f32)
+    for c in range(2):
+        hi, lo = split(v_ref[c].T)
+        f_ref[c * 128:(c + 1) * 128, :] = hi
+        f_ref[256 + c * 128:256 + (c + 1) * 128, :] = lo
 
     def rows_of(sl):
         return [p_ref[k:k + 1, sl] for k in range(2, 8)]
@@ -211,8 +203,8 @@
     return out
 
 
-def interp_kernel(r_ref, v_ref, out_ref, cell_ref, f_ref):
-    S = 8
+def interp_kernel(r_ref, f_ref, out_ref, cell_ref):
+    S = 16
     side = around()
 
     def from_side(dx, dy, k):
@@ -220,10 +212,6 @@
         row = r_ref[pl.ds(who * HEAD_ROWS + HALO + k, 1), :]
         return jnp.where(inside, row, 0.0)
 
-    for c in range(2):
-        hi, lo = split(v_ref[c].T)
-        f_ref[c * 128:(c + 1) * 128, :] = hi
-        f_ref[256 + c * 128:256 + (c + 1) * 128, :] = lo
     z4 = jnp.zeros((4, 128), f32)
     flat = jnp.concatenate([from_side(dx, 0, c) for c in range(2) for dx in (-1, 1)] + [z4], 0)
     west = jnp.concatenate([from_side(dx, -1, c) for c in range(2) for dx in (-1, 1)] + [z4], 0)
@@ -362,7 +350,7 @@
 
 
 def scratch(width):
-    return [pltpu.VMEM((64 * width, 256), f32), pltpu.VMEM((128 * width, PB), bf16), pltpu.VMEM((256, PB), bf16), pltpu.VMEM((128, 128), f32)]
+    return [pltpu.VMEM((64 * width, 256), f32), pltpu.VMEM((128 * width + 16, PB), bf16), pltpu.VMEM((256, PB), bf16), pltpu.VMEM((8, 128), f32)]
 
 
 def head(particles, key, a, b, velocity):
@@ -372,36 +360,35 @@
         out_shape=(held(OWNERS * HEAD_ROWS, 128), held(1, n), held(128, 128)),
         in_specs=[VMEM] * 5,
         out_specs=(VMEM,) * 3,
-        scratch_shapes=scratch(HEAD) + [pltpu.VMEM((128, 256), bf16), pltpu.VMEM((RB, 128), bf16)],
+        scratch_shapes=scratch(HEAD) + [pltpu.VMEM((256, 256), bf16), pltpu.VMEM((RB // 2, 256), bf16)],
         name="head",
     )(particles, key, a, b, velocity)
 
 
-def body(particles, key, rank, count):
+def body(particles, key, rank, count, velocity):
     return pl.pallas_call(
         body_kernel,
-        out_shape=held(OWNERS * BODY_ROWS, 128),
-        in_specs=[VMEM] * 4,
-        out_specs=VMEM,
+        out_shape=(held(OWNERS * BODY_ROWS, 128), held(512, 256, dt=bf16)),
+        in_specs=[VMEM] * 5,
+        out_specs=(VMEM,) * 2,
         scratch_shapes=scratch(BODY),
         name="body",
-    )(particles, key, near_memory(rank), near_memory(count))
-
-
-def interp(arrived, velocity):
+    )(particles, key, near_memory(rank), near_memory(count), velocity)
+
+
+def interp(arrived, fields):
     return pl.pallas_call(
         interp_kernel,
         out_shape=(held(PAD + 4 * OWNERS + 8, 128), shape(2 * OWNERS, 128, dt=i32)),
         in_specs=[VMEM] * 2,
         out_specs=(VMEM,) * 2,
-        scratch_shapes=[pltpu.VMEM((512, 256), bf16)],
         name="interp",
-    )(arrived, velocity)
+    )(arrived, near_memory(fields))
 
 
 def merge(moved, head_arrived, body_arrived):
     n = OWNERS * 256
-    g = 8
+    g = 4
     return pl.pallas_call(
         merge_kernel,
         out_shape=shape(8, n),
@@ -421,8 +408,9 @@
     key, a, b = [v.reshape(1, -1) for v in (dest_key, cell_a, cell_b)]
     first, rank, count = head(particles, key, a, b, velocity)
     arrived = exchange(first, HEAD_ROWS)
-    rest = exchange(body(particles, key, rank, count), BODY_ROWS)
-    moved, cell = interp(arrived, velocity)
+    second, fields = body(particles, key, rank, count, velocity)
+    rest = exchange(second, BODY_ROWS)
+    moved, cell = interp(arrived, fields)
     return merge(moved, arrived, rest), cell.reshape(-1)
 
 

time: 59.5 us -> 55.7 us (0.936)
  Pallas kernels: 33.6 us -> 28.3 us
  waiting for transfers between devices: 8.89 us -> 10.4 us
    pallas_call x1, Pallas kernels: 18.2 us -> 15.5 us  [interp(): pl.pallas_call(interp_kernel, out_shape=(held(PAD + 4 * OWNERS + 8, 128),...]
    all_to_all x2, waiting for transfers between devices: 8.89 us -> 10.4 us  [exchange(): lax.all_to_all(buckets.reshape(OWNERS, rows, 1, 128), ALL, 0, 0, tiled=True)]
    pallas_call x1, Pallas kernels: 2.81 us -> 1.62 us  [merge(): pl.pallas_call(merge_kernel, out_shape=shape(8, n), grid=(g,), in_specs=[...]
    pallas_call x1, Pallas kernels: 6.5 us -> 5.66 us  [head(): pl.pallas_call(head_kernel, out_shape=(held(OWNERS * HEAD_ROWS, 128), hel...]
    pallas_call x1, Pallas kernels: 6.12 us -> 5.51 us  [body(): pl.pallas_call(body_kernel, out_shape=(held(OWNERS * BODY_ROWS, 128), hel...]
  transfers between devices with their start and end apart: 2 -> 2, of which waited for: 1 -> 2; matrix products, arithmetic and copies ran while one was open for 0% -> 0% of each run, Pallas kernels for 41% -> 38%
where the time goes in v5:
time: 55.7 us; the launch traced here: 55.4 us
  Pallas kernels  28.3 us (51%)
  starting transfers between devices  16 us (29%)
  waiting for transfers between devices  10.4 us (19%)
  between operations  0.66 us (1%)
    all_to_all x2, starting transfers between devices, exchange(): lax.all_to_all(buckets.reshape(OWNERS, rows, 1, 128), ALL, 0, 0, tiled=True)  16 us
    pallas_call x1, Pallas kernels, interp(): pl.pallas_call(interp_kernel, out_shape=(held(PAD + 4 * OWNERS + 8, 128),...  15.5 us
    all_to_all x2, waiting for transfers between devices, exchange(): lax.all_to_all(buckets.reshape(OWNERS, rows, 1, 128), ALL, 0, 0, tiled=True)  10.4 us
    pallas_call x1, Pallas kernels, head(): pl.pallas_call(head_kernel, out_shape=(held(OWNERS * HEAD_ROWS, 128), hel...  5.66 us
    pallas_call x1, Pallas kernels, body(): pl.pallas_call(body_kernel, out_shape=(held(OWNERS * BODY_ROWS, 128), hel...  5.51 us
    pallas_call x1, Pallas kernels, merge(): pl.pallas_call(merge_kernel, out_shape=shape(8, n), grid=(g,), in_specs=[...  1.62 us
  transfers between devices with their start and end apart: 2, of which 2 were waited for; matrix products, arithmetic and copies ran while one was open for 0% of the time, Pallas kernels for 38%

profile of v5, /device:TPU:1, one launch (start us, length us, event | category | flops | bytes accessed | tf_op | source)
XLA Modules:
  0.0 55.4 jit_solution(17228196375270736346)
XLA Ops:
  0.6 5.7 %head.1 = (f32[1280,128]{1,0:T(8,128)}, f32[1,8192]{1,0:T(1,128)S(1)}, f32[128,128]{1,0:T(8,128)S(1)}) custom-call(f32[8,8192]{1,0:T(8,128)} %p_ref.3, s32[1,8192]{1,0:T(1,128)} %bitcast.11, s32[1,8192]{1,0:T(1,128)} %bitcast.13, s32[1,8192]{1,0:T(1,128)} %bitcast.14, f32[2,256,128]{2,1,0:T(8,128)} %v_ref.3), custom_call_target="tpu_custom_call" | custom-call | tf_op jit(solution)/shard_map/head/pallas_call | solution.py:358
  6.3 11.5 %all-to-all-start = ((f32[128,10,1,128]{3,2,1,0:T(1,128)}), f32[128,10,1,128]{3,2,1,0:T(1,128)S(1)}, u32[]{:S(2)}, u32[]{:S(2)}) async-start(f32[128,10,1,128]{3,2,1,0:T(1,128)} %bitcast.3), calls=%async_computation | async-start | bytes 1310720 | tf_op jit(solution)/shard_map/all_to_all | solution.py:403
  17.8 5.5 %body.1 = (f32[1536,128]{1,0:T(8,128)}, bf16[512,256]{1,0:T(8,128)(2,1)S(1)}) custom-call(f32[8,8192]{1,0:T(8,128)} %p_ref.3, s32[1,8192]{1,0:T(1,128)} %bitcast.12, f32[1,8192]{1,0:T(1,128)S(1)} %get-tuple-element.10.rank_ref, f32[128,128]{1,0:T(8,128)S(1)} %get-tuple-element.11.count_ref, f32[2,256,128]{2,1,0:T(8,128)} %v_ref.3), custom_call_target="tpu_custom_call" | custom-call | tf_op jit(solution)/shard_map/body/pallas_call | solution.py:369
  23.3 9.5 %all-to-all-done = f32[128,10,1,128]{3,2,1,0:T(1,128)S(1)} async-done(((f32[128,10,1,128]{3,2,1,0:T(1,128)}), f32[128,10,1,128]{3,2,1,0:T(1,128)S(1)}, u32[]{:S(2)}, u32[]{:S(2)}) %all-to-all-start) | async-done | bytes 655392 | tf_op jit(solution)/shard_map/all_to_all | solution.py:403
  32.8 4.6 %all-to-all-start.1 = ((f32[128,12,1,128]{3,2,1,0:T(1,128)}), f32[128,12,1,128]{3,2,1,0:T(1,128)S(1)}, u32[]{:S(2)}, u32[]{:S(2)}) async-start(f32[128,12,1,128]{3,2,1,0:T(1,128)} %bitcast.5), calls=%async_computation.1 | async-start | bytes 1572864 | tf_op jit(solution)/shard_map/all_to_all | solution.py:403
  37.4 15.5 %interp.1 = (f32[528,128]{1,0:T(8,128)S(1)}, s32[256,128]{1,0:T(8,128)}) custom-call(f32[1280,128]{1,0:T(8,128)S(1)} %bitcast.8, bf16[512,256]{1,0:T(8,128)(2,1)S(1)} %get-tuple-element.12.f_ref), custom_call_target="tpu_custom_call" | custom-call | tf_op jit(solution)/shard_map/interp/pallas_call | solution.py:380
  52.9 0.9 %all-to-all-done.1 = f32[128,12,1,128]{3,2,1,0:T(1,128)S(1)} async-done(((f32[128,12,1,128]{3,2,1,0:T(1,128)}), f32[128,12,1,128]{3,2,1,0:T(1,128)S(1)}, u32[]{:S(2)}, u32[]{:S(2)}) %all-to-all-start.1) | async-done | bytes 786464 | tf_op jit(solution)/shard_map/all_to_all | solution.py:403
  53.8 1.6 %merge.1 = f32[8,32768]{1,0:T(8,128)} custom-call(f32[528,128]{1,0:T(8,128)S(1)} %get-tuple-element.13.d_ref, f32[1280,128]{1,0:T(8,128)S(1)} %bitcast.9, f32[1536,128]{1,0:T(8,128)S(1)} %bitcast.10), custom_call_target="tpu_custom_call" | custom-call | tf_op jit(solution)/shard_map/merge/pallas_call | solution.py:392
Async XLA Ops:
  6.3 26.5 %all-to-all-start = ((f32[128,10,1,128]{3,2,1,0:T(1,128)}), f32[128,10,1,128]{3,2,1,0:T(1,128)S(1)}, u32[]{:S(2)}, u32[]{:S(2)}) async-start(f32[128,10,1,128]{3,2,1,0:T(1,128)} %bitcast.3), calls=%async_computation | async-start | bytes 1310720 | tf_op jit(solution)/shard_map/all_to_all | solution.py:403
  32.8 21.0 %all-to-all-start.1 = ((f32[128,12,1,128]{3,2,1,0:T(1,128)}), f32[128,12,1,128]{3,2,1,0:T(1,128)S(1)}, u32[]{:S(2)}, u32[]{:S(2)}) async-start(f32[128,12,1,128]{3,2,1,0:T(1,128)} %bitcast.5), calls=%async_computation.1 | async-start | bytes 1572864 | tf_op jit(solution)/shard_map/all_to_all | solution.py:403

commit v6 on v5

--- a/solution.py
+++ b/solution.py
@@ -12,11 +12,10 @@
 OWNERS = 128
 HEAD = 3
 BODY = 6
-HEAD_ROWS = 10
+HEAD_ROWS = 8
 BODY_ROWS = 12
 HALO = 6
 PAD = 8
-PB = 4096
 RB = 4096
 VMEM = pl.BlockSpec(memory_space=pltpu.VMEM)
 
@@ -63,13 +62,14 @@
     return BODY * half + k
 
 
-def place_all(rows_of, width, row_at, stride, key_ref, rank_ref, counts, out_ref, acc_ref, left_ref, col_ref, hot_ref):
-    n = key_ref.shape[1] // PB
+def place_all(rows_of, width, row_at, stride, key_ref, rank_ref, counts, out_ref, acc_ref, left_ref, col_ref, hot_ref, more=None):
+    size = left_ref.shape[1]
+    n = key_ref.shape[1] // size
     m = 64 * width
     ids = lax.broadcasted_iota(i32, (128, 128), 0).astype(f32)
     n_full = jnp.sum(jnp.where(counts > 128.0, 1.0, 0.0), axis=0, keepdims=True)
     hot = jnp.max(jnp.where(counts > 128.0, ids, -1.0), axis=0, keepdims=True)
-    lone = jnp.concatenate([jnp.where(n_full <= 1.0, hot, -1.0)] * (PB // 128), 1)
+    lone = jnp.concatenate([jnp.where(n_full <= 1.0, hot, -1.0)] * (size // 128), 1)
 
     def fill(rows, low, t):
         pick = one_hot(64, low)
@@ -85,32 +85,34 @@
                 at = pl.ds(o * 64 * stride + row_at(k, half), 64, stride=stride)
                 out_ref[at, :] = acc_ref[k * 64:(k + 1) * 64, o * 128:(o + 1) * 128]
 
-    acc_ref[...] = jnp.zeros(acc_ref.shape, f32)
-    hot_ref[...] = jnp.zeros(hot_ref.shape, f32)
     for i in range(n):
-        sl = block(i, PB)
+        sl = block(i, size)
         key, rank = key_ref[0:1, sl], rank_ref[0:1, sl]
         rows = rows_of(sl)
         over = (key.astype(f32) == lone) & (rank >= 128.0)
         low = jnp.where(over, -1.0, (key & 63).astype(f32))
         fill(rows, low, jnp.where(over, rank - 128.0, column_of(key, rank, 0.0)))
-        tail = jnp.concatenate([jnp.where(over, r, 0.0) for r in rows] + [jnp.zeros((8 - width, PB), f32)], 0)
+        tail = jnp.concatenate([jnp.where(over, r, 0.0) for r in rows] + [jnp.zeros((8 - width, size), f32)], 0)
         hi = tail.astype(bf16).astype(f32)
         left_ref[2 * m:, :] = jnp.concatenate([hi, tail - hi], 0).astype(bf16)
         both = nt(left_ref[...], col_ref[...])
-        acc_ref[...] += both[:m] + both[m:2 * m]
-        hot_ref[...] += (both[2 * m:2 * m + 8] + both[2 * m + 8:])[:, :128]
+        placed = both[:m] + both[m:2 * m]
+        spill = (both[2 * m:2 * m + 8] + both[2 * m + 8:])[:, :128]
+        acc_ref[...] = acc_ref[...] + placed if i else placed
+        hot_ref[...] = hot_ref[...] + spill if i else spill
     flush(0)
     base = jnp.max(jnp.maximum(hot, 0.0)).astype(i32) * stride
     for k in range(width):
         out_ref[pl.ds(base + row_at(k, 1), 1), :] = hot_ref[k:k + 1, :]
+    if more:
+        more()
 
     @pl.when(jnp.max(n_full) > 1.0)
     def _():
         acc_ref[...] = jnp.zeros(acc_ref.shape, f32)
 
         def again(i, carry):
-            sl = block(i, PB)
+            sl = block(i, size)
             key = key_ref[0:1, sl]
             fill(rows_of(sl), (key & 63).astype(f32), column_of(key, rank_ref[0:1, sl], 128.0))
             both = nt(left_ref[:2 * m, :], col_ref[...])
@@ -127,13 +129,17 @@
 
     def side(dx, dy):
         inside = (x + dx >= 0) & (x + dx < nx) & (y + dy >= 0) & (y + dy < ny)
-        return inside, jnp.where(inside, (x + dx) * ny + y + dy, 0)
+        return inside, jnp.where(inside, (x + dx) * ny + y + dy, x * ny + y)
 
     return side
 
 
-def head_kernel(p_ref, key_ref, a_ref, b_ref, v_ref, out_ref, rank_ref, count_ref, acc_ref, left_ref, col_ref, hot_ref, ut_ref, oh_ref):
+def head_kernel(p_ref, key_ref, a_ref, b_ref, v_ref, out_ref, rank_ref, count_ref, acc_ref, left_ref, col_ref, hot_ref, ut_ref, oh_ref, edge_ref, sem):
     n = p_ref.shape[1] // RB
+    last = v_ref.shape[1] - 8
+    copies = [pltpu.make_async_copy(v_ref.at[:, pl.ds(r, 8), :], edge_ref.at[e], sem.at[e]) for e, r in enumerate((0, last))]
+    for copy in copies:
+        copy.start()
     out_ref[...] = jnp.zeros(out_ref.shape, f32)
     before = lax.broadcasted_iota(i32, (256, 256), 0) < lax.broadcasted_iota(i32, (256, 256), 1)
     ut_ref[...] = jnp.where(before, 1.0, 0.0).astype(bf16)
@@ -145,44 +151,42 @@
         res = nn(oh_ref[...], ut_ref[...])
         ranks = []
         for k in range(RB // 256):
-            hot = oh_ref[k * 128:(k + 1) * 128, :].astype(f32)
-            ranks.append(jnp.sum(hot * (res[k * 128:(k + 1) * 128] + base), axis=0, keepdims=True))
-            base = base + jnp.sum(hot, axis=1, keepdims=True)
+            hot = oh_ref[k * 128:(k + 1) * 128, :]
+            here = hot * (res[k * 128:(k + 1) * 128].astype(bf16) + base.astype(bf16))
+            tree = [here[j * 16:(j + 1) * 16] for j in range(8)]
+            while len(tree) > 1:
+                tree = [u + v for u, v in zip(tree[::2], tree[1::2])]
+            ranks.append(jnp.sum(tree[0].astype(f32), axis=0, keepdims=True))
+            pair = (hot[:, :128] + hot[:, 128:]).astype(f32)
+            base = base + jnp.sum(pair, axis=1, keepdims=True)
         rank_ref[0:1, block(i, RB)] = jnp.concatenate(ranks, 1)
     count_ref[...] = jnp.broadcast_to(base, (128, 128))
+    for copy in copies:
+        copy.wait()
+    side = around()
 
     def rows_of(sl):
         cell = (a_ref[0:1, sl] * 128 + b_ref[0:1, sl] + 1).astype(f32)
         return [p_ref[0:1, sl], p_ref[1:2, sl], cell]
 
-    place_all(rows_of, HEAD, head_row, HEAD_ROWS, key_ref, rank_ref, count_ref[...], out_ref, acc_ref, left_ref, col_ref, hot_ref)
-
-    side = around()
-    height, width = v_ref.shape[1:]
-    turned = [v_ref[c].T for c in range(2)]
-    for dx in (-1, 0, 1):
-        for dy in (-1, 0, 1):
-            if dx == 0 and dy == 0:
-                continue
-            row = height - 1 if dx > 0 else 0
-            col = width - 1 if dy > 0 else 0
-            inside, who = side(dx, dy)
-            base = who * HEAD_ROWS + HALO
-
-            @pl.when(inside)
-            def _():
+    def halo():
+        for e, dx in enumerate((-1, 1)):
+            for dy in (-1, 0, 1):
+                at = side(dx, dy)[1] * HEAD_ROWS + HALO
                 for c in range(2):
-                    if dx:
-                        out_ref[pl.ds(base + c, 1), :] = v_ref[c, row:row + 1, :]
-                    else:
-                        for h in range(2):
-                            out_ref[pl.ds(base + 2 * c + h, 1), :] = turned[c][col:col + 1, h * 128:(h + 1) * 128]
-
-
-def body_kernel(p_ref, key_ref, rank_ref, count_ref, v_ref, out_ref, f_ref, acc_ref, left_ref, col_ref, hot_ref):
+                    row = 7 if e else 0
+                    out_ref[pl.ds(at + c, 1), :] = edge_ref[e, c, row:row + 1, :]
+
+    place_all(rows_of, HEAD, head_row, HEAD_ROWS, key_ref, rank_ref, count_ref[...], out_ref, acc_ref, left_ref, col_ref, hot_ref, halo)
+
+
+def body_kernel(p_ref, key_ref, rank_ref, count_ref, v_ref, out_ref, f_ref, first_ref, last_ref, acc_ref, left_ref, col_ref, hot_ref):
     out_ref[...] = jnp.zeros(out_ref.shape, f32)
     for c in range(2):
-        hi, lo = split(v_ref[c].T)
+        turned = v_ref[c].T
+        first_ref[c:c + 1, :] = turned[0:1]
+        last_ref[c:c + 1, :] = turned[127:128]
+        hi, lo = split(turned)
         f_ref[c * 128:(c + 1) * 128, :] = hi
         f_ref[256 + c * 128:256 + (c + 1) * 128, :] = lo
 
@@ -203,7 +207,7 @@
     return out
 
 
-def interp_kernel(r_ref, f_ref, out_ref, cell_ref):
+def interp_kernel(r_ref, f_ref, tall_ref, out_ref, cell_ref):
     S = 16
     side = around()
 
@@ -218,7 +222,7 @@
     east = jnp.concatenate([from_side(dx, 1, c) for c in range(2) for dx in (-1, 1)] + [z4], 0)
     west = jnp.broadcast_to(west[:, 127:128], (8, 128))
     east = jnp.broadcast_to(east[:, 0:1], (8, 128))
-    tall = jnp.concatenate([from_side(0, dy, 2 * c + h) for h in range(2) for c in range(2) for dy in (-1, 1)], 0)
+    tall = tall_ref[...]
     sub = lax.broadcasted_iota(i32, (8, 128), 0)
     even = (sub & 1) == 0
     upper = sub < 4
@@ -327,7 +331,8 @@
     for s in range(S):
         for h in range(2):
             src = s0 + s
-            w = r1_ref[pl.ds(src * HEAD_ROWS + 2 * h, 8), :]
+            w = r1_ref[pl.ds(pl.multiple_of(src * HEAD_ROWS, HEAD_ROWS), 8), :]
+            w = pltpu.roll(w, 6, 0) if h else w
             at = src * BODY_ROWS + BODY * h - 2
             if s == 0 and h == 0:
                 u = jnp.where(s0 == 0, lead, r2_ref[pl.ds(jnp.maximum(at, 0), 8), :])
@@ -349,8 +354,8 @@
     return pltpu.with_memory_space_constraint(x, pltpu.VMEM)
 
 
-def scratch(width):
-    return [pltpu.VMEM((64 * width, 256), f32), pltpu.VMEM((128 * width + 16, PB), bf16), pltpu.VMEM((256, PB), bf16), pltpu.VMEM((8, 128), f32)]
+def scratch(width, size):
+    return [pltpu.VMEM((64 * width, 256), f32), pltpu.VMEM((128 * width + 16, size), bf16), pltpu.VMEM((256, size), bf16), pltpu.VMEM((8, 128), f32)]
 
 
 def head(particles, key, a, b, velocity):
@@ -358,9 +363,10 @@
     return pl.pallas_call(
         head_kernel,
         out_shape=(held(OWNERS * HEAD_ROWS, 128), held(1, n), held(128, 128)),
-        in_specs=[VMEM] * 5,
+        in_specs=[VMEM] * 4 + [pl.BlockSpec(memory_space=pl.ANY)],
         out_specs=(VMEM,) * 3,
-        scratch_shapes=scratch(HEAD) + [pltpu.VMEM((256, 256), bf16), pltpu.VMEM((RB // 2, 256), bf16)],
+        scratch_shapes=scratch(HEAD, n // 2)
+        + [pltpu.VMEM((256, 256), bf16), pltpu.VMEM((RB // 2, 256), bf16), pltpu.VMEM((2, 2, 8, 128), f32), pltpu.SemaphoreType.DMA((2,))],
         name="head",
     )(particles, key, a, b, velocity)
 
@@ -368,22 +374,33 @@
 def body(particles, key, rank, count, velocity):
     return pl.pallas_call(
         body_kernel,
-        out_shape=(held(OWNERS * BODY_ROWS, 128), held(512, 256, dt=bf16)),
+        out_shape=(held(OWNERS * BODY_ROWS, 128), held(512, 256, dt=bf16), shape(2, 256), shape(2, 256)),
         in_specs=[VMEM] * 5,
-        out_specs=(VMEM,) * 2,
-        scratch_shapes=scratch(BODY),
+        out_specs=(VMEM,) * 4,
+        scratch_shapes=scratch(BODY, particles.shape[1]),
         name="body",
     )(particles, key, near_memory(rank), near_memory(count), velocity)
 
 
-def interp(arrived, fields):
+def tall_kernel(west_ref, east_ref, out_ref):
+    for h in range(2):
+        for c in range(2):
+            for k, ref in enumerate((west_ref, east_ref)):
+                out_ref[4 * h + 2 * c + k:4 * h + 2 * c + k + 1, :] = ref[c:c + 1, h * 128:(h + 1) * 128]
+
+
+def tall_sides(west, east):
+    return pl.pallas_call(tall_kernel, out_shape=held(8, 128), in_specs=[VMEM] * 2, out_specs=VMEM, name="tall")(near_memory(west), near_memory(east))
+
+
+def interp(arrived, fields, tall):
     return pl.pallas_call(
         interp_kernel,
         out_shape=(held(PAD + 4 * OWNERS + 8, 128), shape(2 * OWNERS, 128, dt=i32)),
-        in_specs=[VMEM] * 2,
+        in_specs=[VMEM] * 3,
         out_specs=(VMEM,) * 2,
         name="interp",
-    )(arrived, near_memory(fields))
+    )(arrived, near_memory(fields), near_memory(tall))
 
 
 def merge(moved, head_arrived, body_arrived):
@@ -399,6 +416,13 @@
     )(near_memory(moved), head_arrived, body_arrived)
 
 
+def both_sides(first, last, axis):
+    peers = lax.axis_size(axis)
+    up = [(i, i + 1) for i in range(peers - 1)]
+    down = [(j, i) for i, j in up]
+    return lax.ppermute(last, axis, up), lax.ppermute(first, axis, down)
+
+
 def exchange(buckets, rows):
     out = lax.all_to_all(buckets.reshape(OWNERS, rows, 1, 128), ALL, 0, 0, tiled=True)
     return near_memory(out.reshape(OWNERS * rows, 128))
@@ -406,11 +430,12 @@
 
 def shards(particles, dest_key, cell_a, cell_b, velocity):
     key, a, b = [v.reshape(1, -1) for v in (dest_key, cell_a, cell_b)]
-    first, rank, count = head(particles, key, a, b, velocity)
-    arrived = exchange(first, HEAD_ROWS)
-    second, fields = body(particles, key, rank, count, velocity)
-    rest = exchange(second, BODY_ROWS)
-    moved, cell = interp(arrived, fields)
+    near, rank, count = head(particles, key, a, b, velocity)
+    arrived = exchange(near, HEAD_ROWS)
+    far, fields, first, last = body(particles, key, rank, count, velocity)
+    tall = tall_sides(*both_sides(first, last, WIDE))
+    rest = exchange(far, BODY_ROWS)
+    moved, cell = interp(arrived, fields, tall)
     return merge(moved, arrived, rest), cell.reshape(-1)
 
 

time: 55.7 us -> 64.2 us (1.15)
  starting transfers between devices: 16 us -> 21.6 us
  waiting for transfers between devices: 10.4 us -> 12.9 us
    ppermute x0 -> x2, starting transfers between devices: none -> 5.46 us  [both_sides(): return (lax.ppermute(last, axis, up), lax.ppermute(first, axis, down))]
    ppermute x0 -> x2, waiting for transfers between devices: none -> 4.87 us  [both_sides(): return (lax.ppermute(last, axis, up), lax.ppermute(first, axis, down))]
    all_to_all x2, waiting for transfers between devices: 10.4 us -> 8.07 us  [exchange(): lax.all_to_all(buckets.reshape(OWNERS, rows, 1, 128), ALL, 0, 0, tiled=True)]
  transfers between devices with their start and end apart: 2 -> 4, of which waited for: 2 -> 3; matrix products, arithmetic and copies ran while one was open for 0% -> 0% of each run, Pallas kernels for 38% -> 33%
where the time goes in v6:
time: 64.2 us; the launch traced here: 63.8 us
  Pallas kernels  28.6 us (45%)
  starting transfers between devices  21.6 us (34%)
  waiting for transfers between devices  12.9 us (20%)
  between operations  0.71 us (1%)
    all_to_all x2, starting transfers between devices, exchange(): lax.all_to_all(buckets.reshape(OWNERS, rows, 1, 128), ALL, 0, 0, tiled=True)  16.1 us
    pallas_call x1, Pallas kernels, interp(): pl.pallas_call(interp_kernel, out_shape=(held(PAD + 4 * OWNERS + 8, 128),...  15.5 us
    all_to_all x2, waiting for transfers between devices, exchange(): lax.all_to_all(buckets.reshape(OWNERS, rows, 1, 128), ALL, 0, 0, tiled=True)  8.07 us
    pallas_call x1, Pallas kernels, head(): pl.pallas_call(head_kernel, out_shape=(held(OWNERS * HEAD_ROWS, 128), hel...  5.91 us
    pallas_call x1, Pallas kernels, body(): pl.pallas_call(body_kernel, out_shape=(held(OWNERS * BODY_ROWS, 128), hel...  5.54 us
    ppermute x2, starting transfers between devices, both_sides(): return (lax.ppermute(last, axis, up), lax.ppermute(first, axis, down))  5.46 us
    ppermute x2, waiting for transfers between devices, both_sides(): return (lax.ppermute(last, axis, up), lax.ppermute(first, axis, down))  4.87 us
    pallas_call x1, Pallas kernels, merge(): pl.pallas_call(merge_kernel, out_shape=shape(8, n), grid=(g,), in_specs=[...  1.63 us
  transfers between devices with their start and end apart: 4, of which 3 were waited for; matrix products, arithmetic and copies ran while one was open for 0% of the time, Pallas kernels for 33%

profile of v6, /device:TPU:1, one launch (start us, length us, event | category | flops | bytes accessed | tf_op | source)
XLA Modules:
  0.0 63.8 jit_solution(1889880616055078858)
XLA Ops:
  0.6 5.9 %head.1 = (f32[1024,128]{1,0:T(8,128)}, f32[1,8192]{1,0:T(1,128)S(1)}, f32[128,128]{1,0:T(8,128)S(1)}) custom-call(f32[8,8192]{1,0:T(8,128)} %p_ref.3, s32[1,8192]{1,0:T(1,128)} %bitcast.13, s32[1,8192]{1,0:T(1,128)} %bitcast.15, s32[1,8192]{1,0:T(1,128)} %bitcast.16, f32[2,256,128]{2,1,0:T(8,128)} %v_ref.3), custom_call_target="tpu_custom_call" | custom-call | tf_op jit(solution)/shard_map/head/pallas_call | solution.py:363
  6.6 11.5 %all-to-all-start = ((f32[128,8,1,128]{3,1,2,0:T(8,128)}), f32[128,8,1,128]{3,1,2,0:T(8,128)S(1)}, u32[]{:S(2)}, u32[]{:S(2)}) async-start(f32[128,8,1,128]{3,1,2,0:T(8,128)} %bitcast.4), calls=%async_computation | async-start | bytes 1048576 | tf_op jit(solution)/shard_map/all_to_all | solution.py:427
  18.1 5.5 %body.1 = (f32[1536,128]{1,0:T(8,128)}, bf16[512,256]{1,0:T(8,128)(2,1)S(1)}, f32[2,256]{1,0:T(2,128)}, f32[2,256]{1,0:T(2,128)}) custom-call(f32[8,8192]{1,0:T(8,128)} %p_ref.3, s32[1,8192]{1,0:T(1,128)} %bitcast.14, f32[1,8192]{1,0:T(1,128)S(1)} %get-tuple-element.12.rank_ref, f32[128,128]{1,0:T(8,128)S(1)} %get-tuple-element.13.count_ref, ...), custom_call_target="tpu_custom_call" | custom-call | tf_op jit(solution)/shard_map/body/pallas_call | solution.py:375
  23.6 8.1 %all-to-all-done = f32[128,8,1,128]{3,1,2,0:T(8,128)S(1)} async-done(((f32[128,8,1,128]{3,1,2,0:T(8,128)}), f32[128,8,1,128]{3,1,2,0:T(8,128)S(1)}, u32[]{:S(2)}, u32[]{:S(2)}) %all-to-all-start) | async-done | bytes 524320 | tf_op jit(solution)/shard_map/all_to_all | solution.py:427
  31.7 0.0 copy-start.1
  31.7 4.6 %all-to-all-start.1 = ((f32[128,12,1,128]{3,2,1,0:T(1,128)}), f32[128,12,1,128]{3,2,1,0:T(1,128)S(1)}, u32[]{:S(2)}, u32[]{:S(2)}) async-start(f32[128,12,1,128]{3,2,1,0:T(1,128)} %bitcast.6), calls=%async_computation.1 | async-start | bytes 1572864 | tf_op jit(solution)/shard_map/all_to_all | solution.py:427
  36.3 0.0 copy-start
  36.3 0.0 copy-done.1
  36.3 3.5 %collective-permute-start = (f32[2,256]{1,0:T(2,128)S(1)}, f32[2,256]{1,0:T(2,128)S(1)}, u32[]{:S(2)}, u32[]{:S(2)}) collective-permute-start(f32[2,256]{1,0:T(2,128)S(1)} %copy-done.1), channel_id=1, source_target_pairs={{0,1},{1,2},{2,3},{3,4},{4,5},{5,6},{6,7},{7,8},{8,9},{9,10},{10,1... | collective-permute-start | bytes 6152 | tf_op jit(solution)/shard_map/ppermute | solution.py:423
  39.8 0.0 copy-done
  39.9 1.9 %collective-permute-start.1 = (f32[2,256]{1,0:T(2,128)S(1)}, f32[2,256]{1,0:T(2,128)S(1)}, u32[]{:S(2)}, u32[]{:S(2)}) collective-permute-start(f32[2,256]{1,0:T(2,128)S(1)} %copy-done), channel_id=1, source_target_pairs={{1,0},{2,1},{3,2},{4,3},{5,4},{6,5},{7,6},{8,7},{9,8},{10,9},{11,1... | collective-permute-start | bytes 6152 | tf_op jit(solution)/shard_map/ppermute | solution.py:423
  41.8 1.6 %collective-permute-done.west_ref = f32[2,256]{1,0:T(2,128)S(1)} collective-permute-done((f32[2,256]{1,0:T(2,128)S(1)}, f32[2,256]{1,0:T(2,128)S(1)}, u32[]{:S(2)}, u32[]{:S(2)}) %collective-permute-start) | collective-permute-done | bytes 2080 | tf_op jit(solution)/shard_map/ppermute | solution.py:423
  43.4 3.2 %collective-permute-done.1.east_ref = f32[2,256]{1,0:T(2,128)S(1)} collective-permute-done((f32[2,256]{1,0:T(2,128)S(1)}, f32[2,256]{1,0:T(2,128)S(1)}, u32[]{:S(2)}, u32[]{:S(2)}) %collective-permute-start.1) | collective-permute-done | bytes 2080 | tf_op jit(solution)/shard_map/ppermute | solution.py:423
  46.7 15.5 %interp.1 = (f32[528,128]{1,0:T(8,128)S(1)}, s32[256,128]{1,0:T(8,128)}) custom-call(f32[1024,128]{1,0:T(8,128)S(1)} %bitcast.10, bf16[512,256]{1,0:T(8,128)(2,1)S(1)} %get-tuple-element.14.f_ref, f32[8,128]{1,0:T(8,128)S(1)} %tall.1.tall_ref), custom_call_target="tpu_custom_call" | custom-call | tf_op jit(solution)/shard_map/interp/pallas_call | solution.py:397
  62.2 0.0 all-to-all-done.1
  62.2 1.6 %merge.1 = f32[8,32768]{1,0:T(8,128)} custom-call(f32[528,128]{1,0:T(8,128)S(1)} %get-tuple-element.17.d_ref, f32[1024,128]{1,0:T(8,128)S(1)} %bitcast.11, f32[1536,128]{1,0:T(8,128)S(1)} %bitcast.12), custom_call_target="tpu_custom_call" | custom-call | tf_op jit(solution)/shard_map/merge/pallas_call | solution.py:409
  (1 shorter events, 0.0 us)
Async XLA Ops:
  6.6 25.1 %all-to-all-start = ((f32[128,8,1,128]{3,1,2,0:T(8,128)}), f32[128,8,1,128]{3,1,2,0:T(8,128)S(1)}, u32[]{:S(2)}, u32[]{:S(2)}) async-start(f32[128,8,1,128]{3,1,2,0:T(8,128)} %bitcast.4), calls=%async_computation | async-start | bytes 1048576 | tf_op jit(solution)/shard_map/all_to_all | solution.py:427
  31.7 4.6 %copy-start.1 = (f32[2,256]{1,0:T(2,128)S(1)}, f32[2,256]{1,0:T(2,128)}, u32[]{:S(2)}) copy-start(f32[2,256]{1,0:T(2,128)} %get-tuple-element.15) | copy-start | bytes 6148
  31.7 30.5 %all-to-all-start.1 = ((f32[128,12,1,128]{3,2,1,0:T(1,128)}), f32[128,12,1,128]{3,2,1,0:T(1,128)S(1)}, u32[]{:S(2)}, u32[]{:S(2)}) async-start(f32[128,12,1,128]{3,2,1,0:T(1,128)} %bitcast.6), calls=%async_computation.1 | async-start | bytes 1572864 | tf_op jit(solution)/shard_map/all_to_all | solution.py:427
  36.3 3.6 %copy-start = (f32[2,256]{1,0:T(2,128)S(1)}, f32[2,256]{1,0:T(2,128)}, u32[]{:S(2)}) copy-start(f32[2,256]{1,0:T(2,128)} %get-tuple-element.16) | copy-start | bytes 6148
  36.3 7.1 %collective-permute-start = (f32[2,256]{1,0:T(2,128)S(1)}, f32[2,256]{1,0:T(2,128)S(1)}, u32[]{:S(2)}, u32[]{:S(2)}) collective-permute-start(f32[2,256]{1,0:T(2,128)S(1)} %copy-done.1), channel_id=1, source_target_pairs={{0,1},{1,2},{2,3},{3,4},{4,5},{5,6},{6,7},{7,8},{8,9},{9,10},{10,1... | collective-permute-start | bytes 6152 | tf_op jit(solution)/shard_map/ppermute | solution.py:423
  39.9 6.8 %collective-permute-start.1 = (f32[2,256]{1,0:T(2,128)S(1)}, f32[2,256]{1,0:T(2,128)S(1)}, u32[]{:S(2)}, u32[]{:S(2)}) collective-permute-start(f32[2,256]{1,0:T(2,128)S(1)} %copy-done), channel_id=1, source_target_pairs={{1,0},{2,1},{3,2},{4,3},{5,4},{6,5},{7,6},{8,7},{9,8},{10,9},{11,1... | collective-permute-start | bytes 6152 | tf_op jit(solution)/shard_map/ppermute | solution.py:423

commit v7 on v5

--- a/solution.py
+++ b/solution.py
@@ -16,7 +16,6 @@
 BODY_ROWS = 12
 HALO = 6
 PAD = 8
-PB = 4096
 RB = 4096
 VMEM = pl.BlockSpec(memory_space=pltpu.VMEM)
 
@@ -63,13 +62,14 @@
     return BODY * half + k
 
 
-def place_all(rows_of, width, row_at, stride, key_ref, rank_ref, counts, out_ref, acc_ref, left_ref, col_ref, hot_ref):
-    n = key_ref.shape[1] // PB
+def place_all(rows_of, width, row_at, stride, key_ref, rank_ref, counts, out_ref, acc_ref, left_ref, col_ref, more=None):
+    size = left_ref.shape[1]
+    n = key_ref.shape[1] // size
     m = 64 * width
     ids = lax.broadcasted_iota(i32, (128, 128), 0).astype(f32)
     n_full = jnp.sum(jnp.where(counts > 128.0, 1.0, 0.0), axis=0, keepdims=True)
     hot = jnp.max(jnp.where(counts > 128.0, ids, -1.0), axis=0, keepdims=True)
-    lone = jnp.concatenate([jnp.where(n_full <= 1.0, hot, -1.0)] * (PB // 128), 1)
+    lone = jnp.concatenate([jnp.where(n_full <= 1.0, hot, -1.0)] * (size // 128), 1)
 
     def fill(rows, low, t):
         pick = one_hot(64, low)
@@ -79,46 +79,47 @@
             left_ref[m + k * 64:m + (k + 1) * 64, :] = pick * lo
         col_ref[...] = one_hot(256, t)
 
-    def flush(half):
+    def flush(half, terms):
         for k in range(width):
             for o in range(2):
                 at = pl.ds(o * 64 * stride + row_at(k, half), 64, stride=stride)
-                out_ref[at, :] = acc_ref[k * 64:(k + 1) * 64, o * 128:(o + 1) * 128]
-
-    acc_ref[...] = jnp.zeros(acc_ref.shape, f32)
-    hot_ref[...] = jnp.zeros(hot_ref.shape, f32)
+                lanes = slice(o * 128, (o + 1) * 128)
+                out_ref[at, :] = sum(acc_ref[t, r + k * 64:r + (k + 1) * 64, lanes] for t, r in terms)
+
     for i in range(n):
-        sl = block(i, PB)
+        sl = block(i, size)
         key, rank = key_ref[0:1, sl], rank_ref[0:1, sl]
         rows = rows_of(sl)
         over = (key.astype(f32) == lone) & (rank >= 128.0)
         low = jnp.where(over, -1.0, (key & 63).astype(f32))
         fill(rows, low, jnp.where(over, rank - 128.0, column_of(key, rank, 0.0)))
-        tail = jnp.concatenate([jnp.where(over, r, 0.0) for r in rows] + [jnp.zeros((8 - width, PB), f32)], 0)
+        tail = jnp.concatenate([jnp.where(over, r, 0.0) for r in rows] + [jnp.zeros((8 - width, size), f32)], 0)
         hi = tail.astype(bf16).astype(f32)
         left_ref[2 * m:, :] = jnp.concatenate([hi, tail - hi], 0).astype(bf16)
-        both = nt(left_ref[...], col_ref[...])
-        acc_ref[...] += both[:m] + both[m:2 * m]
-        hot_ref[...] += (both[2 * m:2 * m + 8] + both[2 * m + 8:])[:, :128]
-    flush(0)
+        for k in range(2):
+            lanes = slice(k * size // 2, (k + 1) * size // 2)
+            acc_ref[2 * i + k] = nt(left_ref[:, lanes], col_ref[:, lanes])
+    flush(0, [(k, part * m) for k in range(2 * n) for part in range(2)])
+    spill = sum(acc_ref[k, 2 * m + 8 * j:2 * m + 8 * j + 8, :128] for k in range(2 * n) for j in range(2))
     base = jnp.max(jnp.maximum(hot, 0.0)).astype(i32) * stride
     for k in range(width):
-        out_ref[pl.ds(base + row_at(k, 1), 1), :] = hot_ref[k:k + 1, :]
+        out_ref[pl.ds(base + row_at(k, 1), 1), :] = spill[k:k + 1]
+    if more:
+        more()
 
     @pl.when(jnp.max(n_full) > 1.0)
     def _():
-        acc_ref[...] = jnp.zeros(acc_ref.shape, f32)
+        acc_ref[0] = jnp.zeros(acc_ref.shape[1:], f32)
 
         def again(i, carry):
-            sl = block(i, PB)
+            sl = block(i, size)
             key = key_ref[0:1, sl]
             fill(rows_of(sl), (key & 63).astype(f32), column_of(key, rank_ref[0:1, sl], 128.0))
-            both = nt(left_ref[:2 * m, :], col_ref[...])
-            acc_ref[...] += both[:m] + both[m:]
+            acc_ref[0, :2 * m, :] += nt(left_ref[:2 * m, :], col_ref[...])
             return carry
 
         lax.fori_loop(0, n, again, 0)
-        flush(1)
+        flush(1, [(0, 0), (0, m)])
 
 
 def around():
@@ -127,59 +128,68 @@
 
     def side(dx, dy):
         inside = (x + dx >= 0) & (x + dx < nx) & (y + dy >= 0) & (y + dy < ny)
-        return inside, jnp.where(inside, (x + dx) * ny + y + dy, 0)
+        return inside, jnp.where(inside, (x + dx) * ny + y + dy, x * ny + y)
 
     return side
 
 
-def head_kernel(p_ref, key_ref, a_ref, b_ref, v_ref, out_ref, rank_ref, count_ref, acc_ref, left_ref, col_ref, hot_ref, ut_ref, oh_ref):
+def head_kernel(p_ref, key_ref, a_ref, b_ref, v_ref, out_ref, rank_ref, count_ref, acc_ref, left_ref, col_ref, ut_ref, oh_ref, edge_ref, sem):
     n = p_ref.shape[1] // RB
+    copy = pltpu.make_async_copy(v_ref, edge_ref, sem)
+    copy.start()
     out_ref[...] = jnp.zeros(out_ref.shape, f32)
     before = lax.broadcasted_iota(i32, (256, 256), 0) < lax.broadcasted_iota(i32, (256, 256), 1)
     ut_ref[...] = jnp.where(before, 1.0, 0.0).astype(bf16)
-    base = jnp.zeros((128, 1), f32)
-    for i in range(n):
-        key = key_ref[0:1, block(i, RB)].astype(f32)
+    count_ref[...] = jnp.zeros(count_ref.shape, f32)
+
+    def rank_block(i, carry):
+        sl = block(i, RB)
+        key = key_ref[0:1, sl].astype(f32)
         for k in range(RB // 256):
             oh_ref[k * 128:(k + 1) * 128, :] = one_hot(128, key[:, k * 256:(k + 1) * 256])
         res = nn(oh_ref[...], ut_ref[...])
+        base = count_ref[...]
         ranks = []
         for k in range(RB // 256):
-            hot = oh_ref[k * 128:(k + 1) * 128, :].astype(f32)
-            ranks.append(jnp.sum(hot * (res[k * 128:(k + 1) * 128] + base), axis=0, keepdims=True))
-            base = base + jnp.sum(hot, axis=1, keepdims=True)
-        rank_ref[0:1, block(i, RB)] = jnp.concatenate(ranks, 1)
-    count_ref[...] = jnp.broadcast_to(base, (128, 128))
+            hot = oh_ref[k * 128:(k + 1) * 128, :]
+            low = base.astype(bf16)
+            here = hot * (res[k * 128:(k + 1) * 128].astype(bf16) + jnp.concatenate([low, low], 1))
+            tree = [here[j * 16:(j + 1) * 16] for j in range(8)]
+            while len(tree) > 1:
+                tree = [u + v for u, v in zip(tree[::2], tree[1::2])]
+            ranks.append(jnp.sum(tree[0].astype(f32), axis=0, keepdims=True))
+            pair = (hot[:, :128] + hot[:, 128:]).astype(f32)
+            base = base + jnp.sum(pair, axis=1, keepdims=True)
+        count_ref[...] = base
+        rank_ref[0:1, sl] = jnp.concatenate(ranks, 1)
+        return carry
+
+    lax.fori_loop(0, n, rank_block, 0)
+    copy.wait()
+    side = around()
+    turned = [edge_ref[c].T for c in range(2)]
 
     def rows_of(sl):
         cell = (a_ref[0:1, sl] * 128 + b_ref[0:1, sl] + 1).astype(f32)
         return [p_ref[0:1, sl], p_ref[1:2, sl], cell]
 
-    place_all(rows_of, HEAD, head_row, HEAD_ROWS, key_ref, rank_ref, count_ref[...], out_ref, acc_ref, left_ref, col_ref, hot_ref)
-
-    side = around()
-    height, width = v_ref.shape[1:]
-    turned = [v_ref[c].T for c in range(2)]
-    for dx in (-1, 0, 1):
-        for dy in (-1, 0, 1):
-            if dx == 0 and dy == 0:
-                continue
-            row = height - 1 if dx > 0 else 0
-            col = width - 1 if dy > 0 else 0
-            inside, who = side(dx, dy)
-            base = who * HEAD_ROWS + HALO
-
-            @pl.when(inside)
-            def _():
+    def halo():
+        for dx in (-1, 0, 1):
+            for dy in (-1, 0, 1):
+                at = side(dx, dy)[1] * HEAD_ROWS + HALO
                 for c in range(2):
                     if dx:
-                        out_ref[pl.ds(base + c, 1), :] = v_ref[c, row:row + 1, :]
-                    else:
+                        row = edge_ref.shape[1] - 1 if dx > 0 else 0
+                        out_ref[pl.ds(at + c, 1), :] = edge_ref[c, row:row + 1, :]
+                    elif dy:
+                        col = edge_ref.shape[2] - 1 if dy > 0 else 0
                         for h in range(2):
-                            out_ref[pl.ds(base + 2 * c + h, 1), :] = turned[c][col:col + 1, h * 128:(h + 1) * 128]
-
-
-def body_kernel(p_ref, key_ref, rank_ref, count_ref, v_ref, out_ref, f_ref, acc_ref, left_ref, col_ref, hot_ref):
+                            out_ref[pl.ds(at + 2 * c + h, 1), :] = turned[c][col:col + 1, h * 128:(h + 1) * 128]
+
+    place_all(rows_of, HEAD, head_row, HEAD_ROWS, key_ref, rank_ref, count_ref[...], out_ref, acc_ref, left_ref, col_ref, halo)
+
+
+def body_kernel(p_ref, key_ref, rank_ref, count_ref, v_ref, out_ref, f_ref, acc_ref, left_ref, col_ref):
     out_ref[...] = jnp.zeros(out_ref.shape, f32)
     for c in range(2):
         hi, lo = split(v_ref[c].T)
@@ -189,7 +199,7 @@
     def rows_of(sl):
         return [p_ref[k:k + 1, sl] for k in range(2, 8)]
 
-    place_all(rows_of, BODY, body_row, BODY_ROWS, key_ref, rank_ref, count_ref[...], out_ref, acc_ref, left_ref, col_ref, hot_ref)
+    place_all(rows_of, BODY, body_row, BODY_ROWS, key_ref, rank_ref, count_ref[...], out_ref, acc_ref, left_ref, col_ref)
 
 
 def quad(t):
@@ -349,8 +359,9 @@
     return pltpu.with_memory_space_constraint(x, pltpu.VMEM)
 
 
-def scratch(width):
-    return [pltpu.VMEM((64 * width, 256), f32), pltpu.VMEM((128 * width + 16, PB), bf16), pltpu.VMEM((256, PB), bf16), pltpu.VMEM((8, 128), f32)]
+def scratch(width, size):
+    rows = 128 * width + 16
+    return [pltpu.VMEM((16384 // size, rows, 256), f32), pltpu.VMEM((rows, size), bf16), pltpu.VMEM((256, size), bf16)]
 
 
 def head(particles, key, a, b, velocity):
@@ -358,9 +369,10 @@
     return pl.pallas_call(
         head_kernel,
         out_shape=(held(OWNERS * HEAD_ROWS, 128), held(1, n), held(128, 128)),
-        in_specs=[VMEM] * 5,
+        in_specs=[VMEM] * 4 + [pl.BlockSpec(memory_space=pl.ANY)],
         out_specs=(VMEM,) * 3,
-        scratch_shapes=scratch(HEAD) + [pltpu.VMEM((256, 256), bf16), pltpu.VMEM((RB // 2, 256), bf16)],
+        scratch_shapes=scratch(HEAD, n // 2)
+        + [pltpu.VMEM((256, 256), bf16), pltpu.VMEM((RB // 2, 256), bf16), pltpu.VMEM((2, 256, 128), f32), pltpu.SemaphoreType.DMA],
         name="head",
     )(particles, key, a, b, velocity)
 
@@ -371,7 +383,7 @@
         out_shape=(held(OWNERS * BODY_ROWS, 128), held(512, 256, dt=bf16)),
         in_specs=[VMEM] * 5,
         out_specs=(VMEM,) * 2,
-        scratch_shapes=scratch(BODY),
+        scratch_shapes=scratch(BODY, particles.shape[1] // 2),
         name="body",
     )(particles, key, near_memory(rank), near_memory(count), velocity)
 

time: 55.7 us -> 55 us (0.987)
  Pallas kernels: 28.3 us -> 27.6 us
    pallas_call x1, Pallas kernels: 5.66 us -> 4.95 us  [head(): pl.pallas_call(head_kernel, out_shape=(held(OWNERS * HEAD_ROWS, 128), hel...]
  transfers between devices with their start and end apart: 2 -> 2, of which waited for: 2 -> 2; matrix products, arithmetic and copies ran while one was open for 0% -> 0% of each run, Pallas kernels for 38% -> 39%
where the time goes in v7:
time: 55 us; the launch traced here: 54.7 us
  Pallas kernels  27.6 us (50%)
  starting transfers between devices  16.1 us (29%)
  waiting for transfers between devices  10.4 us (19%)
  between operations  0.66 us (1%)
    all_to_all x2, starting transfers between devices, exchange(): lax.all_to_all(buckets.reshape(OWNERS, rows, 1, 128), ALL, 0, 0, tiled=True)  16.1 us
    pallas_call x1, Pallas kernels, interp(): pl.pallas_call(interp_kernel, out_shape=(held(PAD + 4 * OWNERS + 8, 128),...  15.5 us
    all_to_all x2, waiting for transfers between devices, exchange(): lax.all_to_all(buckets.reshape(OWNERS, rows, 1, 128), ALL, 0, 0, tiled=True)  10.4 us
    pallas_call x1, Pallas kernels, body(): pl.pallas_call(body_kernel, out_shape=(held(OWNERS * BODY_ROWS, 128), hel...  5.52 us
    pallas_call x1, Pallas kernels, head(): pl.pallas_call(head_kernel, out_shape=(held(OWNERS * HEAD_ROWS, 128), hel...  4.95 us
    pallas_call x1, Pallas kernels, merge(): pl.pallas_call(merge_kernel, out_shape=shape(8, n), grid=(g,), in_specs=[...  1.62 us
  transfers between devices with their start and end apart: 2, of which 2 were waited for; matrix products, arithmetic and copies ran while one was open for 0% of the time, Pallas kernels for 39%

profile of v7, /device:TPU:1, one launch (start us, length us, event | category | flops | bytes accessed | tf_op | source)
XLA Modules:
  0.0 54.7 jit_solution(4747055498860717824)
XLA Ops:
  0.6 5.0 %head.1 = (f32[1280,128]{1,0:T(8,128)}, f32[1,8192]{1,0:T(1,128)S(1)}, f32[128,128]{1,0:T(8,128)S(1)}) custom-call(f32[8,8192]{1,0:T(8,128)} %p_ref.3, s32[1,8192]{1,0:T(1,128)} %bitcast.11, s32[1,8192]{1,0:T(1,128)} %bitcast.13, s32[1,8192]{1,0:T(1,128)} %bitcast.14, f32[2,256,128]{2,1,0:T(8,128)} %v_ref.3), custom_call_target="tpu_custom_call" | custom-call | tf_op jit(solution)/shard_map/head/pallas_call | solution.py:369
  5.6 11.5 %all-to-all-start = ((f32[128,10,1,128]{3,2,1,0:T(1,128)}), f32[128,10,1,128]{3,2,1,0:T(1,128)S(1)}, u32[]{:S(2)}, u32[]{:S(2)}) async-start(f32[128,10,1,128]{3,2,1,0:T(1,128)} %bitcast.3), calls=%async_computation | async-start | bytes 1310720 | tf_op jit(solution)/shard_map/all_to_all | solution.py:415
  17.1 5.5 %body.1 = (f32[1536,128]{1,0:T(8,128)}, bf16[512,256]{1,0:T(8,128)(2,1)S(1)}) custom-call(f32[8,8192]{1,0:T(8,128)} %p_ref.3, s32[1,8192]{1,0:T(1,128)} %bitcast.12, f32[1,8192]{1,0:T(1,128)S(1)} %get-tuple-element.10.rank_ref, f32[128,128]{1,0:T(8,128)S(1)} %get-tuple-element.11.count_ref, f32[2,256,128]{2,1,0:T(8,128)} %v_ref.3), custom_call_target="tpu_custom_call" | custom-call | tf_op jit(solution)/shard_map/body/pallas_call | solution.py:381
  22.6 9.5 %all-to-all-done = f32[128,10,1,128]{3,2,1,0:T(1,128)S(1)} async-done(((f32[128,10,1,128]{3,2,1,0:T(1,128)}), f32[128,10,1,128]{3,2,1,0:T(1,128)S(1)}, u32[]{:S(2)}, u32[]{:S(2)}) %all-to-all-start) | async-done | bytes 655392 | tf_op jit(solution)/shard_map/all_to_all | solution.py:415
  32.1 4.6 %all-to-all-start.1 = ((f32[128,12,1,128]{3,2,1,0:T(1,128)}), f32[128,12,1,128]{3,2,1,0:T(1,128)S(1)}, u32[]{:S(2)}, u32[]{:S(2)}) async-start(f32[128,12,1,128]{3,2,1,0:T(1,128)} %bitcast.5), calls=%async_computation.1 | async-start | bytes 1572864 | tf_op jit(solution)/shard_map/all_to_all | solution.py:415
  36.7 15.5 %interp.1 = (f32[528,128]{1,0:T(8,128)S(1)}, s32[256,128]{1,0:T(8,128)}) custom-call(f32[1280,128]{1,0:T(8,128)S(1)} %bitcast.8, bf16[512,256]{1,0:T(8,128)(2,1)S(1)} %get-tuple-element.12.f_ref), custom_call_target="tpu_custom_call" | custom-call | tf_op jit(solution)/shard_map/interp/pallas_call | solution.py:392
  52.2 0.9 %all-to-all-done.1 = f32[128,12,1,128]{3,2,1,0:T(1,128)S(1)} async-done(((f32[128,12,1,128]{3,2,1,0:T(1,128)}), f32[128,12,1,128]{3,2,1,0:T(1,128)S(1)}, u32[]{:S(2)}, u32[]{:S(2)}) %all-to-all-start.1) | async-done | bytes 786464 | tf_op jit(solution)/shard_map/all_to_all | solution.py:415
  53.1 1.6 %merge.1 = f32[8,32768]{1,0:T(8,128)} custom-call(f32[528,128]{1,0:T(8,128)S(1)} %get-tuple-element.13.d_ref, f32[1280,128]{1,0:T(8,128)S(1)} %bitcast.9, f32[1536,128]{1,0:T(8,128)S(1)} %bitcast.10), custom_call_target="tpu_custom_call" | custom-call | tf_op jit(solution)/shard_map/merge/pallas_call | solution.py:404
Async XLA Ops:
  5.6 26.5 %all-to-all-start = ((f32[128,10,1,128]{3,2,1,0:T(1,128)}), f32[128,10,1,128]{3,2,1,0:T(1,128)S(1)}, u32[]{:S(2)}, u32[]{:S(2)}) async-start(f32[128,10,1,128]{3,2,1,0:T(1,128)} %bitcast.3), calls=%async_computation | async-start | bytes 1310720 | tf_op jit(solution)/shard_map/all_to_all | solution.py:415
  32.1 21.0 %all-to-all-start.1 = ((f32[128,12,1,128]{3,2,1,0:T(1,128)}), f32[128,12,1,128]{3,2,1,0:T(1,128)S(1)}, u32[]{:S(2)}, u32[]{:S(2)}) async-start(f32[128,12,1,128]{3,2,1,0:T(1,128)} %bitcast.5), calls=%async_computation.1 | async-start | bytes 1572864 | tf_op jit(solution)/shard_map/all_to_all | solution.py:415

commit v8 on v7

--- a/solution.py
+++ b/solution.py
@@ -17,6 +17,7 @@
 HALO = 6
 PAD = 8
 RB = 4096
+MERGES = 4
 VMEM = pl.BlockSpec(memory_space=pltpu.VMEM)
 
 
@@ -133,10 +134,11 @@
     return side
 
 
-def head_kernel(p_ref, key_ref, a_ref, b_ref, v_ref, out_ref, rank_ref, count_ref, acc_ref, left_ref, col_ref, ut_ref, oh_ref, edge_ref, sem):
+def head_kernel(far_ref, key_ref, a_ref, b_ref, v_ref, out_ref, rank_ref, count_ref, acc_ref, left_ref, col_ref, ut_ref, oh_ref, edge_ref, p_ref, sem):
     n = p_ref.shape[1] // RB
-    copy = pltpu.make_async_copy(v_ref, edge_ref, sem)
-    copy.start()
+    copies = [pltpu.make_async_copy(far_ref, p_ref, sem.at[0]), pltpu.make_async_copy(v_ref, edge_ref, sem.at[1])]
+    for copy in copies:
+        copy.start()
     out_ref[...] = jnp.zeros(out_ref.shape, f32)
     before = lax.broadcasted_iota(i32, (256, 256), 0) < lax.broadcasted_iota(i32, (256, 256), 1)
     ut_ref[...] = jnp.where(before, 1.0, 0.0).astype(bf16)
@@ -165,7 +167,8 @@
         return carry
 
     lax.fori_loop(0, n, rank_block, 0)
-    copy.wait()
+    for copy in copies:
+        copy.wait()
     side = around()
     turned = [edge_ref[c].T for c in range(2)]
 
@@ -328,23 +331,24 @@
     lax.fori_loop(0, OWNERS // S, step, 0)
 
 
-def merge_kernel(d_ref, r1_ref, r2_ref, out_ref):
-    S = out_ref.shape[1] // 256
-    s0 = pl.program_id(0) * S
+def merge_kernel(d_ref, r1_ref, r2_ref, out_ref, tile_ref, sem):
     sub = lax.broadcasted_iota(i32, (8, 128), 0)
     top, mid = sub < 2, sub < 4
-    lead = pltpu.roll(r2_ref[0:8, :], 2, 0)
-    for s in range(S):
-        for h in range(2):
-            src = s0 + s
-            w = r1_ref[pl.ds(src * HEAD_ROWS + 2 * h, 8), :]
-            at = src * BODY_ROWS + BODY * h - 2
-            if s == 0 and h == 0:
-                u = jnp.where(s0 == 0, lead, r2_ref[pl.ds(jnp.maximum(at, 0), 8), :])
-            else:
-                u = r2_ref[pl.ds(at, 8), :]
-            d = d_ref[pl.ds(PAD + 2 * (2 * src + h) - 2, 8), :]
-            out_ref[:, s * 256 + h * 128:s * 256 + h * 128 + 128] = jnp.where(top, w, jnp.where(mid, u + d, u))
+    copies = []
+    for k in range(MERGES):
+        for src in range(k * OWNERS // MERGES, (k + 1) * OWNERS // MERGES):
+            for h in range(2):
+                slot = 2 * src + h
+                w = r1_ref[src * HEAD_ROWS + 2 * h:src * HEAD_ROWS + 2 * h + 8, :]
+                at = src * BODY_ROWS + BODY * h - 2
+                u = r2_ref[at:at + 8, :] if slot else pltpu.roll(r2_ref[0:8, :], 2, 0)
+                d = d_ref[PAD + 2 * slot - 2:PAD + 2 * slot + 6, :]
+                tile_ref[:, slot * 128:slot * 128 + 128] = jnp.where(top, w, jnp.where(mid, u + d, u))
+        lanes = pl.ds(k * (tile_ref.shape[1] // MERGES), tile_ref.shape[1] // MERGES)
+        copies.append(pltpu.make_async_copy(tile_ref.at[:, lanes], out_ref.at[:, lanes], sem.at[k]))
+        copies[-1].start()
+    for copy in copies:
+        copy.wait()
 
 
 def shape(*dims, dt=f32):
@@ -369,10 +373,10 @@
     return pl.pallas_call(
         head_kernel,
         out_shape=(held(OWNERS * HEAD_ROWS, 128), held(1, n), held(128, 128)),
-        in_specs=[VMEM] * 4 + [pl.BlockSpec(memory_space=pl.ANY)],
+        in_specs=[pl.BlockSpec(memory_space=pl.ANY)] + [VMEM] * 3 + [pl.BlockSpec(memory_space=pl.ANY)],
         out_specs=(VMEM,) * 3,
         scratch_shapes=scratch(HEAD, n // 2)
-        + [pltpu.VMEM((256, 256), bf16), pltpu.VMEM((RB // 2, 256), bf16), pltpu.VMEM((2, 256, 128), f32), pltpu.SemaphoreType.DMA],
+        + [pltpu.VMEM((256, 256), bf16), pltpu.VMEM((RB // 2, 256), bf16), pltpu.VMEM((2, 256, 128), f32), pltpu.VMEM((8, n), f32), pltpu.SemaphoreType.DMA((2,))],
         name="head",
     )(particles, key, a, b, velocity)
 
@@ -400,13 +404,12 @@
 
 def merge(moved, head_arrived, body_arrived):
     n = OWNERS * 256
-    g = 4
     return pl.pallas_call(
         merge_kernel,
         out_shape=shape(8, n),
-        grid=(g,),
         in_specs=[VMEM] * 3,
-        out_specs=pl.BlockSpec((8, n // g), lambda i: (0, i)),
+        out_specs=pl.BlockSpec(memory_space=pl.ANY),
+        scratch_shapes=[pltpu.VMEM((8, n), f32), pltpu.SemaphoreType.DMA((MERGES,))],
         name="merge",
     )(near_memory(moved), head_arrived, body_arrived)
 

time: 55 us -> 54.3 us (0.987)
  Pallas kernels: 27.6 us -> 26.9 us
    pallas_call x1, Pallas kernels: 1.62 us -> 1.06 us  [merge(): pl.pallas_call(merge_kernel, out_shape=shape(8, n), in_specs=[VMEM] * 3,...]
where the time goes in v8:
time: 54.3 us; the launch traced here: 54 us
  Pallas kernels  26.9 us (50%)
  starting transfers between devices  16 us (29%)
  waiting for transfers between devices  10.4 us (19%)
  between operations  0.66 us (1%)
    all_to_all x2, starting transfers between devices, exchange(): lax.all_to_all(buckets.reshape(OWNERS, rows, 1, 128), ALL, 0, 0, tiled=True)  16 us
    pallas_call x1, Pallas kernels, interp(): pl.pallas_call(interp_kernel, out_shape=(held(PAD + 4 * OWNERS + 8, 128),...  15.5 us
    all_to_all x2, waiting for transfers between devices, exchange(): lax.all_to_all(buckets.reshape(OWNERS, rows, 1, 128), ALL, 0, 0, tiled=True)  10.4 us
    pallas_call x1, Pallas kernels, body(): pl.pallas_call(body_kernel, out_shape=(held(OWNERS * BODY_ROWS, 128), hel...  5.51 us
    pallas_call x1, Pallas kernels, head(): pl.pallas_call(head_kernel, out_shape=(held(OWNERS * HEAD_ROWS, 128), hel...  4.78 us
  transfers between devices with their start and end apart: 2, of which 2 were waited for; matrix products, arithmetic and copies ran while one was open for 0% of the time, Pallas kernels for 39%

profile of v8, /device:TPU:1, one launch (start us, length us, event | category | flops | bytes accessed | tf_op | source)
XLA Modules:
  0.0 54.0 jit_solution(14867792407361635134)
XLA Ops:
  0.6 4.8 %head.1 = (f32[1280,128]{1,0:T(8,128)}, f32[1,8192]{1,0:T(1,128)S(1)}, f32[128,128]{1,0:T(8,128)S(1)}) custom-call(f32[8,8192]{1,0:T(8,128)} %p_ref.1, s32[1,8192]{1,0:T(1,128)} %bitcast.11, s32[1,8192]{1,0:T(1,128)} %bitcast.13, s32[1,8192]{1,0:T(1,128)} %bitcast.14, f32[2,256,128]{2,1,0:T(8,128)} %v_ref.3), custom_call_target="tpu_custom_call" | custom-call | tf_op jit(solution)/shard_map/head/pallas_call | solution.py:373
  5.4 11.5 %all-to-all-start = ((f32[128,10,1,128]{3,2,1,0:T(1,128)}), f32[128,10,1,128]{3,2,1,0:T(1,128)S(1)}, u32[]{:S(2)}, u32[]{:S(2)}) async-start(f32[128,10,1,128]{3,2,1,0:T(1,128)} %bitcast.3), calls=%async_computation | async-start | bytes 1310720 | tf_op jit(solution)/shard_map/all_to_all | solution.py:418
  16.9 5.5 %body.1 = (f32[1536,128]{1,0:T(8,128)}, bf16[512,256]{1,0:T(8,128)(2,1)S(1)}) custom-call(f32[8,8192]{1,0:T(8,128)} %p_ref.1, s32[1,8192]{1,0:T(1,128)} %bitcast.12, f32[1,8192]{1,0:T(1,128)S(1)} %get-tuple-element.10.rank_ref, f32[128,128]{1,0:T(8,128)S(1)} %get-tuple-element.11.count_ref, f32[2,256,128]{2,1,0:T(8,128)} %v_ref.3), custom_call_target="tpu_custom_call" | custom-call | tf_op jit(solution)/shard_map/body/pallas_call | solution.py:385
  22.4 9.5 %all-to-all-done = f32[128,10,1,128]{3,2,1,0:T(1,128)S(1)} async-done(((f32[128,10,1,128]{3,2,1,0:T(1,128)}), f32[128,10,1,128]{3,2,1,0:T(1,128)S(1)}, u32[]{:S(2)}, u32[]{:S(2)}) %all-to-all-start) | async-done | bytes 655392 | tf_op jit(solution)/shard_map/all_to_all | solution.py:418
  31.9 4.6 %all-to-all-start.1 = ((f32[128,12,1,128]{3,2,1,0:T(1,128)}), f32[128,12,1,128]{3,2,1,0:T(1,128)S(1)}, u32[]{:S(2)}, u32[]{:S(2)}) async-start(f32[128,12,1,128]{3,2,1,0:T(1,128)} %bitcast.5), calls=%async_computation.1 | async-start | bytes 1572864 | tf_op jit(solution)/shard_map/all_to_all | solution.py:418
  36.5 15.5 %interp.1 = (f32[528,128]{1,0:T(8,128)S(1)}, s32[256,128]{1,0:T(8,128)}) custom-call(f32[1280,128]{1,0:T(8,128)S(1)} %bitcast.8, bf16[512,256]{1,0:T(8,128)(2,1)S(1)} %get-tuple-element.12.f_ref), custom_call_target="tpu_custom_call" | custom-call | tf_op jit(solution)/shard_map/interp/pallas_call | solution.py:396
  52.0 0.9 %all-to-all-done.1 = f32[128,12,1,128]{3,2,1,0:T(1,128)S(1)} async-done(((f32[128,12,1,128]{3,2,1,0:T(1,128)}), f32[128,12,1,128]{3,2,1,0:T(1,128)S(1)}, u32[]{:S(2)}, u32[]{:S(2)}) %all-to-all-start.1) | async-done | bytes 786464 | tf_op jit(solution)/shard_map/all_to_all | solution.py:418
  52.9 1.1 %merge.1 = f32[8,32768]{1,0:T(8,128)} custom-call(f32[528,128]{1,0:T(8,128)S(1)} %get-tuple-element.13.d_ref, f32[1280,128]{1,0:T(8,128)S(1)} %bitcast.9, f32[1536,128]{1,0:T(8,128)S(1)} %bitcast.10), custom_call_target="tpu_custom_call" | custom-call | tf_op jit(solution)/shard_map/merge/pallas_call | solution.py:407
Async XLA Ops:
  5.4 26.5 %all-to-all-start = ((f32[128,10,1,128]{3,2,1,0:T(1,128)}), f32[128,10,1,128]{3,2,1,0:T(1,128)S(1)}, u32[]{:S(2)}, u32[]{:S(2)}) async-start(f32[128,10,1,128]{3,2,1,0:T(1,128)} %bitcast.3), calls=%async_computation | async-start | bytes 1310720 | tf_op jit(solution)/shard_map/all_to_all | solution.py:418
  31.9 21.0 %all-to-all-start.1 = ((f32[128,12,1,128]{3,2,1,0:T(1,128)}), f32[128,12,1,128]{3,2,1,0:T(1,128)S(1)}, u32[]{:S(2)}, u32[]{:S(2)}) async-start(f32[128,12,1,128]{3,2,1,0:T(1,128)} %bitcast.5), calls=%async_computation.1 | async-start | bytes 1572864 | tf_op jit(solution)/shard_map/all_to_all | solution.py:418

commit v9 on v8

--- a/solution.py
+++ b/solution.py
@@ -134,9 +134,10 @@
     return side
 
 
-def head_kernel(far_ref, key_ref, a_ref, b_ref, v_ref, out_ref, rank_ref, count_ref, acc_ref, left_ref, col_ref, ut_ref, oh_ref, edge_ref, p_ref, sem):
+def head_kernel(far_ref, far_key_ref, far_a_ref, far_b_ref, v_ref, out_ref, rank_ref, count_ref, acc_ref, left_ref, col_ref, ut_ref, oh_ref, edge_ref, p_ref, key_ref, a_ref, b_ref, sem):
     n = p_ref.shape[1] // RB
-    copies = [pltpu.make_async_copy(far_ref, p_ref, sem.at[0]), pltpu.make_async_copy(v_ref, edge_ref, sem.at[1])]
+    pairs = ((far_key_ref, key_ref), (far_a_ref, a_ref), (far_b_ref, b_ref), (far_ref, p_ref), (v_ref, edge_ref))
+    copies = [pltpu.make_async_copy(source, target, sem.at[k]) for k, (source, target) in enumerate(pairs)]
     for copy in copies:
         copy.start()
     out_ref[...] = jnp.zeros(out_ref.shape, f32)
@@ -166,8 +167,9 @@
         rank_ref[0:1, sl] = jnp.concatenate(ranks, 1)
         return carry
 
+    copies[0].wait()
     lax.fori_loop(0, n, rank_block, 0)
-    for copy in copies:
+    for copy in copies[1:]:
         copy.wait()
     side = around()
     turned = [edge_ref[c].T for c in range(2)]
@@ -373,10 +375,11 @@
     return pl.pallas_call(
         head_kernel,
         out_shape=(held(OWNERS * HEAD_ROWS, 128), held(1, n), held(128, 128)),
-        in_specs=[pl.BlockSpec(memory_space=pl.ANY)] + [VMEM] * 3 + [pl.BlockSpec(memory_space=pl.ANY)],
+        in_specs=[pl.BlockSpec(memory_space=pl.ANY)] * 5,
         out_specs=(VMEM,) * 3,
         scratch_shapes=scratch(HEAD, n // 2)
-        + [pltpu.VMEM((256, 256), bf16), pltpu.VMEM((RB // 2, 256), bf16), pltpu.VMEM((2, 256, 128), f32), pltpu.VMEM((8, n), f32), pltpu.SemaphoreType.DMA((2,))],
+        + [pltpu.VMEM((256, 256), bf16), pltpu.VMEM((RB // 2, 256), bf16), pltpu.VMEM((2, 256, 128), f32), pltpu.VMEM((8, n), f32)]
+        + [pltpu.VMEM((1, n), i32)] * 3 + [pltpu.SemaphoreType.DMA((5,))],
         name="head",
     )(particles, key, a, b, velocity)
 

time: 54.3 us -> 54.2 us (level)
  no operation moved by 1% of the time
where the time goes in v9:
time: 54.2 us; the launch traced here: 53.9 us
  Pallas kernels  26.8 us (49%)
  starting transfers between devices  16 us (30%)
  waiting for transfers between devices  10.4 us (19%)
  between operations  0.66 us (1%)
    all_to_all x2, starting transfers between devices, exchange(): lax.all_to_all(buckets.reshape(OWNERS, rows, 1, 128), ALL, 0, 0, tiled=True)  16 us
    pallas_call x1, Pallas kernels, interp(): pl.pallas_call(interp_kernel, out_shape=(held(PAD + 4 * OWNERS + 8, 128),...  15.5 us
    all_to_all x2, waiting for transfers between devices, exchange(): lax.all_to_all(buckets.reshape(OWNERS, rows, 1, 128), ALL, 0, 0, tiled=True)  10.4 us
    pallas_call x1, Pallas kernels, body(): pl.pallas_call(body_kernel, out_shape=(held(OWNERS * BODY_ROWS, 128), hel...  5.52 us
    pallas_call x1, Pallas kernels, head(): pl.pallas_call(head_kernel, out_shape=(held(OWNERS * HEAD_ROWS, 128), hel...  4.72 us
  transfers between devices with their start and end apart: 2, of which 2 were waited for; matrix products, arithmetic and copies ran while one was open for 0% of the time, Pallas kernels for 39%

profile of v9, /device:TPU:1, one launch (start us, length us, event | category | flops | bytes accessed | tf_op | source)
XLA Modules:
  0.0 53.9 jit_solution(16393846823518806947)
XLA Ops:
  0.6 4.7 %head.1 = (f32[1280,128]{1,0:T(8,128)}, f32[1,8192]{1,0:T(1,128)S(1)}, f32[128,128]{1,0:T(8,128)S(1)}) custom-call(f32[8,8192]{1,0:T(8,128)} %p_ref.1, s32[1,8192]{1,0:T(1,128)} %bitcast.11, s32[1,8192]{1,0:T(1,128)} %bitcast.13, s32[1,8192]{1,0:T(1,128)} %bitcast.14, f32[2,256,128]{2,1,0:T(8,128)} %v_ref.3), custom_call_target="tpu_custom_call" | custom-call | tf_op jit(solution)/shard_map/head/pallas_call | solution.py:375
  5.4 11.5 %all-to-all-start = ((f32[128,10,1,128]{3,2,1,0:T(1,128)}), f32[128,10,1,128]{3,2,1,0:T(1,128)S(1)}, u32[]{:S(2)}, u32[]{:S(2)}) async-start(f32[128,10,1,128]{3,2,1,0:T(1,128)} %bitcast.3), calls=%async_computation | async-start | bytes 1310720 | tf_op jit(solution)/shard_map/all_to_all | solution.py:421
  16.9 5.5 %body.1 = (f32[1536,128]{1,0:T(8,128)}, bf16[512,256]{1,0:T(8,128)(2,1)S(1)}) custom-call(f32[8,8192]{1,0:T(8,128)} %p_ref.1, s32[1,8192]{1,0:T(1,128)} %bitcast.12, f32[1,8192]{1,0:T(1,128)S(1)} %get-tuple-element.10.rank_ref, f32[128,128]{1,0:T(8,128)S(1)} %get-tuple-element.11.count_ref, f32[2,256,128]{2,1,0:T(8,128)} %v_ref.3), custom_call_target="tpu_custom_call" | custom-call | tf_op jit(solution)/shard_map/body/pallas_call | solution.py:388
  22.4 9.5 %all-to-all-done = f32[128,10,1,128]{3,2,1,0:T(1,128)S(1)} async-done(((f32[128,10,1,128]{3,2,1,0:T(1,128)}), f32[128,10,1,128]{3,2,1,0:T(1,128)S(1)}, u32[]{:S(2)}, u32[]{:S(2)}) %all-to-all-start) | async-done | bytes 655392 | tf_op jit(solution)/shard_map/all_to_all | solution.py:421
  31.9 4.6 %all-to-all-start.1 = ((f32[128,12,1,128]{3,2,1,0:T(1,128)}), f32[128,12,1,128]{3,2,1,0:T(1,128)S(1)}, u32[]{:S(2)}, u32[]{:S(2)}) async-start(f32[128,12,1,128]{3,2,1,0:T(1,128)} %bitcast.5), calls=%async_computation.1 | async-start | bytes 1572864 | tf_op jit(solution)/shard_map/all_to_all | solution.py:421
  36.4 15.5 %interp.1 = (f32[528,128]{1,0:T(8,128)S(1)}, s32[256,128]{1,0:T(8,128)}) custom-call(f32[1280,128]{1,0:T(8,128)S(1)} %bitcast.8, bf16[512,256]{1,0:T(8,128)(2,1)S(1)} %get-tuple-element.12.f_ref), custom_call_target="tpu_custom_call" | custom-call | tf_op jit(solution)/shard_map/interp/pallas_call | solution.py:399
  52.0 0.9 %all-to-all-done.1 = f32[128,12,1,128]{3,2,1,0:T(1,128)S(1)} async-done(((f32[128,12,1,128]{3,2,1,0:T(1,128)}), f32[128,12,1,128]{3,2,1,0:T(1,128)S(1)}, u32[]{:S(2)}, u32[]{:S(2)}) %all-to-all-start.1) | async-done | bytes 786464 | tf_op jit(solution)/shard_map/all_to_all | solution.py:421
  52.9 1.1 %merge.1 = f32[8,32768]{1,0:T(8,128)} custom-call(f32[528,128]{1,0:T(8,128)S(1)} %get-tuple-element.13.d_ref, f32[1280,128]{1,0:T(8,128)S(1)} %bitcast.9, f32[1536,128]{1,0:T(8,128)S(1)} %bitcast.10), custom_call_target="tpu_custom_call" | custom-call | tf_op jit(solution)/shard_map/merge/pallas_call | solution.py:410
Async XLA Ops:
  5.4 26.5 %all-to-all-start = ((f32[128,10,1,128]{3,2,1,0:T(1,128)}), f32[128,10,1,128]{3,2,1,0:T(1,128)S(1)}, u32[]{:S(2)}, u32[]{:S(2)}) async-start(f32[128,10,1,128]{3,2,1,0:T(1,128)} %bitcast.3), calls=%async_computation | async-start | bytes 1310720 | tf_op jit(solution)/shard_map/all_to_all | solution.py:421
  31.9 21.0 %all-to-all-start.1 = ((f32[128,12,1,128]{3,2,1,0:T(1,128)}), f32[128,12,1,128]{3,2,1,0:T(1,128)S(1)}, u32[]{:S(2)}, u32[]{:S(2)}) async-start(f32[128,12,1,128]{3,2,1,0:T(1,128)} %bitcast.5), calls=%async_computation.1 | async-start | bytes 1572864 | tf_op jit(solution)/shard_map/all_to_all | solution.py:421

commit v10 on v8

--- a/solution.py
+++ b/solution.py
@@ -375,7 +375,7 @@
         out_shape=(held(OWNERS * HEAD_ROWS, 128), held(1, n), held(128, 128)),
         in_specs=[pl.BlockSpec(memory_space=pl.ANY)] + [VMEM] * 3 + [pl.BlockSpec(memory_space=pl.ANY)],
         out_specs=(VMEM,) * 3,
-        scratch_shapes=scratch(HEAD, n // 2)
+        scratch_shapes=scratch(HEAD, n)
         + [pltpu.VMEM((256, 256), bf16), pltpu.VMEM((RB // 2, 256), bf16), pltpu.VMEM((2, 256, 128), f32), pltpu.VMEM((8, n), f32), pltpu.SemaphoreType.DMA((2,))],
         name="head",
     )(particles, key, a, b, velocity)

time: 54.3 us -> 54.3 us (level)
  no operation moved by 1% of the time
where the time goes in v10:
time: 54.3 us; the launch traced here: 54 us
  Pallas kernels  26.9 us (50%)
  starting transfers between devices  16 us (29%)
  waiting for transfers between devices  10.4 us (19%)
  between operations  0.66 us (1%)
    all_to_all x2, starting transfers between devices, exchange(): lax.all_to_all(buckets.reshape(OWNERS, rows, 1, 128), ALL, 0, 0, tiled=True)  16 us
    pallas_call x1, Pallas kernels, interp(): pl.pallas_call(interp_kernel, out_shape=(held(PAD + 4 * OWNERS + 8, 128),...  15.5 us
    all_to_all x2, waiting for transfers between devices, exchange(): lax.all_to_all(buckets.reshape(OWNERS, rows, 1, 128), ALL, 0, 0, tiled=True)  10.4 us
    pallas_call x1, Pallas kernels, body(): pl.pallas_call(body_kernel, out_shape=(held(OWNERS * BODY_ROWS, 128), hel...  5.52 us
    pallas_call x1, Pallas kernels, head(): pl.pallas_call(head_kernel, out_shape=(held(OWNERS * HEAD_ROWS, 128), hel...  4.79 us
  transfers between devices with their start and end apart: 2, of which 2 were waited for; matrix products, arithmetic and copies ran while one was open for 0% of the time, Pallas kernels for 39%

profile of v10, /device:TPU:1, one launch (start us, length us, event | category | flops | bytes accessed | tf_op | source)
XLA Modules:
  0.0 54.0 jit_solution(7238715021488689186)
XLA Ops:
  0.6 4.8 %head.1 = (f32[1280,128]{1,0:T(8,128)}, f32[1,8192]{1,0:T(1,128)S(1)}, f32[128,128]{1,0:T(8,128)S(1)}) custom-call(f32[8,8192]{1,0:T(8,128)} %p_ref.1, s32[1,8192]{1,0:T(1,128)} %bitcast.11, s32[1,8192]{1,0:T(1,128)} %bitcast.13, s32[1,8192]{1,0:T(1,128)} %bitcast.14, f32[2,256,128]{2,1,0:T(8,128)} %v_ref.3), custom_call_target="tpu_custom_call" | custom-call | tf_op jit(solution)/shard_map/head/pallas_call | solution.py:373
  5.4 11.5 %all-to-all-start = ((f32[128,10,1,128]{3,2,1,0:T(1,128)}), f32[128,10,1,128]{3,2,1,0:T(1,128)S(1)}, u32[]{:S(2)}, u32[]{:S(2)}) async-start(f32[128,10,1,128]{3,2,1,0:T(1,128)} %bitcast.3), calls=%async_computation | async-start | bytes 1310720 | tf_op jit(solution)/shard_map/all_to_all | solution.py:418
  16.9 5.5 %body.1 = (f32[1536,128]{1,0:T(8,128)}, bf16[512,256]{1,0:T(8,128)(2,1)S(1)}) custom-call(f32[8,8192]{1,0:T(8,128)} %p_ref.1, s32[1,8192]{1,0:T(1,128)} %bitcast.12, f32[1,8192]{1,0:T(1,128)S(1)} %get-tuple-element.10.rank_ref, f32[128,128]{1,0:T(8,128)S(1)} %get-tuple-element.11.count_ref, f32[2,256,128]{2,1,0:T(8,128)} %v_ref.3), custom_call_target="tpu_custom_call" | custom-call | tf_op jit(solution)/shard_map/body/pallas_call | solution.py:385
  22.4 9.5 %all-to-all-done = f32[128,10,1,128]{3,2,1,0:T(1,128)S(1)} async-done(((f32[128,10,1,128]{3,2,1,0:T(1,128)}), f32[128,10,1,128]{3,2,1,0:T(1,128)S(1)}, u32[]{:S(2)}, u32[]{:S(2)}) %all-to-all-start) | async-done | bytes 655392 | tf_op jit(solution)/shard_map/all_to_all | solution.py:418
  31.9 4.6 %all-to-all-start.1 = ((f32[128,12,1,128]{3,2,1,0:T(1,128)}), f32[128,12,1,128]{3,2,1,0:T(1,128)S(1)}, u32[]{:S(2)}, u32[]{:S(2)}) async-start(f32[128,12,1,128]{3,2,1,0:T(1,128)} %bitcast.5), calls=%async_computation.1 | async-start | bytes 1572864 | tf_op jit(solution)/shard_map/all_to_all | solution.py:418
  36.5 15.5 %interp.1 = (f32[528,128]{1,0:T(8,128)S(1)}, s32[256,128]{1,0:T(8,128)}) custom-call(f32[1280,128]{1,0:T(8,128)S(1)} %bitcast.8, bf16[512,256]{1,0:T(8,128)(2,1)S(1)} %get-tuple-element.12.f_ref), custom_call_target="tpu_custom_call" | custom-call | tf_op jit(solution)/shard_map/interp/pallas_call | solution.py:396
  52.0 0.9 %all-to-all-done.1 = f32[128,12,1,128]{3,2,1,0:T(1,128)S(1)} async-done(((f32[128,12,1,128]{3,2,1,0:T(1,128)}), f32[128,12,1,128]{3,2,1,0:T(1,128)S(1)}, u32[]{:S(2)}, u32[]{:S(2)}) %all-to-all-start.1) | async-done | bytes 786464 | tf_op jit(solution)/shard_map/all_to_all | solution.py:418
  52.9 1.1 %merge.1 = f32[8,32768]{1,0:T(8,128)} custom-call(f32[528,128]{1,0:T(8,128)S(1)} %get-tuple-element.13.d_ref, f32[1280,128]{1,0:T(8,128)S(1)} %bitcast.9, f32[1536,128]{1,0:T(8,128)S(1)} %bitcast.10), custom_call_target="tpu_custom_call" | custom-call | tf_op jit(solution)/shard_map/merge/pallas_call | solution.py:407
Async XLA Ops:
  5.4 26.5 %all-to-all-start = ((f32[128,10,1,128]{3,2,1,0:T(1,128)}), f32[128,10,1,128]{3,2,1,0:T(1,128)S(1)}, u32[]{:S(2)}, u32[]{:S(2)}) async-start(f32[128,10,1,128]{3,2,1,0:T(1,128)} %bitcast.3), calls=%async_computation | async-start | bytes 1310720 | tf_op jit(solution)/shard_map/all_to_all | solution.py:418
  31.9 21.0 %all-to-all-start.1 = ((f32[128,12,1,128]{3,2,1,0:T(1,128)}), f32[128,12,1,128]{3,2,1,0:T(1,128)S(1)}, u32[]{:S(2)}, u32[]{:S(2)}) async-start(f32[128,12,1,128]{3,2,1,0:T(1,128)} %bitcast.5), calls=%async_computation.1 | async-start | bytes 1572864 | tf_op jit(solution)/shard_map/all_to_all | solution.py:418
